TPU v7x, 512 devices: a whole 4x4x16 slice. The times are simulated.
512 devices in a mesh: gx: 4 (over x), gy: 16 (over z), gz: 8 (over y, core).
Axes of the slice: x: 4, y: 4, z: 16, core: 2. Of those that a mesh axis runs over, the one named last changes fastest.
Arguments:
- old_data: float32 [6144, 5, 16, 256], P(('gx', 'gy', 'gz')), may hold values from -6 to 24, as said below
- pair_old: int32 [16384], P(('gx', 'gy', 'gz')), may hold values from 0 to 11
- pair_slot: int32 [16384], P(('gx', 'gy', 'gz')), may hold values from 0 to 2
- pair_shift: int32 [16384, 3], P(('gx', 'gy', 'gz')), may hold values from -2 to 2
- pair_dest: int32 [16384, 1], P(('gx', 'gy', 'gz')), may hold values from 0 to 31; in each aligned block of 32 rows (0 to 31, 32 to 63, ...) at most 2 rows name the same one
- new_ratio: int32 [1536], replicated, may hold values from 1 to 2, as said below
- neighbor_side: int32 [1536, 6], P(('gx', 'gy', 'gz')), may hold values from 0 to 3
- neighbor_patch: int32 [1536, 6], P(('gx', 'gy', 'gz')), may hold values from 0 to 2
Outputs:
- new_data: float32 [1536, 5, 16, 256], P(('gx', 'gy', 'gz'))
- interface_jump: float32 [1536, 5, 6, 256], P(('gx', 'gy', 'gz'))
- mass_totals: float32 [2, 5], replicated
Inputs may be any that keep to these rules, and one draw needn't show every extreme that they name: `old_data`: values of order one whose level differs from patch to patch and field to field. `pair_dest`: on the rows of one device no owner is named more than 2 times, and some device names some owner exactly 2 times. `new_ratio`: 1 marks a new patch on the old level, 2 one coarser by a factor of two in each direction. `neighbor_side`: 0: on the device before in the order d, 1: on the same device, 2: on the device after, 3: no neighbour.
All inputs are finite; a program needn't handle non-finite values.
Results may differ from a plain program's by a relative error of at most 0.0001.
Values sent between devices are 32-bit elements; how exact they have to be, the bound alone decides.
No kernel may reach another device: no remote copies, remote signals or barrier semaphores. Data moves between devices by JAX's collectives and lax.ppermute only.
A program may use at most 64 MiB of HBM per device.

v0:
```python
import jax
import jax.numpy as jnp
from jax import lax
from jax.sharding import Mesh
from jax.sharding import PartitionSpec as P

CAP = 2
GZ = ("gz_0", "gz_1")
GX_GY_GZ = ("gx", "gy", "gz_0", "gz_1")
GX_GZ = ("gx", "gz_0", "gz_1")


precise = lax.Precision.HIGHEST


def one_axis_at_a_time(shard, axes):
    for axis in axes:
        shard = lax.psum(shard, axis)
    return shard


def shifted(block, axis, distance):
    devices = range(lax.axis_size(axis))
    route = [(i - distance, i) for i in devices if i - distance in devices]
    return lax.ppermute(block, axis, route)


def intersection_weights(offsets, ratios, edge_cells):
    cell_index = jnp.arange(edge_cells, dtype=jnp.int32)
    distance = cell_index[None, None, :] - offsets[:, None, None]
    within = (distance >= 0) & (
        jnp.floor_divide(distance, ratios[:, None, None]) == cell_index[None, :, None]
    )
    scaled = 1.0 / ratios[:, None, None].astype(jnp.float32)
    return jnp.where(within, scaled, jnp.zeros_like(scaled))


def remap_block(pieces):
    old_block, offsets, ratios = pieces
    block_count, fields, edge_cells, face_cells = old_block.shape
    weight_x = intersection_weights(offsets[:, 0], ratios, edge_cells)
    weight_y = intersection_weights(offsets[:, 1], ratios, edge_cells)
    weight_z = intersection_weights(offsets[:, 2], ratios, edge_cells)
    section_x = jnp.einsum("bim,bfmc->bfic", weight_x, old_block, precision=precise)
    section_x = section_x.reshape(block_count, fields, edge_cells, edge_cells, edge_cells)
    section_y = jnp.einsum("bjn,bfinl->bfijl", weight_y, section_x, precision=precise)
    section_z = jnp.einsum("bkl,bfijl->bfijk", weight_z, section_y, precision=precise)
    return section_z.reshape(block_count, fields, edge_cells, face_cells)


def body(
    old_data, pair_old, pair_slot, pair_shift, pair_dest, new_ratio, neighbor_side, neighbor_patch
):
    old_count, fields, edge_cells, face_cells = old_data.shape
    cell_count = edge_cells * face_cells
    pair_count = pair_old.shape[0]
    new_count = neighbor_side.shape[0]
    size_x = lax.axis_size("gx")
    size_y = lax.axis_size("gy")
    size_z = lax.axis_size(GZ)
    group_size = size_x * size_z
    devices = size_x * size_y * size_z
    index_y = lax.axis_index("gy")
    linear = (lax.axis_index("gx") * size_y + index_y) * size_z + lax.axis_index(GZ)
    target = pair_dest[:, 0]
    owner_device = (target // size_z * size_y + index_y) * size_z + target % size_z
    global_new = owner_device * new_count + pair_slot
    table_hits = global_new[:, None] == jnp.arange(new_ratio.shape[0], dtype=jnp.int32)[None, :]
    ratios = jnp.sum(jnp.where(table_hits, new_ratio[None, :], 0), axis=1)
    source = jnp.take(old_data, pair_old, axis=0)
    blocks = pair_count // 8
    partials = lax.map(
        remap_block,
        (
            source.reshape(blocks, 8, fields, edge_cells, face_cells),
            pair_shift.reshape(blocks, 8, 3),
            ratios.reshape(blocks, 8),
        ),
    )
    flat_partials = partials.reshape(pair_count, fields * cell_count)
    old_part = jnp.sum(old_data, axis=(0, 2, 3))
    ratio_cubes = ratios.astype(jnp.float32) ** 3
    new_part = jnp.sum(
        ratio_cubes[:, None]
        * jnp.sum(flat_partials.reshape(pair_count, fields, cell_count), axis=2),
        axis=0,
    )
    early_totals = (one_axis_at_a_time(old_part, GX_GY_GZ), one_axis_at_a_time(new_part, GX_GY_GZ))
    same_owner = target[:, None] == target[None, :]
    pair_order = jnp.arange(pair_count, dtype=jnp.int32)
    earlier = pair_order[None, :] < pair_order[:, None]
    slot_rank = jnp.sum((same_owner & earlier).astype(jnp.int32), axis=1)
    position = target * CAP + slot_rank
    placing = jnp.arange(group_size * CAP, dtype=jnp.int32)[:, None] == position[None, :]
    filled = jnp.any(placing, axis=1)
    source_pair = jnp.sum(jnp.where(placing, pair_order[None, :], 0), axis=1)
    taken = jnp.take(flat_partials, source_pair, axis=0)
    outgoing = jnp.where(filled[:, None], taken, jnp.zeros_like(taken))
    out_slots = jnp.sum(jnp.where(placing, pair_slot[None, :] + 1, 0), axis=1) - 1
    arrived, arrived_slots = (
        lax.all_to_all(
            outgoing.reshape(group_size, CAP, fields * cell_count),
            GX_GZ,
            split_axis=0,
            concat_axis=0,
            tiled=True,
        ),
        lax.all_to_all(
            out_slots.reshape(group_size, CAP), GX_GZ, split_axis=0, concat_axis=0, tiled=True
        ),
    )
    received = arrived.reshape(group_size * CAP, fields * cell_count)
    slot_list = arrived_slots.reshape(group_size * CAP)
    picking = (jnp.arange(new_count, dtype=jnp.int32)[:, None] == slot_list[None, :]).astype(
        jnp.float32
    )
    new_flat = jnp.dot(picking, received, precision=precise)
    new_data = new_flat.reshape(new_count, fields, edge_cells, face_cells)
    cube_view = new_data.reshape(new_count, fields, edge_cells, edge_cells, edge_cells)
    face_layers = jnp.stack(
        [
            cube_view[:, :, 0],
            cube_view[:, :, -1],
            cube_view[:, :, :, 0],
            cube_view[:, :, :, -1],
            cube_view[:, :, :, :, 0],
            cube_view[:, :, :, :, -1],
        ],
        axis=2,
    ).reshape(new_count, fields, 6, face_cells)
    opposite = face_layers.reshape(new_count, fields, 3, 2, face_cells)[:, :, :, ::-1].reshape(
        new_count, fields, 6, face_cells
    )
    from_before = shifted(opposite, GX_GY_GZ, 1)
    from_after = shifted(opposite, GX_GY_GZ, -1)
    candidates = jnp.concatenate([from_before, opposite, from_after], axis=0)
    source_device = linear + neighbor_side - 1
    present = (neighbor_side < 3) & (source_device >= 0) & (source_device < devices)
    chosen = neighbor_side * new_count + neighbor_patch
    selector = (
        (jnp.arange(3 * new_count, dtype=jnp.int32)[None, None, :] == chosen[:, :, None])
        & present[:, :, None]
    ).astype(jnp.float32)
    ghosts = jnp.einsum("qes,sfec->qfec", selector, candidates, precision=precise)
    interface_jump = ghosts - face_layers * present[:, None, :, None].astype(jnp.float32)
    old_total, new_total = early_totals
    total_cells = old_count * devices * cell_count
    mass_totals = jnp.stack([old_total, new_total]) / total_cells
    return (new_data, interface_jump, mass_totals)


def solution(mesh):
    torus = Mesh(
        mesh.devices.reshape(mesh.shape["gx"], mesh.shape["gy"], 4, 2), ("gx", "gy", "gz_0", "gz_1")
    )
    return jax.shard_map(
        body,
        mesh=torus,
        in_specs=(
            P(GX_GY_GZ, None, None, None),
            P(GX_GY_GZ),
            P(GX_GY_GZ),
            P(GX_GY_GZ, None),
            P(GX_GY_GZ, None),
            P(),
            P(GX_GY_GZ, None),
            P(GX_GY_GZ, None),
        ),
        out_specs=(P(GX_GY_GZ, None, None, None), P(GX_GY_GZ, None, None, None), P()),
        check_vma=False,
    )
```

profile of v0, /device:TPU:25, one launch (start us, length us, event | category | flops | bytes accessed | tf_op | source)
XLA Modules:
  0.0 329.1 jit_solution(16362286978885154212)
XLA Ops:
  0.6 0.9 convert_reduce_fusion
  3.1 9.4 %all-to-all-start = ((s32[32,1,2]{2,1,0:T(1,128)}), s32[32,1,2]{2,1,0:T(1,128)S(1)}, u32[]{:S(2)}, u32[]{:S(2)}) async-start(s32[32,1,2]{2,1,0:T(1,128)} %bitcast.25), calls=%async_computation | async-start | bytes 32768 | tf_op jit(solution)/shard_map/all_to_all | solution.py:108
  14.0 0.9 select_reduce_fusion
  15.0 0.8 reshape.310
  15.8 3.4 %gather_fusion = f32[32,5,16,256]{3,2,1,0:T(8,128)} fusion(f32[12,5,16,256]{3,2,1,0:T(8,128)} %param.12, s32[1024]{0:T(1024)S(1)} %get-tuple-element.112), kind=kCustom, calls=%fused_computation | custom fusion | bytes 5243008 | tf_op jit(solution)/shard_map/jit(_take)/gather | solution.py:70
  19.2 2.0 broadcast_select_fusion
  21.2 120.4 %while.10 = (s32[]{:T(128)}, f32[4,8,5,16,256]{4,3,2,1,0:T(8,128)}, f32[4,8,5,16,256]{4,3,2,1,0:T(8,128)S(1)}, s32[4,8,3]{1,0,2:T(4,128)S(1)}, s32[4,8]{1,0:T(4,128)S(1)}, /*index=5*/s32[]{:T(128)}) while((s32[]{:T(128)}, f32[4,8,5,16,256]{4,3,2,1,0:T(8,128)}, f32[4,8,5,16,256]{4,3,2,1,0:T(8,128)S(1)}, s32[4,8,3]{1,0,2:T(4,128)S(1)}, ...), condition=%wide.region_6.8_spmd, body=%wide.region_5.7_spmd.sunk | while | flops 94394520 | bytes 7874841 | solution.py:72
  22.3 3.2 reshape.348
  25.6 10.4 %fusion.84 = f32[8,5,16,16,16]{4,3,2,1,0:T(8,128)S(1)} fusion(f32[8,5,16,16,16]{4,3,2,1,0:T(8,128)} %reshape.348, s32[8,16]{1,0:T(8,128)S(1)} %get-tuple-element.156, f32[8]{0:T(128)S(1)} %divide_bitcast_fusion.2, pred[8,16]{1,0:T(8,128)(4,1)S(1)} %get-tuple-element.157), kind=kOutput, calls=%fused_computation.8.clone.1 | convolution fusion | flops 31463424 | bytes 1311392 | tf_op jit(solution)/shard_map/while/body/eval_jaxpr/bjn,bfinl->bfijl/dot_general | solution.py:46
  36.0 10.2 %fusion.85 = f32[8,5,16,16,16]{4,3,2,1,0:T(8,128)} fusion(f32[8,5,16,16,16]{4,3,2,1,0:T(8,128)S(1)} %fusion.84, s32[8,16]{1,0:T(8,128)S(1)} %get-tuple-element.158, f32[8]{0:T(128)S(1)} %divide_bitcast_fusion.2, pred[8,16]{1,0:T(8,128)(4,1)S(1)} %get-tuple-element.159), kind=kOutput, calls=%fused_computation.2.clone.1 | convolution fusion | flops 31463424 | bytes 1311392 | tf_op jit(solution)/shard_map/while/body/eval_jaxpr/bkl,bfijl->bfijk/dot_general | solution.py:47
  46.2 4.2 %broadcast_in_dim.196 = f32[1,8,5,16,256]{4,3,2,1,0:T(8,128)S(1)} reshape(f32[8,5,16,16,16]{4,3,2,1,0:T(8,128)} %fusion.85) | data formatting | bytes 1310720 | tf_op jit(solution)/shard_map/while/body/jit(dynamic_update_index_in_dim)/broadcast_in_dim | solution.py:72
  50.4 0.9 constant_dynamic-update-slice_fusion.12
  52.5 3.2 reshape.348
  55.7 10.4 %fusion.84 = f32[8,5,16,16,16]{4,3,2,1,0:T(8,128)S(1)} fusion(f32[8,5,16,16,16]{4,3,2,1,0:T(8,128)} %reshape.348, s32[8,16]{1,0:T(8,128)S(1)} %get-tuple-element.156, f32[8]{0:T(128)S(1)} %divide_bitcast_fusion.2, pred[8,16]{1,0:T(8,128)(4,1)S(1)} %get-tuple-element.157), kind=kOutput, calls=%fused_computation.8.clone.1 | convolution fusion | flops 31463424 | bytes 1311392 | tf_op jit(solution)/shard_map/while/body/eval_jaxpr/bjn,bfinl->bfijl/dot_general | solution.py:46
  66.1 10.2 %fusion.85 = f32[8,5,16,16,16]{4,3,2,1,0:T(8,128)} fusion(f32[8,5,16,16,16]{4,3,2,1,0:T(8,128)S(1)} %fusion.84, s32[8,16]{1,0:T(8,128)S(1)} %get-tuple-element.158, f32[8]{0:T(128)S(1)} %divide_bitcast_fusion.2, pred[8,16]{1,0:T(8,128)(4,1)S(1)} %get-tuple-element.159), kind=kOutput, calls=%fused_computation.2.clone.1 | convolution fusion | flops 31463424 | bytes 1311392 | tf_op jit(solution)/shard_map/while/body/eval_jaxpr/bkl,bfijl->bfijk/dot_general | solution.py:47
  76.3 4.2 %broadcast_in_dim.196 = f32[1,8,5,16,256]{4,3,2,1,0:T(8,128)S(1)} reshape(f32[8,5,16,16,16]{4,3,2,1,0:T(8,128)} %fusion.85) | data formatting | bytes 1310720 | tf_op jit(solution)/shard_map/while/body/jit(dynamic_update_index_in_dim)/broadcast_in_dim | solution.py:72
  80.6 0.9 constant_dynamic-update-slice_fusion.12
  82.5 3.2 reshape.348
  85.8 10.4 %fusion.84 = f32[8,5,16,16,16]{4,3,2,1,0:T(8,128)S(1)} fusion(f32[8,5,16,16,16]{4,3,2,1,0:T(8,128)} %reshape.348, s32[8,16]{1,0:T(8,128)S(1)} %get-tuple-element.156, f32[8]{0:T(128)S(1)} %divide_bitcast_fusion.2, pred[8,16]{1,0:T(8,128)(4,1)S(1)} %get-tuple-element.157), kind=kOutput, calls=%fused_computation.8.clone.1 | convolution fusion | flops 31463424 | bytes 1311392 | tf_op jit(solution)/shard_map/while/body/eval_jaxpr/bjn,bfinl->bfijl/dot_general | solution.py:46
  96.2 10.2 %fusion.85 = f32[8,5,16,16,16]{4,3,2,1,0:T(8,128)} fusion(f32[8,5,16,16,16]{4,3,2,1,0:T(8,128)S(1)} %fusion.84, s32[8,16]{1,0:T(8,128)S(1)} %get-tuple-element.158, f32[8]{0:T(128)S(1)} %divide_bitcast_fusion.2, pred[8,16]{1,0:T(8,128)(4,1)S(1)} %get-tuple-element.159), kind=kOutput, calls=%fused_computation.2.clone.1 | convolution fusion | flops 31463424 | bytes 1311392 | tf_op jit(solution)/shard_map/while/body/eval_jaxpr/bkl,bfijl->bfijk/dot_general | solution.py:47
  106.4 4.2 %broadcast_in_dim.196 = f32[1,8,5,16,256]{4,3,2,1,0:T(8,128)S(1)} reshape(f32[8,5,16,16,16]{4,3,2,1,0:T(8,128)} %fusion.85) | data formatting | bytes 1310720 | tf_op jit(solution)/shard_map/while/body/jit(dynamic_update_index_in_dim)/broadcast_in_dim | solution.py:72
  110.6 0.9 constant_dynamic-update-slice_fusion.12
  112.6 3.2 reshape.348
  115.9 10.4 %fusion.84 = f32[8,5,16,16,16]{4,3,2,1,0:T(8,128)S(1)} fusion(f32[8,5,16,16,16]{4,3,2,1,0:T(8,128)} %reshape.348, s32[8,16]{1,0:T(8,128)S(1)} %get-tuple-element.156, f32[8]{0:T(128)S(1)} %divide_bitcast_fusion.2, pred[8,16]{1,0:T(8,128)(4,1)S(1)} %get-tuple-element.157), kind=kOutput, calls=%fused_computation.8.clone.1 | convolution fusion | flops 31463424 | bytes 1311392 | tf_op jit(solution)/shard_map/while/body/eval_jaxpr/bjn,bfinl->bfijl/dot_general | solution.py:46
  126.3 10.2 %fusion.85 = f32[8,5,16,16,16]{4,3,2,1,0:T(8,128)} fusion(f32[8,5,16,16,16]{4,3,2,1,0:T(8,128)S(1)} %fusion.84, s32[8,16]{1,0:T(8,128)S(1)} %get-tuple-element.158, f32[8]{0:T(128)S(1)} %divide_bitcast_fusion.2, pred[8,16]{1,0:T(8,128)(4,1)S(1)} %get-tuple-element.159), kind=kOutput, calls=%fused_computation.2.clone.1 | convolution fusion | flops 31463424 | bytes 1311392 | tf_op jit(solution)/shard_map/while/body/eval_jaxpr/bkl,bfijl->bfijk/dot_general | solution.py:47
  136.5 4.2 %broadcast_in_dim.196 = f32[1,8,5,16,256]{4,3,2,1,0:T(8,128)S(1)} reshape(f32[8,5,16,16,16]{4,3,2,1,0:T(8,128)} %fusion.85) | data formatting | bytes 1310720 | tf_op jit(solution)/shard_map/while/body/jit(dynamic_update_index_in_dim)/broadcast_in_dim | solution.py:72
  140.7 0.9 constant_dynamic-update-slice_fusion.12
  141.7 2.0 reshape.312
  143.6 4.3 %gather_fusion.1 = f32[64,20480]{1,0:T(8,128)} fusion(f32[32,20480]{1,0:T(8,128)S(1)} %reshape.312, s32[1024]{0:T(1024)S(1)} %get-tuple-element.111), kind=kCustom, calls=%fused_computation.1 | custom fusion | bytes 10486016 | tf_op jit(solution)/shard_map/jit(_take)/gather | solution.py:97
  147.9 6.7 %gather.15 = f32[32,2,20480]{2,1,0:T(2,128)} reshape(f32[64,20480]{1,0:T(8,128)} %gather_fusion.1) | data formatting | bytes 10485760 | tf_op jit(solution)/shard_map/jit(_take)/gather | solution.py:97
  154.7 9.7 %select_select_fusion = f32[32,2,20480]{2,1,0:T(2,128)} fusion(f32[32,2,20480]{2,1,0:T(2,128)} %gather.15, pred[32,2]{1,0:T(8,128)(4,1)S(1)} %compare_and_fusion, pred[32,2]{1,0:T(8,128)(4,1)S(1)} %broadcast_in_dim.134), kind=kLoop, calls=%fused_computation.68 | loop fusion | flops 2621440 | bytes 10485888 | tf_op jit(solution)/shard_map/jit(_where)/select_n | solution.py:98
  164.4 7.5 %all-to-all-start.1 = ((f32[32,2,20480]{2,1,0:T(2,128)}), f32[32,2,20480]{2,1,0:T(2,128)}, u32[]{:S(2)}, u32[]{:S(2)}) async-start(f32[32,2,20480]{2,1,0:T(2,128)} %select_select_fusion), calls=%async_computation.1 | async-start | bytes 10485760 | tf_op jit(solution)/shard_map/all_to_all | solution.py:101
  172.0 2.2 reduce_sum.74
  174.4 61.9 %all-reduce.2 = (f32[5]{0:T(128)S(1)}, f32[5]{0:T(128)S(1)}) all-reduce(f32[5]{0:T(128)S(1)} %multiply_reduce_fusion, f32[5]{0:T(128)S(1)} %reduce_sum.73), channel_id=1, replica_groups=mesh['gx'=4,'gy'=16,'gz_0'=4,'gz_1'=2] {'gx'}, use_global_device_ids=true, to_apply=%region_14.16 | all-reduce | flops 10 | bytes 80 | tf_op jit(solution)/shard_map/psum | solution.py:18
  236.4 27.4 %all-reduce = (f32[5]{0:T(128)S(1)}, f32[5]{0:T(128)S(1)}) all-reduce(f32[5]{0:T(128)S(1)} %get-tuple-element.88, f32[5]{0:T(128)S(1)} %get-tuple-element.89), channel_id=1, replica_groups=mesh['gx'=4,'gy'=16,'gz_0'=4,'gz_1'=2] {'gy'}, use_global_device_ids=true, to_apply=%region_15.17 | all-reduce | flops 10 | bytes 80 | tf_op jit(solution)/shard_map/psum | solution.py:18
  263.8 10.7 %all-reduce.1 = (f32[5]{0:T(128)S(1)}, f32[5]{0:T(128)S(1)}) all-reduce(f32[5]{0:T(128)S(1)} %get-tuple-element.84, f32[5]{0:T(128)S(1)} %get-tuple-element.85), channel_id=1, replica_groups=mesh['gx'=4,'gy'=16,'gz_0'=4,'gz_1'=2] {'gz_0'}, use_global_device_ids=true, to_apply=%region_16.18 | all-reduce | flops 10 | bytes 80 | tf_op jit(solution)/shard_map/psum | solution.py:18
  274.4 13.2 %all-reduce.3 = (f32[1,5]{1,0:T(1,128)S(1)}, f32[1,5]{1,0:T(1,128)S(1)}) all-reduce(f32[1,5]{1,0:T(1,128)S(1)} %bitcast.173, f32[1,5]{1,0:T(1,128)S(1)} %bitcast.174), channel_id=1, replica_groups=mesh['gx'=4,'gy'=16,'gz_0'=4,'gz_1'=2] {'gz_1'}, use_global_device_ids=true, to_apply=%region_17.19 | all-reduce | flops 10 | bytes 80 | tf_op jit(solution)/shard_map/psum | solution.py:18
  291.6 7.2 %reshape.313 = f32[64,20480]{1,0:T(8,128)} reshape(f32[32,2,20480]{2,1,0:T(2,128)} %all-to-all-done.1) | data formatting | bytes 10485760 | tf_op jit(solution)/shard_map/reshape | solution.py:112
  298.8 4.3 %fusion.54 = f32[3,20480]{1,0:T(4,128)S(1)} fusion(f32[64,20480]{1,0:T(8,128)} %reshape.313, s32[64]{0:T(128)S(1)} %eq.121), kind=kOutput, calls=%fused_computation.116 | convolution fusion | flops 47186112 | bytes 5488896 | tf_op jit(solution)/shard_map/dot_general | solution.py:117
  304.7 2.5 fusion.60
  307.2 3.0 copy.127
  310.4 3.0 copy.128
  314.4 4.6 %collective-permute-start = (f32[3,5,6,256]{3,0,1,2:T(4,128)S(1)}, f32[3,5,6,256]{3,0,1,2:T(4,128)S(1)}, u32[]{:S(2)}, u32[]{:S(2)}) collective-permute-start(f32[3,5,6,256]{3,0,1,2:T(4,128)S(1)} %bitcast.169), channel_id=1, source_target_pairs={{0,1},{1,2},{2,3},{3,4},{4,5},{5,6},{6,7},{7,8},{8,9},{9,10},{10,1... | collective-permute-start | bytes 276488 | tf_op jit(solution)/shard_map/ppermute | solution.py:25
  318.9 1.9 collective-permute-start.1
  320.9 1.0 stack.27
  322.4 0.7 copy.129
  323.1 4.2 %collective-permute-done.1 = f32[3,5,6,256]{3,0,1,2:T(4,128)S(1)} collective-permute-done((f32[3,5,6,256]{3,0,1,2:T(4,128)S(1)}, f32[3,5,6,256]{3,0,1,2:T(4,128)S(1)}, u32[]{:S(2)}, u32[]{:S(2)}) %collective-permute-start.1) | collective-permute-done | bytes 92192 | tf_op jit(solution)/shard_map/ppermute | solution.py:25
  327.3 1.1 fusion.41
  (107 shorter events, 15.8 us)
Async XLA Ops:
  3.1 161.4 %all-to-all-start = ((s32[32,1,2]{2,1,0:T(1,128)}), s32[32,1,2]{2,1,0:T(1,128)S(1)}, u32[]{:S(2)}, u32[]{:S(2)}) async-start(s32[32,1,2]{2,1,0:T(1,128)} %bitcast.25), calls=%async_computation | async-start | bytes 32768 | tf_op jit(solution)/shard_map/all_to_all | solution.py:108
  164.4 127.2 %all-to-all-start.1 = ((f32[32,2,20480]{2,1,0:T(2,128)}), f32[32,2,20480]{2,1,0:T(2,128)}, u32[]{:S(2)}, u32[]{:S(2)}) async-start(f32[32,2,20480]{2,1,0:T(2,128)} %select_select_fusion), calls=%async_computation.1 | async-start | bytes 10485760 | tf_op jit(solution)/shard_map/all_to_all | solution.py:101
  171.9 2.3 copy-start
  172.0 115.7 %copy-start.2 = (s32[3,6]{1,0:T(4,128)S(1)}, s32[3,6]{1,0:T(4,128)}, u32[]{:S(2)}) copy-start(s32[3,6]{1,0:T(4,128)} %param.18) | copy-start | bytes 220
  172.0 117.1 %copy-start.5 = (s32[3,6]{1,0:T(4,128)S(1)}, s32[3,6]{1,0:T(4,128)}, u32[]{:S(2)}) copy-start(s32[3,6]{1,0:T(4,128)} %param.19) | copy-start | bytes 220
  313.5 8.4 %copy-start.1 = (f32[3,5,1,16,16]{4,3,1,0,2:T(8,128)S(1)}, f32[3,5,1,16,16]{4,3,1,0,2:T(8,128)}, u32[]{:S(2)}) copy-start(f32[3,5,1,16,16]{4,3,1,0,2:T(8,128)} %get-tuple-element.102) | copy-start | bytes 46084
  313.5 13.7 %copy-start.3 = (f32[3,6]{0,1:T(8,128)S(1)}, f32[3,6]{0,1:T(8,128)}, u32[]{:S(2)}) copy-start(f32[3,6]{0,1:T(8,128)} %copy.111) | copy-start | bytes 220
  313.5 13.7 %copy-start.4 = (s32[3,6]{0,1:T(8,128)S(1)}, s32[3,6]{0,1:T(8,128)}, u32[]{:S(2)}) copy-start(s32[3,6]{0,1:T(8,128)} %copy.103) | copy-start | bytes 220
  314.4 8.7 %collective-permute-start = (f32[3,5,6,256]{3,0,1,2:T(4,128)S(1)}, f32[3,5,6,256]{3,0,1,2:T(4,128)S(1)}, u32[]{:S(2)}, u32[]{:S(2)}) collective-permute-start(f32[3,5,6,256]{3,0,1,2:T(4,128)S(1)} %bitcast.169), channel_id=1, source_target_pairs={{0,1},{1,2},{2,3},{3,4},{4,5},{5,6},{6,7},{7,8},{8,9},{9,10},{10,1... | collective-permute-start | bytes 276488 | tf_op jit(solution)/shard_map/ppermute | solution.py:25
  318.9 8.3 %collective-permute-start.1 = (f32[3,5,6,256]{3,0,1,2:T(4,128)S(1)}, f32[3,5,6,256]{3,0,1,2:T(4,128)S(1)}, u32[]{:S(2)}, u32[]{:S(2)}) collective-permute-start(f32[3,5,6,256]{3,0,1,2:T(4,128)S(1)} %bitcast.170), channel_id=1, source_target_pairs={{1,0},{2,1},{3,2},{4,3},{5,4},{6,5},{7,6},{8,7},{9,8},{10,9},{11,1... | collective-permute-start | bytes 276488 | tf_op jit(solution)/shard_map/ppermute | solution.py:25
where the time goes:
time: 330 us; the launch traced here: 329 us
  blocking collectives  113 us (34%)
  matrix products  90.7 us (27%)
  local copies, waits for them, and re-layouts  75.4 us (23%)
  starting transfers between devices  23.4 us (7%)
  other arithmetic  21 us (6%)
  waiting for transfers between devices  4.16 us (1%)
    psum x4, blocking collectives, one_axis_at_a_time(): shard = lax.psum(shard, axis)  113 us
    dot_general x4, matrix products, remap_block(): jnp.einsum('bjn,bfinl->bfijl', weight_y, section_x, precision=precise)  41.6 us
    dot_general x4, matrix products, remap_block(): jnp.einsum('bkl,bfijl->bfijk', weight_z, section_y, precision=precise)  40.8 us
    broadcast_in_dim x4, local copies, waits for them, and re-layouts, body(): lax.map(remap_block, (source.reshape(blocks, 8, fields, edge_cells, face_...  16.9 us
    reshape x4, local copies, waits for them, and re-layouts, remap_block(): section_x.reshape(block_count, fields, edge_cells, edge_cells, edge_cells)  12.8 us
    gather x2, local copies, waits for them, and re-layouts, body(): taken = jnp.take(flat_partials, source_pair, axis=0)  11 us
    select_n x1, other arithmetic, body(): outgoing = jnp.where(filled[:, None], taken, jnp.zeros_like(taken))  9.71 us
    all_to_all x1, starting transfers between devices, body(): lax.all_to_all(out_slots.reshape(group_size, CAP), GX_GZ, split_axis=0, c...  9.37 us
  transfers between devices with their start and end apart: 4, of which 1 were waited for; matrix products, arithmetic and copies ran while one was open for 49% of the time, Pallas kernels for 0%

commit v1 on v0

v1 whole, which is shorter than its diff:
```python
import functools

import jax
import jax.numpy as jnp
from jax import lax
from jax.experimental import pallas as pl
from jax.experimental.pallas import tpu as pltpu
from jax.sharding import Mesh
from jax.sharding import PartitionSpec as P

ALL_AXES = ("gx", "gy", "gz_0", "gz_1")
PLANE = ("gx", "gz_0")
COLUMN = ("gy", "gz_1")
UNROLL = 4
BF16 = jnp.bfloat16
F32 = jnp.float32
I32 = jnp.int32
VMEM = pltpu.VMEM
SMEM = pltpu.SMEM


def shifted(block, axis, distance):
    devices = range(lax.axis_size(axis))
    route = [(i - distance, i) for i in devices if i - distance in devices]
    return lax.ppermute(block, axis, route)


def halves(block):
    high = block.astype(BF16)
    low = (block - high.astype(F32)).astype(BF16)
    return high, low


def iota(shape, dim):
    return lax.broadcasted_iota(I32, shape, dim)


def partials_kernel(
    place, meta_own, meta_peer, ratio, own, peer,
    out_a, out_b, out_mass,
    table, split, code_k, code_x,
    *, patches, fields, edge, size_x, size_y, chips_y, cores, new_count, pairs,
):
    rows = fields * edge
    lanes = edge * edge
    half = lanes // 2
    index_y = place[0]
    core = place[1]
    size_z = chips_y * cores
    owners = size_x * chips_y * new_count

    def prepare(o, totals):
        block = own[o]
        high, low = halves(block)
        split[o, 0:rows] = high
        split[o, rows:2 * rows] = low
        high, low = halves(peer[o])
        split[patches + o, 0:rows] = high
        split[patches + o, rows:2 * rows] = low
        return totals + (block[:, :half] + block[:, half:])

    old_sums = lax.fori_loop(0, patches, prepare, jnp.zeros((rows, half), F32))

    out_a[...] = jnp.zeros_like(out_a)
    out_b[...] = jnp.zeros_like(out_b)
    cell = iota((lanes, lanes), 0)
    code_k[...] = (cell // edge) * 4096 + cell % edge
    row = iota((rows, 2 * rows), 0)
    col = iota((rows, 2 * rows), 1) % rows
    code_x[...] = (col // edge - row // edge) * 4096 + col % edge

    def enlist(p, found, meta, base):
        dest = meta[5, p]
        mine = dest % cores == core

        @pl.when(mine)
        def _():
            table[0, found] = base + meta[0, p]
            iz = dest % size_z
            ix = dest // size_z
            slot = meta[1, p]
            owner = (ix * size_y + index_y) * size_z + iz
            table[1, found] = ratio[owner * new_count + slot]
            table[2, found] = meta[2, p]
            table[3, found] = meta[3, p] * 4096 + meta[4, p]
            table[4, found] = (ix * chips_y + iz // cores) * new_count + slot
            table[5, found] = ((iz // cores) * size_x + ix) * new_count + slot

        return found + mine.astype(I32)

    found = lax.fori_loop(0, pairs, functools.partial(enlist, meta=meta_own, base=0), jnp.int32(0))
    found = lax.fori_loop(0, pairs, functools.partial(enlist, meta=meta_peer, base=patches), found)

    for extra in range(UNROLL - 1):
        table[0, found + extra] = 0
        table[1, found + extra] = 1
        table[2, found + extra] = 0
        table[3, found + extra] = 0
        table[4, found + extra] = 0
        table[5, found + extra] = 0

    lane_k = iota((1, lanes), 1)
    lane_code = (lane_k // edge) * 4096 + lane_k % edge
    row_x = iota((rows, 1), 0) % edge

    def remap(step, sums):
        results = []
        for u in range(UNROLL):
            p = step * UNROLL + u
            live = (p < found).astype(F32)
            r = table[1, p]
            inverse = jnp.where(r == 2, 0.5, 1.0).astype(F32)
            spread = code_x[...] - (row_x * r + table[2, p])
            weight_x = jnp.where((spread & ~(r - 1)) == 0, inverse, 0.0).astype(BF16)
            section = jnp.dot(weight_x, split[table[0, p]], preferred_element_type=F32)
            spread = code_k[...] - (lane_code * r + table[3, p])
            weight_k = jnp.where((spread & ~((r - 1) * 4097)) == 0, inverse * inverse, 0.0).astype(BF16)
            high, low = halves(section)
            stacked = jnp.concatenate([high, low], axis=0)
            product = jnp.dot(stacked, weight_k, preferred_element_type=F32)
            part = (product[:rows] + product[rows:]) * live
            cube = (r * r * r).astype(F32)
            sums = sums + cube * (part[:, :half] + part[:, half:])
            results.append((p, part))
        for p, part in results:
            to_a = table[4, p]
            to_b = table[5, p]
            out_a[to_a] = out_a[to_a] + part[:, :half]
            out_b[to_b] = out_b[to_b] + part[:, half:]
        return sums

    steps = (found + UNROLL - 1) // UNROLL
    new_sums = lax.fori_loop(0, steps, remap, jnp.zeros((rows, half), F32))

    lane = iota((1, half), 1)
    lines = []
    for f in range(fields):
        old_f = jnp.sum(old_sums[f * edge:(f + 1) * edge], keepdims=True)
        new_f = jnp.sum(new_sums[f * edge:(f + 1) * edge], keepdims=True)
        lines.append(jnp.where(lane == 0, old_f, jnp.where(lane == 1, new_f, 0.0)))
    lines.append(jnp.zeros((8 - fields, half), F32))
    packed = jnp.concatenate(lines, axis=0)
    out_mass[...] = jnp.broadcast_to(packed[None], out_mass.shape)


def gather_kernel(a, b, new_data, faces, *, count, fields, edge):
    rows = fields * edge
    lanes = edge * edge
    half = lanes // 2
    sources = a.shape[0]
    total_a = a[0]
    total_b = b[0]
    for s in range(1, sources):
        total_a = total_a + a[s]
        total_b = total_b + b[s]
    whole = jnp.concatenate([total_a, total_b], axis=1)
    new_data[...] = whole
    high, low = halves(whole)
    stacked = jnp.concatenate([high, low], axis=0)
    source = iota((lanes, lanes), 0)
    target = iota((lanes, lanes), 1) % edge
    here = (iota((edge, lanes), 1) // edge) == iota((edge, lanes), 0)
    picks = (
        source == target,
        source == target + (lanes - edge),
        source == target * edge,
        source == target * edge + (edge - 1),
    )
    for q in range(count):
        for f in range(fields):
            start = q * rows + f * edge
            faces[q, 0, f:f + 1, :] = whole[start:start + 1]
            faces[q, 1, f:f + 1, :] = whole[start + edge - 1:start + edge]
    for e, pick in enumerate(picks):
        weight = jnp.where(pick, 1.0, 0.0).astype(BF16)
        product = jnp.dot(stacked, weight, preferred_element_type=F32)
        layer = product[:count * rows] + product[count * rows:]
        for q in range(count):
            for f in range(fields):
                start = q * rows + f * edge
                line = jnp.sum(jnp.where(here, layer[start:start + edge], 0.0), axis=0, keepdims=True)
                faces[q, 2 + e, f:f + 1, :] = line


def jump_kernel(place, side, patch, own, before, after, jump, *, count, fields, devices):
    linear = place[2]
    for q in range(count):
        for e in range(6):
            u = side[q, e]
            n = patch[q, e]
            at = linear + u - 1
            present = (u < 3) & (at >= 0) & (at < devices)
            other = e ^ 1
            ghost = jnp.where(
                u == 0, before[n, other], jnp.where(u == 1, own[n, other], after[n, other])
            )
            line = jnp.where(present, ghost - own[q, e], 0.0)
            for f in range(fields):
                jump[q, f, e:e + 1, :] = line[f:f + 1]


def body(
    old_data, pair_old, pair_slot, pair_shift, pair_dest, new_ratio, neighbor_side, neighbor_patch
):
    patches, fields, edge, lanes = old_data.shape
    pairs = pair_old.shape[0]
    count = neighbor_side.shape[0]
    rows = fields * edge
    half = lanes // 2
    size_x = lax.axis_size("gx")
    size_y = lax.axis_size("gy")
    chips_y = lax.axis_size("gz_0")
    cores = lax.axis_size("gz_1")
    devices = size_x * size_y * chips_y * cores
    index_y = lax.axis_index("gy")
    core = lax.axis_index("gz_1")
    linear = (lax.axis_index("gx") * size_y + index_y) * chips_y * cores + lax.axis_index("gz_0") * cores + core
    place = jnp.stack([index_y, core, linear]).astype(I32)
    meta = jnp.concatenate(
        [pair_old[None], pair_slot[None], pair_shift.T, pair_dest.T], axis=0
    )
    own = old_data.reshape(patches, rows, lanes)
    swap = [(i, cores - 1 - i) for i in range(cores)]
    peer_meta = lax.ppermute(meta, "gz_1", swap)
    peer = lax.ppermute(own, "gz_1", swap)
    owners = size_x * chips_y * count
    smem = pl.BlockSpec(memory_space=SMEM)
    vmem = pl.BlockSpec(memory_space=VMEM)
    out_a, out_b, mass = pl.pallas_call(
        functools.partial(
            partials_kernel, patches=patches, fields=fields, edge=edge, size_x=size_x,
            size_y=size_y, chips_y=chips_y, cores=cores, new_count=count, pairs=pairs,
        ),
        out_shape=(
            jax.ShapeDtypeStruct((owners, rows, half), F32),
            jax.ShapeDtypeStruct((owners, rows, half), F32),
            jax.ShapeDtypeStruct((size_y * cores, 8, half), F32),
        ),
        in_specs=[smem, smem, smem, smem, vmem, vmem],
        out_specs=(vmem, vmem, vmem),
        scratch_shapes=[
            pltpu.SMEM((6, 2 * pairs + UNROLL), I32),
            pltpu.VMEM((2 * patches, 2 * rows, lanes), BF16),
            pltpu.VMEM((lanes, lanes), I32),
            pltpu.VMEM((rows, 2 * rows), I32),
        ],
        name="partials",
    )(place, meta, peer_meta, new_ratio, own, peer)

    first_a = lax.all_to_all(out_a, "gx", 0, 0, tiled=True)
    first_b = lax.all_to_all(out_b, "gz_0", 0, 0, tiled=True)
    column = lax.all_to_all(mass, COLUMN, 0, 0, tiled=True)
    column_sum = jnp.broadcast_to(jnp.sum(column, axis=0)[None], (size_x * chips_y, 8, half))
    plane = lax.all_to_all(column_sum, PLANE, 0, 0, tiled=True)
    mid_a = jnp.sum(first_a.reshape(size_x, chips_y * count * rows, half), axis=0)
    mid_b = jnp.sum(first_b.reshape(chips_y, size_x * count * rows, half), axis=0)
    last_a = lax.all_to_all(mid_a.reshape(chips_y * count, rows, half), "gz_0", 0, 0, tiled=True)
    last_b = lax.all_to_all(mid_b.reshape(size_x * count, rows, half), "gx", 0, 0, tiled=True)

    new_data, faces = pl.pallas_call(
        functools.partial(gather_kernel, count=count, fields=fields, edge=edge),
        out_shape=(
            jax.ShapeDtypeStruct((count * rows, lanes), F32),
            jax.ShapeDtypeStruct((count, 6, fields, lanes), F32),
        ),
        in_specs=[vmem, vmem],
        out_specs=(vmem, vmem),
        name="gather",
    )(
        last_a.reshape(chips_y, count * rows, half),
        last_b.reshape(size_x, count * rows, half),
    )
    before = shifted(faces, ALL_AXES, 1)
    after = shifted(faces, ALL_AXES, -1)
    interface_jump = pl.pallas_call(
        functools.partial(jump_kernel, count=count, fields=fields, devices=devices),
        out_shape=jax.ShapeDtypeStruct((count, fields, 6, lanes), F32),
        in_specs=[smem, smem, smem, vmem, vmem, vmem],
        out_specs=vmem,
        name="jump",
    )(place, neighbor_side, neighbor_patch, faces, before, after)
    total_cells = patches * devices * edge * lanes
    mass_totals = jnp.sum(plane, axis=0)[:fields, :2].T / total_cells
    return (new_data.reshape(count, fields, edge, lanes), interface_jump, mass_totals)


def solution(mesh):
    torus = Mesh(
        mesh.devices.reshape(mesh.shape["gx"], mesh.shape["gy"], 4, 2), ("gx", "gy", "gz_0", "gz_1")
    )
    return jax.shard_map(
        body,
        mesh=torus,
        in_specs=(
            P(ALL_AXES, None, None, None),
            P(ALL_AXES),
            P(ALL_AXES),
            P(ALL_AXES, None),
            P(ALL_AXES, None),
            P(),
            P(ALL_AXES, None),
            P(ALL_AXES, None),
        ),
        out_specs=(P(ALL_AXES, None, None, None), P(ALL_AXES, None, None, None), P()),
        check_vma=False,
    )
```

time: 330 us -> 160 us (0.48)
  the two profiles are of different devices: /device:TPU:25 before, /device:TPU:2 now
where the time goes in v1:
time: 160 us; the launch traced here: 159 us
  blocking collectives  73.9 us (46%)
  waiting for transfers between devices  40.9 us (26%)
  starting transfers between devices  20.6 us (13%)
  Pallas kernels  14.6 us (9%)
  other arithmetic  4.71 us (3%)
  local copies, waits for them, and re-layouts  3.62 us (2%)
    all_to_all x1, blocking collectives, body(): column = lax.all_to_all(mass, COLUMN, 0, 0, tiled=True)  32.7 us
    all_to_all x1, blocking collectives, body(): first_a = lax.all_to_all(out_a, 'gx', 0, 0, tiled=True)  27.3 us
    all_to_all x1, waiting for transfers between devices, body(): first_b = lax.all_to_all(out_b, 'gz_0', 0, 0, tiled=True)  19.4 us
    all_to_all x1, blocking collectives, body(): plane = lax.all_to_all(column_sum, PLANE, 0, 0, tiled=True)  13.8 us
    pallas_call x1, Pallas kernels, body(): pl.pallas_call(functools.partial(partials_kernel, patches=patches, fields...  10.5 us
    ppermute x2, waiting for transfers between devices, shifted(): return lax.ppermute(block, axis, route)  7.81 us
    all_to_all x1, waiting for transfers between devices, body(): lax.all_to_all(mid_a.reshape(chips_y * count, rows, half), 'gz_0', 0, 0,...  7.01 us
    all_to_all x1, waiting for transfers between devices, body(): lax.all_to_all(mid_b.reshape(size_x * count, rows, half), 'gx', 0, 0, til...  6.43 us
  transfers between devices with their start and end apart: 7, of which 5 were waited for; matrix products, arithmetic and copies ran while one was open for 3% of the time, Pallas kernels for 0%

profile of v1, /device:TPU:2, one launch (start us, length us, event | category | flops | bytes accessed | tf_op | source)
XLA Modules:
  0.0 159.0 jit_solution(6658289887068532937)
XLA Ops:
  0.6 1.9 %collective-permute-start.1 = (f32[12,80,256]{2,1,0:T(8,128)}, f32[12,80,256]{2,1,0:T(8,128)S(1)}, u32[]{:S(2)}, u32[]{:S(2)}) collective-permute-start(f32[12,80,256]{2,1,0:T(8,128)} %bitcast.25), channel_id=1, source_target_pairs={{0,1},{1,0},{2,3},{3,2},{4,5},{5,4},{6,7},{7,6},{8,9},{9,8},{10,11... | collective-permute-start | bytes 2949128 | tf_op jit(solution)/shard_map/ppermute | solution.py:225
  2.6 0.7 pad_add_fusion.meta_own
  3.3 0.0 copy-start.5
  3.3 2.4 %collective-permute-start = (s32[6,32]{1,0:T(8,128)S(1)}, s32[6,32]{1,0:T(8,128)S(1)}, u32[]{:S(2)}, u32[]{:S(2)}) collective-permute-start(s32[6,32]{1,0:T(8,128)S(1)} %pad_add_fusion.meta_own), channel_id=1, source_target_pairs={{0,1},{1,0},{2,3},{3,2},{4,5},{5,4},{6,7},{7,6},{8,9},{9,8},{10,11... | collective-permute-start | bytes 2312 | tf_op jit(solution)/shard_map/ppermute | solution.py:224
  5.7 0.6 pad_add_fusion.1.place
  6.3 0.2 collective-permute-done.meta_peer
  6.5 0.0 copy-start.6
  6.5 0.0 collective-permute-done.1.peer
  6.5 0.0 copy-done.5
  6.5 0.6 copy-done.6
  7.1 0.0 copy-start.2
  7.1 0.9 copy-done.2
  8.0 10.5 %partials.1 = (f32[48,80,128]{2,1,0:T(8,128)}, f32[48,80,128]{2,1,0:T(8,128)}, f32[32,8,128]{2,1,0:T(8,128)}) custom-call(s32[3]{0:T(128)} %pad_add_fusion.1.place, s32[6,32]{1,0:T(8,128)} %copy-done.5, s32[6,32]{1,0:T(8,128)} %copy-done.6, s32[1536]{0:T(1024)} %ratio.1, f32[12,80,256]{2,1,0:T(8,128)} %bitcast.26, f32[12,80,256]{2,1,0:T(8,128)} %copy-done.2), custom_call_target="tpu_custom_call" | custom-call | tf_op jit(solution)/shard_map/partials/pallas_call | solution.py:229
  18.5 32.7 %all_to_all.30 = f32[32,8,128]{2,1,0:T(8,128)S(1)} all-to-all(f32[32,8,128]{2,1,0:T(8,128)} %get-tuple-element.12), channel_id=1, replica_groups=mesh['gx'=4,'gy'=16,'gz_0'=4,'gz_1'=2] {'gy','gz_1'}, dimensions={0} | all-to-all | bytes 262144 | tf_op jit(solution)/shard_map/all_to_all | solution.py:252
  51.3 13.8 %all_to_all.31 = f32[16,8,128]{2,1,0:T(8,128)S(1)} all-to-all(f32[16,8,128]{2,1,0:T(8,128)S(1)} %broadcast_in_dim.14), channel_id=1, replica_groups=mesh['gx'=4,'gy'=16,'gz_0'=4,'gz_1'=2] {'gx','gz_0'}, dimensions={0} | all-to-all | bytes 131072 | tf_op jit(solution)/shard_map/all_to_all | solution.py:254
  65.1 27.3 %all_to_all.32 = f32[48,80,128]{2,1,0:T(8,128)} all-to-all(f32[48,80,128]{2,1,0:T(8,128)} %get-tuple-element.8), channel_id=1, replica_groups=mesh['gx'=4,'gy'=16,'gz_0'=4,'gz_1'=2] {'gx'}, dimensions={0} | all-to-all | bytes 3932160 | tf_op jit(solution)/shard_map/all_to_all | solution.py:250
  92.4 3.6 %all-to-all-start.2 = ((f32[48,80,128]{2,1,0:T(8,128)}), f32[48,80,128]{2,1,0:T(8,128)S(1)}, u32[]{:S(2)}, u32[]{:S(2)}) async-start(f32[48,80,128]{2,1,0:T(8,128)} %get-tuple-element.9), calls=%async_computation.2 | async-start | bytes 3932160 | tf_op jit(solution)/shard_map/all_to_all | solution.py:251
  96.0 2.5 %bitcast_reduce_fusion.1 = f32[960,128]{1,0:T(8,128)} fusion(f32[4,960,128]{2,1,0:T(8,128)} %bitcast.22), kind=kLoop, calls=%fused_computation.1 | loop fusion | flops 368640 | bytes 2457600 | tf_op jit(solution)/shard_map/reduce_sum | solution.py:255
  98.5 19.4 %all-to-all-done.2 = f32[48,80,128]{2,1,0:T(8,128)S(1)} async-done(((f32[48,80,128]{2,1,0:T(8,128)}), f32[48,80,128]{2,1,0:T(8,128)S(1)}, u32[]{:S(2)}, u32[]{:S(2)}) %all-to-all-start.2) | async-done | bytes 1966112 | tf_op jit(solution)/shard_map/all_to_all | solution.py:251
  117.9 3.5 %all-to-all-start.1 = ((f32[12,80,128]{2,1,0:T(8,128)}), f32[12,80,128]{2,1,0:T(8,128)S(1)}, u32[]{:S(2)}, u32[]{:S(2)}) async-start(f32[12,80,128]{2,1,0:T(8,128)} %bitcast.9), calls=%async_computation.1 | async-start | bytes 983040 | tf_op jit(solution)/shard_map/all_to_all | solution.py:257
  121.4 0.9 bitcast_reduce_fusion
  122.3 7.0 %all-to-all-done.1 = f32[12,80,128]{2,1,0:T(8,128)S(1)} async-done(((f32[12,80,128]{2,1,0:T(8,128)}), f32[12,80,128]{2,1,0:T(8,128)S(1)}, u32[]{:S(2)}, u32[]{:S(2)}) %all-to-all-start.1) | async-done | bytes 491552 | tf_op jit(solution)/shard_map/all_to_all | solution.py:257
  129.3 0.0 copy-start
  129.3 4.9 %all-to-all-start.3 = ((f32[12,80,128]{2,1,0:T(8,128)}), f32[12,80,128]{2,1,0:T(8,128)S(1)}, u32[]{:S(2)}, u32[]{:S(2)}) async-start(f32[12,80,128]{2,1,0:T(8,128)} %bitcast.12), calls=%async_computation.3 | async-start | bytes 983040 | tf_op jit(solution)/shard_map/all_to_all | solution.py:258
  134.2 6.4 %all-to-all-done.3 = f32[12,80,128]{2,1,0:T(8,128)S(1)} async-done(((f32[12,80,128]{2,1,0:T(8,128)}), f32[12,80,128]{2,1,0:T(8,128)S(1)}, u32[]{:S(2)}, u32[]{:S(2)}) %all-to-all-start.3) | async-done | bytes 491552 | tf_op jit(solution)/shard_map/all_to_all | solution.py:258
  140.6 0.0 copy-start.1
  140.6 0.0 copy-done
  140.6 0.8 copy-done.1
  141.4 2.3 %gather.1 = (f32[240,256]{1,0:T(8,128)}, f32[3,6,5,256]{3,2,1,0:T(8,128)}) custom-call(f32[4,240,128]{2,1,0:T(8,128)} %bitcast.23, f32[4,240,128]{2,1,0:T(8,128)} %bitcast.24), custom_call_target="tpu_custom_call" | custom-call | tf_op jit(solution)/shard_map/gather/pallas_call | solution.py:260
  143.7 1.9 %collective-permute-start.3 = (f32[3,6,5,256]{3,2,1,0:T(8,128)}, f32[3,6,5,256]{3,2,1,0:T(8,128)S(1)}, u32[]{:S(2)}, u32[]{:S(2)}) collective-permute-start(f32[3,6,5,256]{3,2,1,0:T(8,128)} %get-tuple-element.11.own), channel_id=1, source_target_pairs={{1,0},{2,1},{3,2},{4,3},{5,4},{6,5},{7,6},{8,7},{9,8},{10,9},{11,1... | collective-permute-start | bytes 276488 | tf_op jit(solution)/shard_map/ppermute | solution.py:25
  145.6 2.4 %collective-permute-start.2 = (f32[3,6,5,256]{3,2,1,0:T(8,128)}, f32[3,6,5,256]{3,2,1,0:T(8,128)S(1)}, u32[]{:S(2)}, u32[]{:S(2)}) collective-permute-start(f32[3,6,5,256]{3,2,1,0:T(8,128)} %get-tuple-element.11.own), channel_id=1, source_target_pairs={{0,1},{1,2},{2,3},{3,4},{4,5},{5,6},{6,7},{7,8},{8,9},{9,10},{10,1... | collective-permute-start | bytes 276488 | tf_op jit(solution)/shard_map/ppermute | solution.py:25
  148.0 0.6 copy.11
  148.7 0.0 collective-permute-done.3.after
  148.7 0.0 copy-start.3
  148.7 7.8 %collective-permute-done.2.before = f32[3,6,5,256]{3,2,1,0:T(8,128)S(1)} collective-permute-done((f32[3,6,5,256]{3,2,1,0:T(8,128)}, f32[3,6,5,256]{3,2,1,0:T(8,128)S(1)}, u32[]{:S(2)}, u32[]{:S(2)}) %collective-permute-start.2) | collective-permute-done | bytes 92192 | tf_op jit(solution)/shard_map/ppermute | solution.py:25
  156.5 0.0 copy-done.3
  156.5 0.0 copy-start.4
  156.5 0.7 copy-done.4
  157.2 1.8 %jump.1 = f32[3,5,6,256]{3,2,1,0:T(8,128)} custom-call(s32[3]{0:T(128)} %pad_add_fusion.1.place, s32[3,6]{1,0:T(4,128)} %side.1, s32[3,6]{1,0:T(4,128)} %patch.1, f32[3,6,5,256]{3,2,1,0:T(8,128)} %get-tuple-element.11.own, f32[3,6,5,256]{3,2,1,0:T(8,128)} %copy-done.4, f32[3,6,5,256]{3,2,1,0:T(8,128)} %copy-done.3), custom_call_target="tpu_custom_call" | custom-call | tf_op jit(solution)/shard_map/jump/pallas_call | solution.py:275
  (4 shorter events, 0.1 us)
Async XLA Ops:
  0.6 5.9 %collective-permute-start.1 = (f32[12,80,256]{2,1,0:T(8,128)}, f32[12,80,256]{2,1,0:T(8,128)S(1)}, u32[]{:S(2)}, u32[]{:S(2)}) collective-permute-start(f32[12,80,256]{2,1,0:T(8,128)} %bitcast.25), channel_id=1, source_target_pairs={{0,1},{1,0},{2,3},{3,2},{4,5},{5,4},{6,7},{7,6},{8,9},{9,8},{10,11... | collective-permute-start | bytes 2949128 | tf_op jit(solution)/shard_map/ppermute | solution.py:225
  3.3 3.2 %copy-start.5 = (s32[6,32]{1,0:T(8,128)}, s32[6,32]{1,0:T(8,128)S(1)}, u32[]{:S(2)}) copy-start(s32[6,32]{1,0:T(8,128)S(1)} %pad_add_fusion.meta_own) | copy-start | bytes 2308
  3.3 3.2 %collective-permute-start = (s32[6,32]{1,0:T(8,128)S(1)}, s32[6,32]{1,0:T(8,128)S(1)}, u32[]{:S(2)}, u32[]{:S(2)}) collective-permute-start(s32[6,32]{1,0:T(8,128)S(1)} %pad_add_fusion.meta_own), channel_id=1, source_target_pairs={{0,1},{1,0},{2,3},{3,2},{4,5},{5,4},{6,7},{7,6},{8,9},{9,8},{10,11... | collective-permute-start | bytes 2312 | tf_op jit(solution)/shard_map/ppermute | solution.py:224
  6.5 0.6 copy-start.6
  7.1 0.9 copy-start.2
  92.4 25.5 %all-to-all-start.2 = ((f32[48,80,128]{2,1,0:T(8,128)}), f32[48,80,128]{2,1,0:T(8,128)S(1)}, u32[]{:S(2)}, u32[]{:S(2)}) async-start(f32[48,80,128]{2,1,0:T(8,128)} %get-tuple-element.9), calls=%async_computation.2 | async-start | bytes 3932160 | tf_op jit(solution)/shard_map/all_to_all | solution.py:251
  117.9 11.3 %all-to-all-start.1 = ((f32[12,80,128]{2,1,0:T(8,128)}), f32[12,80,128]{2,1,0:T(8,128)S(1)}, u32[]{:S(2)}, u32[]{:S(2)}) async-start(f32[12,80,128]{2,1,0:T(8,128)} %bitcast.9), calls=%async_computation.1 | async-start | bytes 983040 | tf_op jit(solution)/shard_map/all_to_all | solution.py:257
  129.3 11.4 %copy-start = (f32[12,80,128]{2,1,0:T(8,128)}, f32[12,80,128]{2,1,0:T(8,128)S(1)}, u32[]{:S(2)}) copy-start(f32[12,80,128]{2,1,0:T(8,128)S(1)} %all-to-all-done.1) | copy-start | bytes 1474564
  129.3 11.3 %all-to-all-start.3 = ((f32[12,80,128]{2,1,0:T(8,128)}), f32[12,80,128]{2,1,0:T(8,128)S(1)}, u32[]{:S(2)}, u32[]{:S(2)}) async-start(f32[12,80,128]{2,1,0:T(8,128)} %bitcast.12), calls=%async_computation.3 | async-start | bytes 983040 | tf_op jit(solution)/shard_map/all_to_all | solution.py:258
  140.6 0.8 copy-start.1
  143.7 5.0 %collective-permute-start.3 = (f32[3,6,5,256]{3,2,1,0:T(8,128)}, f32[3,6,5,256]{3,2,1,0:T(8,128)S(1)}, u32[]{:S(2)}, u32[]{:S(2)}) collective-permute-start(f32[3,6,5,256]{3,2,1,0:T(8,128)} %get-tuple-element.11.own), channel_id=1, source_target_pairs={{1,0},{2,1},{3,2},{4,3},{5,4},{6,5},{7,6},{8,7},{9,8},{10,9},{11,1... | collective-permute-start | bytes 276488 | tf_op jit(solution)/shard_map/ppermute | solution.py:25
  145.6 10.9 %collective-permute-start.2 = (f32[3,6,5,256]{3,2,1,0:T(8,128)}, f32[3,6,5,256]{3,2,1,0:T(8,128)S(1)}, u32[]{:S(2)}, u32[]{:S(2)}) collective-permute-start(f32[3,6,5,256]{3,2,1,0:T(8,128)} %get-tuple-element.11.own), channel_id=1, source_target_pairs={{0,1},{1,2},{2,3},{3,4},{4,5},{5,6},{6,7},{7,8},{8,9},{9,10},{10,1... | collective-permute-start | bytes 276488 | tf_op jit(solution)/shard_map/ppermute | solution.py:25
  148.7 7.8 %copy-start.3 = (f32[3,6,5,256]{3,2,1,0:T(8,128)}, f32[3,6,5,256]{3,2,1,0:T(8,128)S(1)}, u32[]{:S(2)}) copy-start(f32[3,6,5,256]{3,2,1,0:T(8,128)S(1)} %collective-permute-done.3.after) | copy-start | bytes 276484
  156.5 0.7 copy-start.4

commit v2 on v1

--- a/solution.py
+++ b/solution.py
@@ -8,9 +8,9 @@
 from jax.sharding import Mesh
 from jax.sharding import PartitionSpec as P
 
+
 ALL_AXES = ("gx", "gy", "gz_0", "gz_1")
 PLANE = ("gx", "gz_0")
-COLUMN = ("gy", "gz_1")
 UNROLL = 4
 BF16 = jnp.bfloat16
 F32 = jnp.float32
@@ -25,6 +25,19 @@
     return lax.ppermute(block, axis, route)
 
 
+def rotated(block, axis, distance):
+    size = lax.axis_size(axis)
+    return lax.ppermute(block, axis, [(i, (i + distance) % size) for i in range(size)])
+
+
+def crossed(block, axis, distance):
+    return block + lax.ppermute(block, axis, [(i, i ^ distance) for i in range(lax.axis_size(axis))])
+
+
+def fast(block):
+    return pltpu.with_memory_space_constraint(block, VMEM)
+
+
 def halves(block):
     high = block.astype(BF16)
     low = (block - high.astype(F32)).astype(BF16)
@@ -35,10 +48,57 @@
     return lax.broadcasted_iota(I32, shape, dim)
 
 
+def mass_kernel(place, meta, ratio, own, out, counts, *, patches, fields, edge, size_y, size_z, new_count, pairs):
+    lanes = edge * edge
+    half = lanes // 2
+    index_y = place[0]
+    counts[...] = jnp.zeros_like(counts)
+    at_x = iota((edge, lanes), 0)
+    at_y = iota((edge, lanes), 1) // edge
+    at_z = iota((edge, lanes), 1) % edge
+
+    def count(p, carry):
+        dest = meta[5, p]
+        owner = ((dest // size_z) * size_y + index_y) * size_z + dest % size_z
+        reach = edge * ratio[owner * new_count + meta[1, p]]
+        hit = jnp.full((edge, lanes), True)
+        for a, at in enumerate((at_x, at_y, at_z)):
+            distance = at - meta[2 + a, p]
+            hit = hit & (distance >= 0) & (distance < reach)
+        o = meta[0, p]
+        counts[o] = counts[o] + jnp.where(hit, 1.0, 0.0)
+        return carry
+
+    lax.fori_loop(0, pairs, count, 0)
+
+    def add(o, sums):
+        weight = counts[o]
+        olds, news = sums
+        old_list, new_list = [], []
+        for f in range(fields):
+            block = own[o, f * edge:(f + 1) * edge]
+            scaled = block * weight
+            old_list.append(olds[f] + (block[:, :half] + block[:, half:]))
+            new_list.append(news[f] + (scaled[:, :half] + scaled[:, half:]))
+        return tuple(old_list), tuple(new_list)
+
+    zero = tuple(jnp.zeros((edge, half), F32) for _ in range(fields))
+    olds, news = lax.fori_loop(0, patches, add, (zero, zero))
+    lane = iota((1, half), 1)
+    lines = []
+    for f in range(fields):
+        old_f = jnp.sum(olds[f], keepdims=True)
+        new_f = jnp.sum(news[f], keepdims=True)
+        lines.append(jnp.where(lane == 0, old_f, jnp.where(lane == 1, new_f, 0.0)))
+    lines.append(jnp.zeros((8 - fields, half), F32))
+    packed = jnp.concatenate(lines, axis=0)
+    out[...] = jnp.broadcast_to(packed[None], out.shape)
+
+
 def partials_kernel(
     place, meta_own, meta_peer, ratio, own, peer,
-    out_a, out_b, out_mass,
-    table, split, code_k, code_x,
+    out_a, out_b0, out_b1, out_b2, out_b3,
+    out_b, table, split, code_k, code_x,
     *, patches, fields, edge, size_x, size_y, chips_y, cores, new_count, pairs,
 ):
     rows = fields * edge
@@ -46,20 +106,20 @@
     half = lanes // 2
     index_y = place[0]
     core = place[1]
+    index_x = place[3]
+    chip_y = place[4]
     size_z = chips_y * cores
-    owners = size_x * chips_y * new_count
-
-    def prepare(o, totals):
-        block = own[o]
-        high, low = halves(block)
+
+    def prepare(o, carry):
+        high, low = halves(own[o])
         split[o, 0:rows] = high
         split[o, rows:2 * rows] = low
         high, low = halves(peer[o])
         split[patches + o, 0:rows] = high
         split[patches + o, rows:2 * rows] = low
-        return totals + (block[:, :half] + block[:, half:])
-
-    old_sums = lax.fori_loop(0, patches, prepare, jnp.zeros((rows, half), F32))
+        return carry
+
+    lax.fori_loop(0, patches, prepare, 0)
 
     out_a[...] = jnp.zeros_like(out_a)
     out_b[...] = jnp.zeros_like(out_b)
@@ -84,7 +144,9 @@
             table[2, found] = meta[2, p]
             table[3, found] = meta[3, p] * 4096 + meta[4, p]
             table[4, found] = (ix * chips_y + iz // cores) * new_count + slot
-            table[5, found] = ((iz // cores) * size_x + ix) * new_count + slot
+            step_y = (iz // cores - chip_y) & (chips_y - 1)
+            step_x = (ix - index_x) & (size_x - 1)
+            table[5, found] = (step_y * size_x + step_x) * new_count + slot
 
         return found + mine.astype(I32)
 
@@ -103,7 +165,7 @@
     lane_code = (lane_k // edge) * 4096 + lane_k % edge
     row_x = iota((rows, 1), 0) % edge
 
-    def remap(step, sums):
+    def remap(step, carry):
         results = []
         for u in range(UNROLL):
             p = step * UNROLL + u
@@ -119,40 +181,43 @@
             stacked = jnp.concatenate([high, low], axis=0)
             product = jnp.dot(stacked, weight_k, preferred_element_type=F32)
             part = (product[:rows] + product[rows:]) * live
-            cube = (r * r * r).astype(F32)
-            sums = sums + cube * (part[:, :half] + part[:, half:])
             results.append((p, part))
         for p, part in results:
             to_a = table[4, p]
             to_b = table[5, p]
             out_a[to_a] = out_a[to_a] + part[:, :half]
             out_b[to_b] = out_b[to_b] + part[:, half:]
-        return sums
+        return carry
 
     steps = (found + UNROLL - 1) // UNROLL
-    new_sums = lax.fori_loop(0, steps, remap, jnp.zeros((rows, half), F32))
-
-    lane = iota((1, half), 1)
-    lines = []
-    for f in range(fields):
-        old_f = jnp.sum(old_sums[f * edge:(f + 1) * edge], keepdims=True)
-        new_f = jnp.sum(new_sums[f * edge:(f + 1) * edge], keepdims=True)
-        lines.append(jnp.where(lane == 0, old_f, jnp.where(lane == 1, new_f, 0.0)))
-    lines.append(jnp.zeros((8 - fields, half), F32))
-    packed = jnp.concatenate(lines, axis=0)
-    out_mass[...] = jnp.broadcast_to(packed[None], out_mass.shape)
-
-
-def gather_kernel(a, b, new_data, faces, *, count, fields, edge):
+    lax.fori_loop(0, steps, remap, 0)
+    chunk = size_x * new_count
+    for k, out in enumerate((out_b0, out_b1, out_b2, out_b3)):
+        out[...] = out_b[k * chunk:(k + 1) * chunk]
+
+
+def fold_kernel(a, out):
+    total = a[0]
+    for s in range(1, a.shape[0]):
+        total = total + a[s]
+    out[...] = total
+
+
+def cross_kernel(b0, b1, b2, b3, *outs):
+    count = outs[0].shape[0]
+    for k, out in enumerate(outs):
+        at = slice(k * count, (k + 1) * count)
+        out[...] = (b0[at] + b1[at]) + (b2[at] + b3[at])
+
+
+def gather_kernel(a, b0, b1, b2, b3, new_data, faces, *, count, fields, edge):
     rows = fields * edge
     lanes = edge * edge
-    half = lanes // 2
     sources = a.shape[0]
     total_a = a[0]
-    total_b = b[0]
+    total_b = (b0[...] + b1[...]) + (b2[...] + b3[...])
     for s in range(1, sources):
         total_a = total_a + a[s]
-        total_b = total_b + b[s]
     whole = jnp.concatenate([total_a, total_b], axis=1)
     new_data[...] = whole
     high, low = halves(whole)
@@ -214,8 +279,10 @@
     devices = size_x * size_y * chips_y * cores
     index_y = lax.axis_index("gy")
     core = lax.axis_index("gz_1")
-    linear = (lax.axis_index("gx") * size_y + index_y) * chips_y * cores + lax.axis_index("gz_0") * cores + core
-    place = jnp.stack([index_y, core, linear]).astype(I32)
+    index_x = lax.axis_index("gx")
+    chip_y = lax.axis_index("gz_0")
+    linear = ((index_x * size_y + index_y) * chips_y + chip_y) * cores + core
+    place = jnp.stack([index_y, core, linear, index_x, chip_y]).astype(I32)
     meta = jnp.concatenate(
         [pair_old[None], pair_slot[None], pair_shift.T, pair_dest.T], axis=0
     )
@@ -224,51 +291,85 @@
     peer_meta = lax.ppermute(meta, "gz_1", swap)
     peer = lax.ppermute(own, "gz_1", swap)
     owners = size_x * chips_y * count
+    chunk = owners // chips_y
     smem = pl.BlockSpec(memory_space=SMEM)
     vmem = pl.BlockSpec(memory_space=VMEM)
-    out_a, out_b, mass = pl.pallas_call(
+    params = pltpu.CompilerParams(vmem_limit_bytes=24 * 1024 * 1024)
+    mass = pl.pallas_call(
+        functools.partial(
+            mass_kernel, patches=patches, fields=fields, edge=edge, size_y=size_y,
+            size_z=chips_y * cores, new_count=count, pairs=pairs,
+        ),
+        out_shape=VMEM((size_x * chips_y, 8, half), F32),
+        in_specs=[smem, smem, smem, vmem],
+        out_specs=vmem,
+        scratch_shapes=[pltpu.VMEM((patches, edge, lanes), F32)],
+        compiler_params=params,
+        name="mass",
+    )(place, meta, new_ratio, own)
+    plane = lax.all_to_all(mass, PLANE, 0, 0, tiled=True)
+    out_a, *out_b = pl.pallas_call(
         functools.partial(
             partials_kernel, patches=patches, fields=fields, edge=edge, size_x=size_x,
             size_y=size_y, chips_y=chips_y, cores=cores, new_count=count, pairs=pairs,
         ),
-        out_shape=(
-            jax.ShapeDtypeStruct((owners, rows, half), F32),
-            jax.ShapeDtypeStruct((owners, rows, half), F32),
-            jax.ShapeDtypeStruct((size_y * cores, 8, half), F32),
-        ),
+        out_shape=(VMEM((owners, rows, half), F32),)
+        + (VMEM((chunk, rows, half), F32),) * chips_y,
         in_specs=[smem, smem, smem, smem, vmem, vmem],
-        out_specs=(vmem, vmem, vmem),
+        out_specs=(vmem,) * (1 + chips_y),
         scratch_shapes=[
+            pltpu.VMEM((owners, rows, half), F32),
             pltpu.SMEM((6, 2 * pairs + UNROLL), I32),
             pltpu.VMEM((2 * patches, 2 * rows, lanes), BF16),
             pltpu.VMEM((lanes, lanes), I32),
             pltpu.VMEM((rows, 2 * rows), I32),
         ],
+        compiler_params=params,
         name="partials",
-    )(place, meta, peer_meta, new_ratio, own, peer)
+    )(place, meta, peer_meta, new_ratio, own, fast(peer))
 
     first_a = lax.all_to_all(out_a, "gx", 0, 0, tiled=True)
-    first_b = lax.all_to_all(out_b, "gz_0", 0, 0, tiled=True)
-    column = lax.all_to_all(mass, COLUMN, 0, 0, tiled=True)
-    column_sum = jnp.broadcast_to(jnp.sum(column, axis=0)[None], (size_x * chips_y, 8, half))
-    plane = lax.all_to_all(column_sum, PLANE, 0, 0, tiled=True)
-    mid_a = jnp.sum(first_a.reshape(size_x, chips_y * count * rows, half), axis=0)
-    mid_b = jnp.sum(first_b.reshape(chips_y, size_x * count * rows, half), axis=0)
-    last_a = lax.all_to_all(mid_a.reshape(chips_y * count, rows, half), "gz_0", 0, 0, tiled=True)
-    last_b = lax.all_to_all(mid_b.reshape(size_x * count, rows, half), "gx", 0, 0, tiled=True)
+    for k in (1, 3, 2):
+        out_b[k] = rotated(out_b[k], "gz_0", k)
+    total = jnp.sum(plane, axis=0)
+    total = crossed(total, "gz_1", 1)
+    distance = 1
+    while distance < size_y:
+        total = crossed(total, "gy", distance)
+        distance = distance * 2
+    mid_a = pl.pallas_call(
+        fold_kernel,
+        out_shape=VMEM((chips_y * count, rows, half), F32),
+        in_specs=[vmem],
+        out_specs=vmem,
+        compiler_params=params,
+        name="fold",
+    )(fast(first_a.reshape(size_x, chips_y * count, rows, half)))
+    last_a = lax.all_to_all(mid_a, "gz_0", 0, 0, tiled=True)
+    mid_b = list(pl.pallas_call(
+        cross_kernel,
+        out_shape=(VMEM((count, rows, half), F32),) * size_x,
+        in_specs=[vmem] * chips_y,
+        out_specs=(vmem,) * size_x,
+        compiler_params=params,
+        name="cross",
+    )(*[fast(b) for b in out_b]))
+    for k in (1, 3, 2):
+        mid_b[k] = rotated(mid_b[k], "gx", k)
 
     new_data, faces = pl.pallas_call(
         functools.partial(gather_kernel, count=count, fields=fields, edge=edge),
         out_shape=(
             jax.ShapeDtypeStruct((count * rows, lanes), F32),
-            jax.ShapeDtypeStruct((count, 6, fields, lanes), F32),
+            VMEM((count, 6, fields, lanes), F32),
         ),
-        in_specs=[vmem, vmem],
+        in_specs=[vmem] * (1 + size_x),
         out_specs=(vmem, vmem),
+        compiler_params=params,
         name="gather",
     )(
-        last_a.reshape(chips_y, count * rows, half),
-        last_b.reshape(size_x, count * rows, half),
+        fast(last_a.reshape(chips_y, count * rows, half)),
+        *[fast(b.reshape(count * rows, half)) for b in mid_b],
     )
     before = shifted(faces, ALL_AXES, 1)
     after = shifted(faces, ALL_AXES, -1)
@@ -278,9 +379,9 @@
         in_specs=[smem, smem, smem, vmem, vmem, vmem],
         out_specs=vmem,
         name="jump",
-    )(place, neighbor_side, neighbor_patch, faces, before, after)
+    )(place, neighbor_side, neighbor_patch, fast(faces), fast(before), fast(after))
     total_cells = patches * devices * edge * lanes
-    mass_totals = jnp.sum(plane, axis=0)[:fields, :2].T / total_cells
+    mass_totals = total[:fields, :2].T / total_cells
     return (new_data.reshape(count, fields, edge, lanes), interface_jump, mass_totals)
 
 

time: 160 us -> 135 us (0.84)
  the two profiles are of different devices: /device:TPU:2 before, /device:TPU:25 now
where the time goes in v2:
time: 135 us; the launch traced here: 133 us
  starting transfers between devices  79.2 us (59%)
  waiting for transfers between devices  30.6 us (23%)
  Pallas kernels  15 us (11%)
  local copies, waits for them, and re-layouts  6.26 us (5%)
    ppermute x5, starting transfers between devices, crossed(): lax.ppermute(block, axis, [(i, i ^ distance) for i in range(lax.axis_size...  26 us
    ppermute x6, starting transfers between devices, rotated(): lax.ppermute(block, axis, [(i, (i + distance) % size) for i in range(size)])  20.8 us
    ppermute x5, waiting for transfers between devices, crossed(): lax.ppermute(block, axis, [(i, i ^ distance) for i in range(lax.axis_size...  10 us
    all_to_all x1, waiting for transfers between devices, body(): first_a = lax.all_to_all(out_a, 'gx', 0, 0, tiled=True)  9.96 us
    all_to_all x1, starting transfers between devices, body(): plane = lax.all_to_all(mass, PLANE, 0, 0, tiled=True)  9.86 us
    ppermute x2, starting transfers between devices, shifted(): return lax.ppermute(block, axis, route)  8.76 us
    pallas_call x1, Pallas kernels, body(): pl.pallas_call(functools.partial(partials_kernel, patches=patches, fields...  7.97 us
    unnamed x19, local copies, waits for them, and re-layouts  6.18 us
  transfers between devices with their start and end apart: 18, of which 9 were waited for; matrix products, arithmetic and copies ran while one was open for 1% of the time, Pallas kernels for 4%

profile of v2, /device:TPU:25, one launch (start us, length us, event | category | flops | bytes accessed | tf_op | source)
XLA Modules:
  0.0 132.7 jit_solution(9737250468824502023)
XLA Ops:
  0.6 2.6 %collective-permute-start.1 = (f32[12,80,256]{2,1,0:T(8,128)}, f32[12,80,256]{2,1,0:T(8,128)S(1)}, u32[]{:S(2)}, u32[]{:S(2)}) collective-permute-start(f32[12,80,256]{2,1,0:T(8,128)} %bitcast.20), channel_id=1, source_target_pairs={{0,1},{1,0},{2,3},{3,2},{4,5},{5,4},{6,7},{7,6},{8,9},{9,8},{10,11... | collective-permute-start | bytes 2949128 | tf_op jit(solution)/shard_map/ppermute | solution.py:292
  3.2 0.7 pad_add_fusion.meta_own.meta
  3.9 1.9 %collective-permute-start = (s32[6,32]{1,0:T(8,128)S(1)}, s32[6,32]{1,0:T(8,128)S(1)}, u32[]{:S(2)}, u32[]{:S(2)}) collective-permute-start(s32[6,32]{1,0:T(8,128)S(1)} %pad_add_fusion.meta_own.meta), channel_id=1, source_target_pairs={{0,1},{1,0},{2,3},{3,2},{4,5},{5,4},{6,7},{7,6},{8,9},{9,8},{10,11... | collective-permute-start | bytes 2312 | tf_op jit(solution)/shard_map/ppermute | solution.py:291
  5.9 0.1 stack.23.place
  6.0 1.0 collective-permute-done.meta_peer
  7.0 1.2 copy-done
  8.2 0.7 copy-done.3
  8.9 8.0 %partials.1 = (f32[48,80,128]{2,1,0:T(8,128)S(1)}, f32[12,80,128]{2,1,0:T(8,128)S(1)}, f32[12,80,128]{2,1,0:T(8,128)S(1)}, f32[12,80,128]{2,1,0:T(8,128)S(1)}, f32[12,80,128]{2,1,0:T(8,128)S(1)}) custom-call(s32[5]{0:T(128)S(1)} %stack.23.place, s32[6,32]{1,0:T(8,128)S(1)} %pad_add_fusion.meta_own.meta, s32[6,32]{1,0:T(8,128)S(1)} %collective-permute-done.meta_peer, ...), custom_call_target="tpu_custom_call" | custom-call | tf_op jit(solution)/shard_map/partials/pallas_call | solution.py:311
  16.9 1.3 copy-done.2
  18.2 0.8 copy-done.6
  18.9 0.8 copy-done.7
  19.7 0.8 copy-done.8
  20.5 4.1 %all-to-all-start = ((f32[48,80,128]{2,1,0:T(8,128)}), f32[48,80,128]{2,1,0:T(8,128)S(1)}, u32[]{:S(2)}, u32[]{:S(2)}) async-start(f32[48,80,128]{2,1,0:T(8,128)} %copy-done.2), calls=%async_computation | async-start | bytes 3932160 | tf_op jit(solution)/shard_map/all_to_all | solution.py:331
  24.7 7.3 %collective-permute-start.2 = (f32[12,80,128]{2,1,0:T(8,128)}, f32[12,80,128]{2,1,0:T(8,128)}, u32[]{:S(2)}, u32[]{:S(2)}) collective-permute-start(f32[12,80,128]{2,1,0:T(8,128)} %copy-done.8), channel_id=1, source_target_pairs={{0,2},{2,4},{4,6},{6,0},{1,3},{3,5},{5,7},{7,1},{8,10},{10,12},{12... | collective-permute-start | bytes 1474568 | tf_op jit(solution)/shard_map/ppermute | solution.py:30
  32.0 1.9 %collective-permute-start.3 = (f32[12,80,128]{2,1,0:T(8,128)}, f32[12,80,128]{2,1,0:T(8,128)}, u32[]{:S(2)}, u32[]{:S(2)}) collective-permute-start(f32[12,80,128]{2,1,0:T(8,128)} %copy-done.7), channel_id=1, source_target_pairs={{0,4},{2,6},{4,0},{6,2},{1,5},{3,7},{5,1},{7,3},{8,12},{10,14},{12... | collective-permute-start | bytes 1474568 | tf_op jit(solution)/shard_map/ppermute | solution.py:30
  33.9 2.5 %collective-permute-start.4 = (f32[12,80,128]{2,1,0:T(8,128)}, f32[12,80,128]{2,1,0:T(8,128)}, u32[]{:S(2)}, u32[]{:S(2)}) collective-permute-start(f32[12,80,128]{2,1,0:T(8,128)} %copy-done.6), channel_id=1, source_target_pairs={{0,6},{2,0},{4,2},{6,4},{1,7},{3,1},{5,3},{7,5},{8,14},{10,8},{12,... | collective-permute-start | bytes 1474568 | tf_op jit(solution)/shard_map/ppermute | solution.py:30
  36.4 2.4 %mass.1 = f32[16,8,128]{2,1,0:T(8,128)} custom-call(s32[5]{0:T(128)S(1)} %stack.23.place, s32[6,32]{1,0:T(8,128)S(1)} %pad_add_fusion.meta_own.meta, s32[1536]{0:T(1024)S(1)} %copy-done.4, f32[12,80,256]{2,1,0:T(8,128)S(1)} %bitcast.22), custom_call_target="tpu_custom_call" | custom-call | tf_op jit(solution)/shard_map/mass/pallas_call | solution.py:298
  38.9 10.0 %all-to-all-done = f32[48,80,128]{2,1,0:T(8,128)S(1)} async-done(((f32[48,80,128]{2,1,0:T(8,128)}), f32[48,80,128]{2,1,0:T(8,128)S(1)}, u32[]{:S(2)}, u32[]{:S(2)}) %all-to-all-start) | async-done | bytes 1966112 | tf_op jit(solution)/shard_map/all_to_all | solution.py:331
  48.8 9.9 %all-to-all-start.2 = ((f32[16,8,128]{2,1,0:T(8,128)}), f32[16,8,128]{2,1,0:T(8,128)S(1)}, u32[]{:S(2)}, u32[]{:S(2)}) async-start(f32[16,8,128]{2,1,0:T(8,128)} %mass.1), calls=%async_computation.2 | async-start | bytes 131072 | tf_op jit(solution)/shard_map/all_to_all | solution.py:310
  58.7 0.9 fold.1
  59.6 4.1 %all-to-all-done.2 = f32[16,8,128]{2,1,0:T(8,128)S(1)} async-done(((f32[16,8,128]{2,1,0:T(8,128)}), f32[16,8,128]{2,1,0:T(8,128)S(1)}, u32[]{:S(2)}, u32[]{:S(2)}) %all-to-all-start.2) | async-done | bytes 65568 | tf_op jit(solution)/shard_map/all_to_all | solution.py:310
  63.6 5.1 %all-to-all-start.1 = ((f32[12,80,128]{2,1,0:T(8,128)}), f32[12,80,128]{2,1,0:T(8,128)S(1)}, u32[]{:S(2)}, u32[]{:S(2)}) async-start(f32[12,80,128]{2,1,0:T(8,128)} %fold.1), calls=%async_computation.1 | async-start | bytes 983040 | tf_op jit(solution)/shard_map/all_to_all | solution.py:348
  68.8 0.0 collective-permute-done.2.b1
  68.8 0.0 collective-permute-done.3.b2
  68.8 0.0 collective-permute-done.4.b3
  68.8 1.4 %cross.1 = (f32[3,80,128]{2,1,0:T(8,128)S(1)}, f32[3,80,128]{2,1,0:T(8,128)S(1)}, f32[3,80,128]{2,1,0:T(8,128)S(1)}, f32[3,80,128]{2,1,0:T(8,128)S(1)}) custom-call(f32[12,80,128]{2,1,0:T(8,128)S(1)} %get-tuple-element.15.b0, f32[12,80,128]{2,1,0:T(8,128)} %collective-permute-done.2.b1, f32[12,80,128]{2,1,0:T(8,128)} %collective-permute-done.3.b2, ...), custom_call_target="tpu_custom_call" | custom-call | tf_op jit(solution)/shard_map/cross/pallas_call | solution.py:349
  70.2 2.2 %collective-permute-start.5 = (f32[3,80,128]{2,1,0:T(8,128)S(1)}, f32[3,80,128]{2,1,0:T(8,128)S(1)}, u32[]{:S(2)}, u32[]{:S(2)}) collective-permute-start(f32[3,80,128]{2,1,0:T(8,128)S(1)} %get-tuple-element.20), channel_id=1, source_target_pairs={{0,128},{128,256},{256,384},{384,0},{1,129},{129,257},{257,385},{3... | collective-permute-start | bytes 368648 | tf_op jit(solution)/shard_map/ppermute | solution.py:30
  72.4 3.7 %collective-permute-start.6 = (f32[3,80,128]{2,1,0:T(8,128)S(1)}, f32[3,80,128]{2,1,0:T(8,128)S(1)}, u32[]{:S(2)}, u32[]{:S(2)}) collective-permute-start(f32[3,80,128]{2,1,0:T(8,128)S(1)} %get-tuple-element.21), channel_id=1, source_target_pairs={{0,256},{128,384},{256,0},{384,128},{1,257},{129,385},{257,1},{385... | collective-permute-start | bytes 368648 | tf_op jit(solution)/shard_map/ppermute | solution.py:30
  76.1 3.2 %collective-permute-start.7 = (f32[3,80,128]{2,1,0:T(8,128)S(1)}, f32[3,80,128]{2,1,0:T(8,128)S(1)}, u32[]{:S(2)}, u32[]{:S(2)}) collective-permute-start(f32[3,80,128]{2,1,0:T(8,128)S(1)} %get-tuple-element.22), channel_id=1, source_target_pairs={{0,384},{128,0},{256,128},{384,256},{1,385},{129,1},{257,129},{385... | collective-permute-start | bytes 368648 | tf_op jit(solution)/shard_map/ppermute | solution.py:30
  79.3 4.4 %collective-permute-start.10 = (f32[8,128]{1,0:T(8,128)S(1)}, f32[8,128]{1,0:T(8,128)S(1)}, u32[]{:S(2)}, u32[]{:S(2)}) collective-permute-start(f32[8,128]{1,0:T(8,128)S(1)} %reduce_sum.9), channel_id=1, source_target_pairs={{0,1},{1,0},{2,3},{3,2},{4,5},{5,4},{6,7},{7,6},{8,9},{9,8},{10,11... | collective-permute-start | bytes 12296 | tf_op jit(solution)/shard_map/ppermute | solution.py:34
  83.7 0.8 collective-permute-done.10
  84.5 1.9 %collective-permute-start.11 = (f32[8,128]{1,0:T(8,128)S(1)}, f32[8,128]{1,0:T(8,128)S(1)}, u32[]{:S(2)}, u32[]{:S(2)}) collective-permute-start(f32[8,128]{1,0:T(8,128)S(1)} %add.27), channel_id=1, source_target_pairs={{0,8},{8,0},{16,24},{24,16},{32,40},{40,32},{48,56},{56,48},{64,72... | collective-permute-start | bytes 12296 | tf_op jit(solution)/shard_map/ppermute | solution.py:34
  86.5 2.4 %collective-permute-done.11 = f32[8,128]{1,0:T(8,128)S(1)} collective-permute-done((f32[8,128]{1,0:T(8,128)S(1)}, f32[8,128]{1,0:T(8,128)S(1)}, u32[]{:S(2)}, u32[]{:S(2)}) %collective-permute-start.11) | collective-permute-done | bytes 4128 | tf_op jit(solution)/shard_map/ppermute | solution.py:34
  88.9 1.9 %collective-permute-start.12 = (f32[8,128]{1,0:T(8,128)S(1)}, f32[8,128]{1,0:T(8,128)S(1)}, u32[]{:S(2)}, u32[]{:S(2)}) collective-permute-start(f32[8,128]{1,0:T(8,128)S(1)} %add.28), channel_id=1, source_target_pairs={{0,16},{8,24},{16,0},{24,8},{32,48},{40,56},{48,32},{56,40},{64,80... | collective-permute-start | bytes 12296 | tf_op jit(solution)/shard_map/ppermute | solution.py:34
  90.8 3.3 %collective-permute-done.12 = f32[8,128]{1,0:T(8,128)S(1)} collective-permute-done((f32[8,128]{1,0:T(8,128)S(1)}, f32[8,128]{1,0:T(8,128)S(1)}, u32[]{:S(2)}, u32[]{:S(2)}) %collective-permute-start.12) | collective-permute-done | bytes 4128 | tf_op jit(solution)/shard_map/ppermute | solution.py:34
  94.1 6.1 %collective-permute-start.13 = (f32[8,128]{1,0:T(8,128)S(1)}, f32[8,128]{1,0:T(8,128)S(1)}, u32[]{:S(2)}, u32[]{:S(2)}) collective-permute-start(f32[8,128]{1,0:T(8,128)S(1)} %add.29), channel_id=1, source_target_pairs={{0,32},{8,40},{16,48},{24,56},{32,0},{40,8},{48,16},{56,24},{64,96... | collective-permute-start | bytes 12296 | tf_op jit(solution)/shard_map/ppermute | solution.py:34
  100.2 2.2 %collective-permute-done.13 = f32[8,128]{1,0:T(8,128)S(1)} collective-permute-done((f32[8,128]{1,0:T(8,128)S(1)}, f32[8,128]{1,0:T(8,128)S(1)}, u32[]{:S(2)}, u32[]{:S(2)}) %collective-permute-start.13) | collective-permute-done | bytes 4128 | tf_op jit(solution)/shard_map/ppermute | solution.py:34
  102.4 11.7 %collective-permute-start.14 = (f32[8,128]{1,0:T(8,128)S(1)}, f32[8,128]{1,0:T(8,128)S(1)}, u32[]{:S(2)}, u32[]{:S(2)}) collective-permute-start(f32[8,128]{1,0:T(8,128)S(1)} %add.30), channel_id=1, source_target_pairs={{0,64},{8,72},{16,80},{24,88},{32,96},{40,104},{48,112},{56,120},{... | collective-permute-start | bytes 12296 | tf_op jit(solution)/shard_map/ppermute | solution.py:34
  114.1 1.3 collective-permute-done.14
  115.4 0.0 collective-permute-done.5
  115.4 0.0 collective-permute-done.6
  115.5 0.0 all-to-all-done.1
  115.5 0.8 gather.1
  116.3 6.3 %collective-permute-start.8 = (f32[3,6,5,256]{3,2,1,0:T(8,128)S(1)}, f32[3,6,5,256]{3,2,1,0:T(8,128)S(1)}, u32[]{:S(2)}, u32[]{:S(2)}) collective-permute-start(f32[3,6,5,256]{3,2,1,0:T(8,128)S(1)} %get-tuple-element.24.own), channel_id=1, source_target_pairs={{0,1},{1,2},{2,3},{3,4},{4,5},{5,6},{6,7},{7,8},{8,9},{9,10},{10,1... | collective-permute-start | bytes 276488 | tf_op jit(solution)/shard_map/ppermute | solution.py:25
  122.6 2.4 %collective-permute-start.9 = (f32[3,6,5,256]{3,2,1,0:T(8,128)S(1)}, f32[3,6,5,256]{3,2,1,0:T(8,128)S(1)}, u32[]{:S(2)}, u32[]{:S(2)}) collective-permute-start(f32[3,6,5,256]{3,2,1,0:T(8,128)S(1)} %get-tuple-element.24.own), channel_id=1, source_target_pairs={{1,0},{2,1},{3,2},{4,3},{5,4},{6,5},{7,6},{8,7},{9,8},{10,9},{11,1... | collective-permute-start | bytes 276488 | tf_op jit(solution)/shard_map/ppermute | solution.py:25
  125.0 0.6 copy.11
  125.7 5.5 %collective-permute-done.9.after = f32[3,6,5,256]{3,2,1,0:T(8,128)S(1)} collective-permute-done((f32[3,6,5,256]{3,2,1,0:T(8,128)S(1)}, f32[3,6,5,256]{3,2,1,0:T(8,128)S(1)}, u32[]{:S(2)}, u32[]{:S(2)}) %collective-permute-start.9) | collective-permute-done | bytes 92192 | tf_op jit(solution)/shard_map/ppermute | solution.py:25
  131.2 1.5 %jump.1 = f32[3,5,6,256]{3,2,1,0:T(8,128)} custom-call(s32[5]{0:T(128)} %copy-done.5, s32[3,6]{1,0:T(4,128)} %side.1, s32[3,6]{1,0:T(4,128)} %patch.1, f32[3,6,5,256]{3,2,1,0:T(8,128)S(1)} %get-tuple-element.24.own, f32[3,6,5,256]{3,2,1,0:T(8,128)S(1)} %collective-permute-done.8.before, f32[3,6,5,256]{3,2,1,0:T(8,128)S(1)} %collective-permute-done.9.after), custom_call_target="tpu_custom_call" | custom-call | tf_op jit(solution)/shard_map/jump/pallas_call | solution.py:376
  (22 shorter events, 0.1 us)
Async XLA Ops:
  0.6 6.4 %collective-permute-start.1 = (f32[12,80,256]{2,1,0:T(8,128)}, f32[12,80,256]{2,1,0:T(8,128)S(1)}, u32[]{:S(2)}, u32[]{:S(2)}) collective-permute-start(f32[12,80,256]{2,1,0:T(8,128)} %bitcast.20), channel_id=1, source_target_pairs={{0,1},{1,0},{2,3},{3,2},{4,5},{5,4},{6,7},{7,6},{8,9},{9,8},{10,11... | collective-permute-start | bytes 2949128 | tf_op jit(solution)/shard_map/ppermute | solution.py:292
  3.9 3.1 %collective-permute-start = (s32[6,32]{1,0:T(8,128)S(1)}, s32[6,32]{1,0:T(8,128)S(1)}, u32[]{:S(2)}, u32[]{:S(2)}) collective-permute-start(s32[6,32]{1,0:T(8,128)S(1)} %pad_add_fusion.meta_own.meta), channel_id=1, source_target_pairs={{0,1},{1,0},{2,3},{3,2},{4,5},{5,4},{6,7},{7,6},{8,9},{9,8},{10,11... | collective-permute-start | bytes 2312 | tf_op jit(solution)/shard_map/ppermute | solution.py:291
  6.0 30.4 %copy-start.5 = (s32[5]{0:T(128)}, s32[5]{0:T(128)S(1)}, u32[]{:S(2)}) copy-start(s32[5]{0:T(128)S(1)} %stack.23.place) | copy-start | bytes 64
  7.0 1.2 copy-start
  8.2 0.7 copy-start.3
  16.9 1.3 copy-start.2
  18.2 0.8 copy-start.6
  18.9 0.8 copy-start.7
  19.7 0.8 copy-start.8
  20.5 15.9 %copy-start.1 = (f32[12,5,16,256]{3,2,1,0:T(8,128)S(1)}, f32[12,5,16,256]{3,2,1,0:T(8,128)}, u32[]{:S(2)}) copy-start(f32[12,5,16,256]{3,2,1,0:T(8,128)} %param.8) | copy-start | bytes 2949124
  20.5 15.9 %copy-start.4 = (s32[1536]{0:T(1024)S(1)}, s32[1536]{0:T(1024)}, u32[]{:S(2)}) copy-start(s32[1536]{0:T(1024)} %ratio.3) | copy-start | bytes 18436
  20.5 28.3 %all-to-all-start = ((f32[48,80,128]{2,1,0:T(8,128)}), f32[48,80,128]{2,1,0:T(8,128)S(1)}, u32[]{:S(2)}, u32[]{:S(2)}) async-start(f32[48,80,128]{2,1,0:T(8,128)} %copy-done.2), calls=%async_computation | async-start | bytes 3932160 | tf_op jit(solution)/shard_map/all_to_all | solution.py:331
  24.7 44.1 %collective-permute-start.2 = (f32[12,80,128]{2,1,0:T(8,128)}, f32[12,80,128]{2,1,0:T(8,128)}, u32[]{:S(2)}, u32[]{:S(2)}) collective-permute-start(f32[12,80,128]{2,1,0:T(8,128)} %copy-done.8), channel_id=1, source_target_pairs={{0,2},{2,4},{4,6},{6,0},{1,3},{3,5},{5,7},{7,1},{8,10},{10,12},{12... | collective-permute-start | bytes 1474568 | tf_op jit(solution)/shard_map/ppermute | solution.py:30
  32.0 36.8 %collective-permute-start.3 = (f32[12,80,128]{2,1,0:T(8,128)}, f32[12,80,128]{2,1,0:T(8,128)}, u32[]{:S(2)}, u32[]{:S(2)}) collective-permute-start(f32[12,80,128]{2,1,0:T(8,128)} %copy-done.7), channel_id=1, source_target_pairs={{0,4},{2,6},{4,0},{6,2},{1,5},{3,7},{5,1},{7,3},{8,12},{10,14},{12... | collective-permute-start | bytes 1474568 | tf_op jit(solution)/shard_map/ppermute | solution.py:30
  33.9 34.9 %collective-permute-start.4 = (f32[12,80,128]{2,1,0:T(8,128)}, f32[12,80,128]{2,1,0:T(8,128)}, u32[]{:S(2)}, u32[]{:S(2)}) collective-permute-start(f32[12,80,128]{2,1,0:T(8,128)} %copy-done.6), channel_id=1, source_target_pairs={{0,6},{2,0},{4,2},{6,4},{1,7},{3,1},{5,3},{7,5},{8,14},{10,8},{12,... | collective-permute-start | bytes 1474568 | tf_op jit(solution)/shard_map/ppermute | solution.py:30
  48.8 14.8 %all-to-all-start.2 = ((f32[16,8,128]{2,1,0:T(8,128)}), f32[16,8,128]{2,1,0:T(8,128)S(1)}, u32[]{:S(2)}, u32[]{:S(2)}) async-start(f32[16,8,128]{2,1,0:T(8,128)} %mass.1), calls=%async_computation.2 | async-start | bytes 131072 | tf_op jit(solution)/shard_map/all_to_all | solution.py:310
  63.6 51.8 %all-to-all-start.1 = ((f32[12,80,128]{2,1,0:T(8,128)}), f32[12,80,128]{2,1,0:T(8,128)S(1)}, u32[]{:S(2)}, u32[]{:S(2)}) async-start(f32[12,80,128]{2,1,0:T(8,128)} %fold.1), calls=%async_computation.1 | async-start | bytes 983040 | tf_op jit(solution)/shard_map/all_to_all | solution.py:348
  70.2 45.2 %collective-permute-start.5 = (f32[3,80,128]{2,1,0:T(8,128)S(1)}, f32[3,80,128]{2,1,0:T(8,128)S(1)}, u32[]{:S(2)}, u32[]{:S(2)}) collective-permute-start(f32[3,80,128]{2,1,0:T(8,128)S(1)} %get-tuple-element.20), channel_id=1, source_target_pairs={{0,128},{128,256},{256,384},{384,0},{1,129},{129,257},{257,385},{3... | collective-permute-start | bytes 368648 | tf_op jit(solution)/shard_map/ppermute | solution.py:30
  72.4 43.0 %collective-permute-start.6 = (f32[3,80,128]{2,1,0:T(8,128)S(1)}, f32[3,80,128]{2,1,0:T(8,128)S(1)}, u32[]{:S(2)}, u32[]{:S(2)}) collective-permute-start(f32[3,80,128]{2,1,0:T(8,128)S(1)} %get-tuple-element.21), channel_id=1, source_target_pairs={{0,256},{128,384},{256,0},{384,128},{1,257},{129,385},{257,1},{385... | collective-permute-start | bytes 368648 | tf_op jit(solution)/shard_map/ppermute | solution.py:30
  76.1 39.4 %collective-permute-start.7 = (f32[3,80,128]{2,1,0:T(8,128)S(1)}, f32[3,80,128]{2,1,0:T(8,128)S(1)}, u32[]{:S(2)}, u32[]{:S(2)}) collective-permute-start(f32[3,80,128]{2,1,0:T(8,128)S(1)} %get-tuple-element.22), channel_id=1, source_target_pairs={{0,384},{128,0},{256,128},{384,256},{1,385},{129,1},{257,129},{385... | collective-permute-start | bytes 368648 | tf_op jit(solution)/shard_map/ppermute | solution.py:30
  79.3 5.2 %collective-permute-start.10 = (f32[8,128]{1,0:T(8,128)S(1)}, f32[8,128]{1,0:T(8,128)S(1)}, u32[]{:S(2)}, u32[]{:S(2)}) collective-permute-start(f32[8,128]{1,0:T(8,128)S(1)} %reduce_sum.9), channel_id=1, source_target_pairs={{0,1},{1,0},{2,3},{3,2},{4,5},{5,4},{6,7},{7,6},{8,9},{9,8},{10,11... | collective-permute-start | bytes 12296 | tf_op jit(solution)/shard_map/ppermute | solution.py:34
  84.5 4.3 %collective-permute-start.11 = (f32[8,128]{1,0:T(8,128)S(1)}, f32[8,128]{1,0:T(8,128)S(1)}, u32[]{:S(2)}, u32[]{:S(2)}) collective-permute-start(f32[8,128]{1,0:T(8,128)S(1)} %add.27), channel_id=1, source_target_pairs={{0,8},{8,0},{16,24},{24,16},{32,40},{40,32},{48,56},{56,48},{64,72... | collective-permute-start | bytes 12296 | tf_op jit(solution)/shard_map/ppermute | solution.py:34
  88.9 5.2 %collective-permute-start.12 = (f32[8,128]{1,0:T(8,128)S(1)}, f32[8,128]{1,0:T(8,128)S(1)}, u32[]{:S(2)}, u32[]{:S(2)}) collective-permute-start(f32[8,128]{1,0:T(8,128)S(1)} %add.28), channel_id=1, source_target_pairs={{0,16},{8,24},{16,0},{24,8},{32,48},{40,56},{48,32},{56,40},{64,80... | collective-permute-start | bytes 12296 | tf_op jit(solution)/shard_map/ppermute | solution.py:34
  94.1 8.2 %collective-permute-start.13 = (f32[8,128]{1,0:T(8,128)S(1)}, f32[8,128]{1,0:T(8,128)S(1)}, u32[]{:S(2)}, u32[]{:S(2)}) collective-permute-start(f32[8,128]{1,0:T(8,128)S(1)} %add.29), channel_id=1, source_target_pairs={{0,32},{8,40},{16,48},{24,56},{32,0},{40,8},{48,16},{56,24},{64,96... | collective-permute-start | bytes 12296 | tf_op jit(solution)/shard_map/ppermute | solution.py:34
  102.4 13.1 %collective-permute-start.14 = (f32[8,128]{1,0:T(8,128)S(1)}, f32[8,128]{1,0:T(8,128)S(1)}, u32[]{:S(2)}, u32[]{:S(2)}) collective-permute-start(f32[8,128]{1,0:T(8,128)S(1)} %add.30), channel_id=1, source_target_pairs={{0,64},{8,72},{16,80},{24,88},{32,96},{40,104},{48,112},{56,120},{... | collective-permute-start | bytes 12296 | tf_op jit(solution)/shard_map/ppermute | solution.py:34
  116.3 9.4 %collective-permute-start.8 = (f32[3,6,5,256]{3,2,1,0:T(8,128)S(1)}, f32[3,6,5,256]{3,2,1,0:T(8,128)S(1)}, u32[]{:S(2)}, u32[]{:S(2)}) collective-permute-start(f32[3,6,5,256]{3,2,1,0:T(8,128)S(1)} %get-tuple-element.24.own), channel_id=1, source_target_pairs={{0,1},{1,2},{2,3},{3,4},{4,5},{5,6},{6,7},{7,8},{8,9},{9,10},{10,1... | collective-permute-start | bytes 276488 | tf_op jit(solution)/shard_map/ppermute | solution.py:25
  122.6 8.6 %collective-permute-start.9 = (f32[3,6,5,256]{3,2,1,0:T(8,128)S(1)}, f32[3,6,5,256]{3,2,1,0:T(8,128)S(1)}, u32[]{:S(2)}, u32[]{:S(2)}) collective-permute-start(f32[3,6,5,256]{3,2,1,0:T(8,128)S(1)} %get-tuple-element.24.own), channel_id=1, source_target_pairs={{1,0},{2,1},{3,2},{4,3},{5,4},{6,5},{7,6},{8,7},{9,8},{10,9},{11,1... | collective-permute-start | bytes 276488 | tf_op jit(solution)/shard_map/ppermute | solution.py:25

commit v3 on v2

--- a/solution.py
+++ b/solution.py
@@ -25,17 +25,25 @@
     return lax.ppermute(block, axis, route)
 
 
-def rotated(block, axis, distance):
-    size = lax.axis_size(axis)
-    return lax.ppermute(block, axis, [(i, (i + distance) % size) for i in range(size)])
-
-
 def crossed(block, axis, distance):
     return block + lax.ppermute(block, axis, [(i, i ^ distance) for i in range(lax.axis_size(axis))])
 
 
 def fast(block):
     return pltpu.with_memory_space_constraint(block, VMEM)
+
+
+def mixed_groups(size_x, size_y, chips_y, cores):
+    def device(x, z, y, c):
+        return ((x * size_y + z) * chips_y + y) * cores + c
+
+    along_x, along_y = [], []
+    for c in range(cores):
+        lines_x = [[device(x, z, y, c) for x in range(size_x)] for z in range(size_y) for y in range(chips_y)]
+        lines_y = [[device(x, z, y, c) for y in range(chips_y)] for z in range(size_y) for x in range(size_x)]
+        along_x += lines_x if c == 0 else lines_y
+        along_y += lines_y if c == 0 else lines_x
+    return along_x, along_y
 
 
 def halves(block):
@@ -97,17 +105,13 @@
 
 def partials_kernel(
     place, meta_own, meta_peer, ratio, own, peer,
-    out_a, out_b0, out_b1, out_b2, out_b3,
-    out_b, table, split, code_k, code_x,
+    out, table, split, code_k, code_x,
     *, patches, fields, edge, size_x, size_y, chips_y, cores, new_count, pairs,
 ):
     rows = fields * edge
     lanes = edge * edge
-    half = lanes // 2
     index_y = place[0]
     core = place[1]
-    index_x = place[3]
-    chip_y = place[4]
     size_z = chips_y * cores
 
     def prepare(o, carry):
@@ -121,8 +125,7 @@
 
     lax.fori_loop(0, patches, prepare, 0)
 
-    out_a[...] = jnp.zeros_like(out_a)
-    out_b[...] = jnp.zeros_like(out_b)
+    out[...] = jnp.zeros_like(out)
     cell = iota((lanes, lanes), 0)
     code_k[...] = (cell // edge) * 4096 + cell % edge
     row = iota((rows, 2 * rows), 0)
@@ -143,10 +146,9 @@
             table[1, found] = ratio[owner * new_count + slot]
             table[2, found] = meta[2, p]
             table[3, found] = meta[3, p] * 4096 + meta[4, p]
-            table[4, found] = (ix * chips_y + iz // cores) * new_count + slot
-            step_y = (iz // cores - chip_y) & (chips_y - 1)
-            step_x = (ix - index_x) & (size_x - 1)
-            table[5, found] = (step_y * size_x + step_x) * new_count + slot
+            chip_y = iz // cores
+            chip = jnp.where(core == 0, ix * chips_y + chip_y, chip_y * size_x + ix)
+            table[4, found] = chip * new_count + slot
 
         return found + mine.astype(I32)
 
@@ -159,7 +161,6 @@
         table[2, found + extra] = 0
         table[3, found + extra] = 0
         table[4, found + extra] = 0
-        table[5, found + extra] = 0
 
     lane_k = iota((1, lanes), 1)
     lane_code = (lane_k // edge) * 4096 + lane_k % edge
@@ -183,17 +184,12 @@
             part = (product[:rows] + product[rows:]) * live
             results.append((p, part))
         for p, part in results:
-            to_a = table[4, p]
-            to_b = table[5, p]
-            out_a[to_a] = out_a[to_a] + part[:, :half]
-            out_b[to_b] = out_b[to_b] + part[:, half:]
+            to = table[4, p]
+            out[to] = out[to] + part
         return carry
 
     steps = (found + UNROLL - 1) // UNROLL
     lax.fori_loop(0, steps, remap, 0)
-    chunk = size_x * new_count
-    for k, out in enumerate((out_b0, out_b1, out_b2, out_b3)):
-        out[...] = out_b[k * chunk:(k + 1) * chunk]
 
 
 def fold_kernel(a, out):
@@ -203,22 +199,12 @@
     out[...] = total
 
 
-def cross_kernel(b0, b1, b2, b3, *outs):
-    count = outs[0].shape[0]
-    for k, out in enumerate(outs):
-        at = slice(k * count, (k + 1) * count)
-        out[...] = (b0[at] + b1[at]) + (b2[at] + b3[at])
-
-
-def gather_kernel(a, b0, b1, b2, b3, new_data, faces, *, count, fields, edge):
+def gather_kernel(a, new_data, faces, *, count, fields, edge):
     rows = fields * edge
     lanes = edge * edge
-    sources = a.shape[0]
-    total_a = a[0]
-    total_b = (b0[...] + b1[...]) + (b2[...] + b3[...])
-    for s in range(1, sources):
-        total_a = total_a + a[s]
-    whole = jnp.concatenate([total_a, total_b], axis=1)
+    whole = a[0]
+    for s in range(1, a.shape[0]):
+        whole = whole + a[s]
     new_data[...] = whole
     high, low = halves(whole)
     stacked = jnp.concatenate([high, low], axis=0)
@@ -291,7 +277,6 @@
     peer_meta = lax.ppermute(meta, "gz_1", swap)
     peer = lax.ppermute(own, "gz_1", swap)
     owners = size_x * chips_y * count
-    chunk = owners // chips_y
     smem = pl.BlockSpec(memory_space=SMEM)
     vmem = pl.BlockSpec(memory_space=VMEM)
     params = pltpu.CompilerParams(vmem_limit_bytes=24 * 1024 * 1024)
@@ -308,18 +293,16 @@
         name="mass",
     )(place, meta, new_ratio, own)
     plane = lax.all_to_all(mass, PLANE, 0, 0, tiled=True)
-    out_a, *out_b = pl.pallas_call(
+    partials = pl.pallas_call(
         functools.partial(
             partials_kernel, patches=patches, fields=fields, edge=edge, size_x=size_x,
             size_y=size_y, chips_y=chips_y, cores=cores, new_count=count, pairs=pairs,
         ),
-        out_shape=(VMEM((owners, rows, half), F32),)
-        + (VMEM((chunk, rows, half), F32),) * chips_y,
+        out_shape=jax.ShapeDtypeStruct((owners, rows, lanes), F32),
         in_specs=[smem, smem, smem, smem, vmem, vmem],
-        out_specs=(vmem,) * (1 + chips_y),
+        out_specs=vmem,
         scratch_shapes=[
-            pltpu.VMEM((owners, rows, half), F32),
-            pltpu.SMEM((6, 2 * pairs + UNROLL), I32),
+            pltpu.SMEM((5, 2 * pairs + UNROLL), I32),
             pltpu.VMEM((2 * patches, 2 * rows, lanes), BF16),
             pltpu.VMEM((lanes, lanes), I32),
             pltpu.VMEM((rows, 2 * rows), I32),
@@ -328,49 +311,34 @@
         name="partials",
     )(place, meta, peer_meta, new_ratio, own, fast(peer))
 
-    first_a = lax.all_to_all(out_a, "gx", 0, 0, tiled=True)
-    for k in (1, 3, 2):
-        out_b[k] = rotated(out_b[k], "gz_0", k)
+    first_groups, last_groups = mixed_groups(size_x, size_y, chips_y, cores)
+    first = lax.all_to_all(partials, ALL_AXES, 0, 0, tiled=True, axis_index_groups=first_groups)
     total = jnp.sum(plane, axis=0)
     total = crossed(total, "gz_1", 1)
     distance = 1
     while distance < size_y:
         total = crossed(total, "gy", distance)
         distance = distance * 2
-    mid_a = pl.pallas_call(
+    folded = pl.pallas_call(
         fold_kernel,
-        out_shape=VMEM((chips_y * count, rows, half), F32),
+        out_shape=VMEM((owners // size_x, rows, lanes), F32),
         in_specs=[vmem],
         out_specs=vmem,
         compiler_params=params,
         name="fold",
-    )(fast(first_a.reshape(size_x, chips_y * count, rows, half)))
-    last_a = lax.all_to_all(mid_a, "gz_0", 0, 0, tiled=True)
-    mid_b = list(pl.pallas_call(
-        cross_kernel,
-        out_shape=(VMEM((count, rows, half), F32),) * size_x,
-        in_specs=[vmem] * chips_y,
-        out_specs=(vmem,) * size_x,
-        compiler_params=params,
-        name="cross",
-    )(*[fast(b) for b in out_b]))
-    for k in (1, 3, 2):
-        mid_b[k] = rotated(mid_b[k], "gx", k)
-
+    )(fast(first.reshape(size_x, owners // size_x, rows, lanes)))
+    last = lax.all_to_all(folded, ALL_AXES, 0, 0, tiled=True, axis_index_groups=last_groups)
     new_data, faces = pl.pallas_call(
         functools.partial(gather_kernel, count=count, fields=fields, edge=edge),
         out_shape=(
             jax.ShapeDtypeStruct((count * rows, lanes), F32),
             VMEM((count, 6, fields, lanes), F32),
         ),
-        in_specs=[vmem] * (1 + size_x),
+        in_specs=[vmem],
         out_specs=(vmem, vmem),
         compiler_params=params,
         name="gather",
-    )(
-        fast(last_a.reshape(chips_y, count * rows, half)),
-        *[fast(b.reshape(count * rows, half)) for b in mid_b],
-    )
+    )(fast(last.reshape(chips_y, count * rows, lanes)))
     before = shifted(faces, ALL_AXES, 1)
     after = shifted(faces, ALL_AXES, -1)
     interface_jump = pl.pallas_call(

time: 135 us -> 128 us (0.948)
  the two profiles are of different devices: /device:TPU:25 before, /device:TPU:2 now
where the time goes in v3:
time: 128 us
  starting transfers between devices  57.6 us (45%)
  waiting for transfers between devices  47.9 us (37%)
  Pallas kernels  16.2 us (13%)
  local copies, waits for them, and re-layouts  4.49 us (4%)
    ppermute x5, starting transfers between devices, crossed(): lax.ppermute(block, axis, [(i, i ^ distance) for i in range(lax.axis_size...  25 us
    all_to_all x1, waiting for transfers between devices, body(): lax.all_to_all(partials, ALL_AXES, 0, 0, tiled=True, axis_index_groups=fi...  22.5 us
    ppermute x5, waiting for transfers between devices, crossed(): lax.ppermute(block, axis, [(i, i ^ distance) for i in range(lax.axis_size...  13.5 us
    all_to_all x1, starting transfers between devices, body(): lax.all_to_all(partials, ALL_AXES, 0, 0, tiled=True, axis_index_groups=fi...  10.3 us
    ppermute x2, starting transfers between devices, shifted(): return lax.ppermute(block, axis, route)  9.74 us
    pallas_call x1, Pallas kernels, body(): pl.pallas_call(functools.partial(partials_kernel, patches=patches, fields...  8.23 us
    ppermute x2, waiting for transfers between devices, shifted(): return lax.ppermute(block, axis, route)  8.09 us
    all_to_all x1, starting transfers between devices, body(): plane = lax.all_to_all(mass, PLANE, 0, 0, tiled=True)  4.77 us
  transfers between devices with their start and end apart: 12, of which 10 were waited for; matrix products, arithmetic and copies ran while one was open for 1% of the time, Pallas kernels for 4%

profile of v3, /device:TPU:2, one launch (start us, length us, event | category | flops | bytes accessed | tf_op | source)
XLA Modules:
  0.0 127.7 jit_solution(14181978509867760270)
XLA Ops:
  0.6 1.9 %collective-permute-start.1 = (f32[12,80,256]{2,1,0:T(8,128)}, f32[12,80,256]{2,1,0:T(8,128)S(1)}, u32[]{:S(2)}, u32[]{:S(2)}) collective-permute-start(f32[12,80,256]{2,1,0:T(8,128)} %bitcast.15), channel_id=1, source_target_pairs={{0,1},{1,0},{2,3},{3,2},{4,5},{5,4},{6,7},{7,6},{8,9},{9,8},{10,11... | collective-permute-start | bytes 2949128 | tf_op jit(solution)/shard_map/ppermute | solution.py:278
  2.6 0.7 pad_add_fusion.meta_own.meta
  3.3 2.4 %collective-permute-start = (s32[6,32]{1,0:T(8,128)S(1)}, s32[6,32]{1,0:T(8,128)S(1)}, u32[]{:S(2)}, u32[]{:S(2)}) collective-permute-start(s32[6,32]{1,0:T(8,128)S(1)} %pad_add_fusion.meta_own.meta), channel_id=1, source_target_pairs={{0,1},{1,0},{2,3},{3,2},{4,5},{5,4},{6,7},{7,6},{8,9},{9,8},{10,11... | collective-permute-start | bytes 2312 | tf_op jit(solution)/shard_map/ppermute | solution.py:277
  5.7 0.1 stack.23.place
  5.8 0.0 copy-start.5
  5.8 0.7 collective-permute-done.meta_peer
  6.5 0.0 collective-permute-done.1.peer
  6.5 0.0 copy-start.1
  6.5 1.2 copy-done.1
  7.7 0.0 copy-start.3
  7.7 0.7 copy-done.3
  8.4 8.2 %partials.1 = f32[48,80,256]{2,1,0:T(8,128)S(1)} custom-call(s32[5]{0:T(128)S(1)} %stack.23.place, s32[6,32]{1,0:T(8,128)S(1)} %pad_add_fusion.meta_own.meta, s32[6,32]{1,0:T(8,128)S(1)} %collective-permute-done.meta_peer, s32[1536]{0:T(1024)S(1)} %copy-done.3, f32[12,80,256]{2,1,0:T(8,128)S(1)} %bitcast.16, f32[12,80,256]{2,1,0:T(8,128)S(1)} %collective-permute-done.1.peer), custom_call_target="tpu_custom_call" | custom-call | tf_op jit(solution)/shard_map/partials/pallas_call | solution.py:296
  16.6 0.0 copy-start
  16.6 1.9 %copy-done = f32[48,80,256]{2,1,0:T(8,128)} copy-done((f32[48,80,256]{2,1,0:T(8,128)}, f32[48,80,256]{2,1,0:T(8,128)S(1)}, u32[]{:S(2)}) %copy-start) | copy-done | bytes 3932184
  18.5 0.0 copy-start.2
  18.5 0.0 copy-start.4
  18.5 10.3 %all-to-all-start = ((f32[48,80,256]{2,1,0:T(8,128)}), f32[48,80,256]{2,1,0:T(8,128)}, u32[]{:S(2)}, u32[]{:S(2)}) async-start(f32[48,80,256]{2,1,0:T(8,128)} %copy-done), calls=%async_computation | async-start | bytes 7864320 | tf_op jit(solution)/shard_map/all_to_all | solution.py:315
  28.7 0.0 copy-done.5
  28.7 0.0 copy-done.2
  28.7 0.0 copy-done.4
  28.8 2.4 %mass.1 = f32[16,8,128]{2,1,0:T(8,128)} custom-call(s32[5]{0:T(128)S(1)} %stack.23.place, s32[6,32]{1,0:T(8,128)S(1)} %pad_add_fusion.meta_own.meta, s32[1536]{0:T(1024)S(1)} %copy-done.4, f32[12,80,256]{2,1,0:T(8,128)S(1)} %bitcast.17), custom_call_target="tpu_custom_call" | custom-call | tf_op jit(solution)/shard_map/mass/pallas_call | solution.py:283
  31.2 22.5 %all-to-all-done = f32[48,80,256]{2,1,0:T(8,128)} async-done(((f32[48,80,256]{2,1,0:T(8,128)}), f32[48,80,256]{2,1,0:T(8,128)}, u32[]{:S(2)}, u32[]{:S(2)}) %all-to-all-start) | async-done | bytes 3932192 | tf_op jit(solution)/shard_map/all_to_all | solution.py:315
  53.7 4.8 %all-to-all-start.2 = ((f32[16,8,128]{2,1,0:T(8,128)}), f32[16,8,128]{2,1,0:T(8,128)S(1)}, u32[]{:S(2)}, u32[]{:S(2)}) async-start(f32[16,8,128]{2,1,0:T(8,128)} %mass.1), calls=%async_computation.2 | async-start | bytes 131072 | tf_op jit(solution)/shard_map/all_to_all | solution.py:295
  58.5 3.2 %fold.1 = f32[12,80,256]{2,1,0:T(8,128)} custom-call(f32[4,12,80,256]{3,2,1,0:T(8,128)} %bitcast.10.a), custom_call_target="tpu_custom_call" | custom-call | tf_op jit(solution)/shard_map/fold/pallas_call | solution.py:322
  61.7 3.1 %all-to-all-done.2 = f32[16,8,128]{2,1,0:T(8,128)S(1)} async-done(((f32[16,8,128]{2,1,0:T(8,128)}), f32[16,8,128]{2,1,0:T(8,128)S(1)}, u32[]{:S(2)}, u32[]{:S(2)}) %all-to-all-start.2) | async-done | bytes 65568 | tf_op jit(solution)/shard_map/all_to_all | solution.py:295
  64.8 3.5 %all-to-all-start.1 = ((f32[12,80,256]{2,1,0:T(8,128)}), f32[12,80,256]{2,1,0:T(8,128)S(1)}, u32[]{:S(2)}, u32[]{:S(2)}) async-start(f32[12,80,256]{2,1,0:T(8,128)} %fold.1), calls=%async_computation.1 | async-start | bytes 1966080 | tf_op jit(solution)/shard_map/all_to_all | solution.py:330
  68.4 1.9 %collective-permute-start.4 = (f32[8,128]{1,0:T(8,128)S(1)}, f32[8,128]{1,0:T(8,128)S(1)}, u32[]{:S(2)}, u32[]{:S(2)}) collective-permute-start(f32[8,128]{1,0:T(8,128)S(1)} %reduce_sum.9), channel_id=1, source_target_pairs={{0,1},{1,0},{2,3},{3,2},{4,5},{5,4},{6,7},{7,6},{8,9},{9,8},{10,11... | collective-permute-start | bytes 12296 | tf_op jit(solution)/shard_map/ppermute | solution.py:29
  70.3 1.1 collective-permute-done.4
  71.4 1.9 %collective-permute-start.5 = (f32[8,128]{1,0:T(8,128)S(1)}, f32[8,128]{1,0:T(8,128)S(1)}, u32[]{:S(2)}, u32[]{:S(2)}) collective-permute-start(f32[8,128]{1,0:T(8,128)S(1)} %add.27), channel_id=1, source_target_pairs={{0,8},{8,0},{16,24},{24,16},{32,40},{40,32},{48,56},{56,48},{64,72... | collective-permute-start | bytes 12296 | tf_op jit(solution)/shard_map/ppermute | solution.py:29
  73.4 3.6 %collective-permute-done.5 = f32[8,128]{1,0:T(8,128)S(1)} collective-permute-done((f32[8,128]{1,0:T(8,128)S(1)}, f32[8,128]{1,0:T(8,128)S(1)}, u32[]{:S(2)}, u32[]{:S(2)}) %collective-permute-start.5) | collective-permute-done | bytes 4128 | tf_op jit(solution)/shard_map/ppermute | solution.py:29
  76.9 2.0 %collective-permute-start.6 = (f32[8,128]{1,0:T(8,128)S(1)}, f32[8,128]{1,0:T(8,128)S(1)}, u32[]{:S(2)}, u32[]{:S(2)}) collective-permute-start(f32[8,128]{1,0:T(8,128)S(1)} %add.28), channel_id=1, source_target_pairs={{0,16},{8,24},{16,0},{24,8},{32,48},{40,56},{48,32},{56,40},{64,80... | collective-permute-start | bytes 12296 | tf_op jit(solution)/shard_map/ppermute | solution.py:29
  79.0 4.3 %collective-permute-done.6 = f32[8,128]{1,0:T(8,128)S(1)} collective-permute-done((f32[8,128]{1,0:T(8,128)S(1)}, f32[8,128]{1,0:T(8,128)S(1)}, u32[]{:S(2)}, u32[]{:S(2)}) %collective-permute-start.6) | collective-permute-done | bytes 4128 | tf_op jit(solution)/shard_map/ppermute | solution.py:29
  83.3 6.6 %collective-permute-start.7 = (f32[8,128]{1,0:T(8,128)S(1)}, f32[8,128]{1,0:T(8,128)S(1)}, u32[]{:S(2)}, u32[]{:S(2)}) collective-permute-start(f32[8,128]{1,0:T(8,128)S(1)} %add.29), channel_id=1, source_target_pairs={{0,32},{8,40},{16,48},{24,56},{32,0},{40,8},{48,16},{56,24},{64,96... | collective-permute-start | bytes 12296 | tf_op jit(solution)/shard_map/ppermute | solution.py:29
  89.9 2.8 %collective-permute-done.7 = f32[8,128]{1,0:T(8,128)S(1)} collective-permute-done((f32[8,128]{1,0:T(8,128)S(1)}, f32[8,128]{1,0:T(8,128)S(1)}, u32[]{:S(2)}, u32[]{:S(2)}) %collective-permute-start.7) | collective-permute-done | bytes 4128 | tf_op jit(solution)/shard_map/ppermute | solution.py:29
  92.7 12.6 %collective-permute-start.8 = (f32[8,128]{1,0:T(8,128)S(1)}, f32[8,128]{1,0:T(8,128)S(1)}, u32[]{:S(2)}, u32[]{:S(2)}) collective-permute-start(f32[8,128]{1,0:T(8,128)S(1)} %add.30), channel_id=1, source_target_pairs={{0,64},{8,72},{16,80},{24,88},{32,96},{40,104},{48,112},{56,120},{... | collective-permute-start | bytes 12296 | tf_op jit(solution)/shard_map/ppermute | solution.py:29
  105.3 1.6 %collective-permute-done.8 = f32[8,128]{1,0:T(8,128)S(1)} collective-permute-done((f32[8,128]{1,0:T(8,128)S(1)}, f32[8,128]{1,0:T(8,128)S(1)}, u32[]{:S(2)}, u32[]{:S(2)}) %collective-permute-start.8) | collective-permute-done | bytes 4128 | tf_op jit(solution)/shard_map/ppermute | solution.py:29
  106.9 0.0 all-to-all-done.1
  106.9 0.8 gather.1
  107.7 7.8 %collective-permute-start.3 = (f32[3,6,5,256]{3,2,1,0:T(8,128)S(1)}, f32[3,6,5,256]{3,2,1,0:T(8,128)S(1)}, u32[]{:S(2)}, u32[]{:S(2)}) collective-permute-start(f32[3,6,5,256]{3,2,1,0:T(8,128)S(1)} %get-tuple-element.6.own), channel_id=1, source_target_pairs={{1,0},{2,1},{3,2},{4,3},{5,4},{6,5},{7,6},{8,7},{9,8},{10,9},{11,1... | collective-permute-start | bytes 276488 | tf_op jit(solution)/shard_map/ppermute | solution.py:25
  115.5 1.9 %collective-permute-start.2 = (f32[3,6,5,256]{3,2,1,0:T(8,128)S(1)}, f32[3,6,5,256]{3,2,1,0:T(8,128)S(1)}, u32[]{:S(2)}, u32[]{:S(2)}) collective-permute-start(f32[3,6,5,256]{3,2,1,0:T(8,128)S(1)} %get-tuple-element.6.own), channel_id=1, source_target_pairs={{0,1},{1,2},{2,3},{3,4},{4,5},{5,6},{6,7},{7,8},{8,9},{9,10},{10,1... | collective-permute-start | bytes 276488 | tf_op jit(solution)/shard_map/ppermute | solution.py:25
  117.5 0.6 copy.11
  118.1 0.1 collective-permute-done.3.after
  118.2 8.0 %collective-permute-done.2.before = f32[3,6,5,256]{3,2,1,0:T(8,128)S(1)} collective-permute-done((f32[3,6,5,256]{3,2,1,0:T(8,128)S(1)}, f32[3,6,5,256]{3,2,1,0:T(8,128)S(1)}, u32[]{:S(2)}, u32[]{:S(2)}) %collective-permute-start.2) | collective-permute-done | bytes 92192 | tf_op jit(solution)/shard_map/ppermute | solution.py:25
  126.2 1.5 %jump.1 = f32[3,5,6,256]{3,2,1,0:T(8,128)} custom-call(s32[5]{0:T(128)} %copy-done.5, s32[3,6]{1,0:T(4,128)} %side.1, s32[3,6]{1,0:T(4,128)} %patch.1, f32[3,6,5,256]{3,2,1,0:T(8,128)S(1)} %get-tuple-element.6.own, f32[3,6,5,256]{3,2,1,0:T(8,128)S(1)} %collective-permute-done.2.before, f32[3,6,5,256]{3,2,1,0:T(8,128)S(1)} %collective-permute-done.3.after), custom_call_target="tpu_custom_call" | custom-call | tf_op jit(solution)/shard_map/jump/pallas_call | solution.py:344
  (7 shorter events, 0.0 us)
Async XLA Ops:
  0.6 5.9 %collective-permute-start.1 = (f32[12,80,256]{2,1,0:T(8,128)}, f32[12,80,256]{2,1,0:T(8,128)S(1)}, u32[]{:S(2)}, u32[]{:S(2)}) collective-permute-start(f32[12,80,256]{2,1,0:T(8,128)} %bitcast.15), channel_id=1, source_target_pairs={{0,1},{1,0},{2,3},{3,2},{4,5},{5,4},{6,7},{7,6},{8,9},{9,8},{10,11... | collective-permute-start | bytes 2949128 | tf_op jit(solution)/shard_map/ppermute | solution.py:278
  3.3 3.2 %collective-permute-start = (s32[6,32]{1,0:T(8,128)S(1)}, s32[6,32]{1,0:T(8,128)S(1)}, u32[]{:S(2)}, u32[]{:S(2)}) collective-permute-start(s32[6,32]{1,0:T(8,128)S(1)} %pad_add_fusion.meta_own.meta), channel_id=1, source_target_pairs={{0,1},{1,0},{2,3},{3,2},{4,5},{5,4},{6,7},{7,6},{8,9},{9,8},{10,11... | collective-permute-start | bytes 2312 | tf_op jit(solution)/shard_map/ppermute | solution.py:277
  5.8 23.0 %copy-start.5 = (s32[5]{0:T(128)}, s32[5]{0:T(128)S(1)}, u32[]{:S(2)}) copy-start(s32[5]{0:T(128)S(1)} %stack.23.place) | copy-start | bytes 64
  6.5 1.2 copy-start.1
  7.7 0.7 copy-start.3
  16.6 1.9 %copy-start = (f32[48,80,256]{2,1,0:T(8,128)}, f32[48,80,256]{2,1,0:T(8,128)S(1)}, u32[]{:S(2)}) copy-start(f32[48,80,256]{2,1,0:T(8,128)S(1)} %partials.1) | copy-start | bytes 11796484
  18.5 10.3 %copy-start.2 = (f32[12,5,16,256]{3,2,1,0:T(8,128)S(1)}, f32[12,5,16,256]{3,2,1,0:T(8,128)}, u32[]{:S(2)}) copy-start(f32[12,5,16,256]{3,2,1,0:T(8,128)} %param.8) | copy-start | bytes 2949124
  18.5 10.3 %copy-start.4 = (s32[1536]{0:T(1024)S(1)}, s32[1536]{0:T(1024)}, u32[]{:S(2)}) copy-start(s32[1536]{0:T(1024)} %ratio.3) | copy-start | bytes 18436
  18.5 35.2 %all-to-all-start = ((f32[48,80,256]{2,1,0:T(8,128)}), f32[48,80,256]{2,1,0:T(8,128)}, u32[]{:S(2)}, u32[]{:S(2)}) async-start(f32[48,80,256]{2,1,0:T(8,128)} %copy-done), calls=%async_computation | async-start | bytes 7864320 | tf_op jit(solution)/shard_map/all_to_all | solution.py:315
  53.7 11.1 %all-to-all-start.2 = ((f32[16,8,128]{2,1,0:T(8,128)}), f32[16,8,128]{2,1,0:T(8,128)S(1)}, u32[]{:S(2)}, u32[]{:S(2)}) async-start(f32[16,8,128]{2,1,0:T(8,128)} %mass.1), calls=%async_computation.2 | async-start | bytes 131072 | tf_op jit(solution)/shard_map/all_to_all | solution.py:295
  64.8 42.1 %all-to-all-start.1 = ((f32[12,80,256]{2,1,0:T(8,128)}), f32[12,80,256]{2,1,0:T(8,128)S(1)}, u32[]{:S(2)}, u32[]{:S(2)}) async-start(f32[12,80,256]{2,1,0:T(8,128)} %fold.1), calls=%async_computation.1 | async-start | bytes 1966080 | tf_op jit(solution)/shard_map/all_to_all | solution.py:330
  68.4 3.1 %collective-permute-start.4 = (f32[8,128]{1,0:T(8,128)S(1)}, f32[8,128]{1,0:T(8,128)S(1)}, u32[]{:S(2)}, u32[]{:S(2)}) collective-permute-start(f32[8,128]{1,0:T(8,128)S(1)} %reduce_sum.9), channel_id=1, source_target_pairs={{0,1},{1,0},{2,3},{3,2},{4,5},{5,4},{6,7},{7,6},{8,9},{9,8},{10,11... | collective-permute-start | bytes 12296 | tf_op jit(solution)/shard_map/ppermute | solution.py:29
  71.4 5.5 %collective-permute-start.5 = (f32[8,128]{1,0:T(8,128)S(1)}, f32[8,128]{1,0:T(8,128)S(1)}, u32[]{:S(2)}, u32[]{:S(2)}) collective-permute-start(f32[8,128]{1,0:T(8,128)S(1)} %add.27), channel_id=1, source_target_pairs={{0,8},{8,0},{16,24},{24,16},{32,40},{40,32},{48,56},{56,48},{64,72... | collective-permute-start | bytes 12296 | tf_op jit(solution)/shard_map/ppermute | solution.py:29
  76.9 6.4 %collective-permute-start.6 = (f32[8,128]{1,0:T(8,128)S(1)}, f32[8,128]{1,0:T(8,128)S(1)}, u32[]{:S(2)}, u32[]{:S(2)}) collective-permute-start(f32[8,128]{1,0:T(8,128)S(1)} %add.28), channel_id=1, source_target_pairs={{0,16},{8,24},{16,0},{24,8},{32,48},{40,56},{48,32},{56,40},{64,80... | collective-permute-start | bytes 12296 | tf_op jit(solution)/shard_map/ppermute | solution.py:29
  83.3 9.4 %collective-permute-start.7 = (f32[8,128]{1,0:T(8,128)S(1)}, f32[8,128]{1,0:T(8,128)S(1)}, u32[]{:S(2)}, u32[]{:S(2)}) collective-permute-start(f32[8,128]{1,0:T(8,128)S(1)} %add.29), channel_id=1, source_target_pairs={{0,32},{8,40},{16,48},{24,56},{32,0},{40,8},{48,16},{56,24},{64,96... | collective-permute-start | bytes 12296 | tf_op jit(solution)/shard_map/ppermute | solution.py:29
  92.7 14.2 %collective-permute-start.8 = (f32[8,128]{1,0:T(8,128)S(1)}, f32[8,128]{1,0:T(8,128)S(1)}, u32[]{:S(2)}, u32[]{:S(2)}) collective-permute-start(f32[8,128]{1,0:T(8,128)S(1)} %add.30), channel_id=1, source_target_pairs={{0,64},{8,72},{16,80},{24,88},{32,96},{40,104},{48,112},{56,120},{... | collective-permute-start | bytes 12296 | tf_op jit(solution)/shard_map/ppermute | solution.py:29
  107.7 10.5 %collective-permute-start.3 = (f32[3,6,5,256]{3,2,1,0:T(8,128)S(1)}, f32[3,6,5,256]{3,2,1,0:T(8,128)S(1)}, u32[]{:S(2)}, u32[]{:S(2)}) collective-permute-start(f32[3,6,5,256]{3,2,1,0:T(8,128)S(1)} %get-tuple-element.6.own), channel_id=1, source_target_pairs={{1,0},{2,1},{3,2},{4,3},{5,4},{6,5},{7,6},{8,7},{9,8},{10,9},{11,1... | collective-permute-start | bytes 276488 | tf_op jit(solution)/shard_map/ppermute | solution.py:25
  115.5 10.7 %collective-permute-start.2 = (f32[3,6,5,256]{3,2,1,0:T(8,128)S(1)}, f32[3,6,5,256]{3,2,1,0:T(8,128)S(1)}, u32[]{:S(2)}, u32[]{:S(2)}) collective-permute-start(f32[3,6,5,256]{3,2,1,0:T(8,128)S(1)} %get-tuple-element.6.own), channel_id=1, source_target_pairs={{0,1},{1,2},{2,3},{3,4},{4,5},{5,6},{6,7},{7,8},{8,9},{9,10},{10,1... | collective-permute-start | bytes 276488 | tf_op jit(solution)/shard_map/ppermute | solution.py:25

commit v4 on v3

--- a/solution.py
+++ b/solution.py
@@ -10,23 +10,20 @@
 
 
 ALL_AXES = ("gx", "gy", "gz_0", "gz_1")
-PLANE = ("gx", "gz_0")
 UNROLL = 4
 BF16 = jnp.bfloat16
 F32 = jnp.float32
 I32 = jnp.int32
 VMEM = pltpu.VMEM
 SMEM = pltpu.SMEM
+HBM = pltpu.HBM
+DMA = pltpu.SemaphoreType.DMA
 
 
 def shifted(block, axis, distance):
     devices = range(lax.axis_size(axis))
     route = [(i - distance, i) for i in devices if i - distance in devices]
     return lax.ppermute(block, axis, route)
-
-
-def crossed(block, axis, distance):
-    return block + lax.ppermute(block, axis, [(i, i ^ distance) for i in range(lax.axis_size(axis))])
 
 
 def fast(block):
@@ -46,6 +43,34 @@
     return along_x, along_y
 
 
+def mixed_steps(size_x, size_y, chips_y, cores):
+    shape = (size_x, size_y, chips_y, cores)
+    spots = [
+        (x, z, y, c) for x in range(size_x) for z in range(size_y) for y in range(chips_y) for c in range(cores)
+    ]
+
+    def number(spot):
+        at = 0
+        for size, i in zip(shape, spot):
+            at = at * size + i
+        return at
+
+    def step(across, distance):
+        def other(spot):
+            axis = (2 if spot[3] == 0 else 0) if across else (0 if spot[3] == 0 else 2)
+            return tuple(i ^ distance if n == axis else i for n, i in enumerate(spot))
+
+        return [(number(spot), number(other(spot))) for spot in spots]
+
+    steps = [step(across, distance) for across in (True, False) for distance in (1, 2)]
+    steps.append([(number(spot), number((*spot[:3], spot[3] ^ 1))) for spot in spots])
+    return steps
+
+
+def slow(block):
+    return pltpu.with_memory_space_constraint(block, HBM)
+
+
 def halves(block):
     high = block.astype(BF16)
     low = (block - high.astype(F32)).astype(BF16)
@@ -56,10 +81,14 @@
     return lax.broadcasted_iota(I32, shape, dim)
 
 
-def mass_kernel(place, meta, ratio, own, out, counts, *, patches, fields, edge, size_y, size_z, new_count, pairs):
+def mass_kernel(place, meta, ratio_in, own_in, out, ratio, own, counts, sems, *, patches, fields, edge, size_y, size_z, new_count, pairs):
     lanes = edge * edge
     half = lanes // 2
     index_y = place[0]
+    ratio_copy = pltpu.make_async_copy(ratio_in, ratio, sems.at[0])
+    own_copy = pltpu.make_async_copy(own_in, own, sems.at[1])
+    ratio_copy.start()
+    own_copy.start()
     counts[...] = jnp.zeros_like(counts)
     at_x = iota((edge, lanes), 0)
     at_y = iota((edge, lanes), 1) // edge
@@ -77,7 +106,9 @@
         counts[o] = counts[o] + jnp.where(hit, 1.0, 0.0)
         return carry
 
+    ratio_copy.wait()
     lax.fori_loop(0, pairs, count, 0)
+    own_copy.wait()
 
     def add(o, sums):
         weight = counts[o]
@@ -104,8 +135,8 @@
 
 
 def partials_kernel(
-    place, meta_own, meta_peer, ratio, own, peer,
-    out, table, split, code_k, code_x,
+    place, meta_own, meta_peer, ratio_in, own_in, peer,
+    out, ratio, own, table, split, code_k, code_x, sems,
     *, patches, fields, edge, size_x, size_y, chips_y, cores, new_count, pairs,
 ):
     rows = fields * edge
@@ -113,6 +144,10 @@
     index_y = place[0]
     core = place[1]
     size_z = chips_y * cores
+    ratio_copy = pltpu.make_async_copy(ratio_in, ratio, sems.at[0])
+    own_copy = pltpu.make_async_copy(own_in, own, sems.at[1])
+    ratio_copy.start()
+    own_copy.start()
 
     def prepare(o, carry):
         high, low = halves(own[o])
@@ -122,8 +157,6 @@
         split[patches + o, 0:rows] = high
         split[patches + o, rows:2 * rows] = low
         return carry
-
-    lax.fori_loop(0, patches, prepare, 0)
 
     out[...] = jnp.zeros_like(out)
     cell = iota((lanes, lanes), 0)
@@ -152,6 +185,7 @@
 
         return found + mine.astype(I32)
 
+    ratio_copy.wait()
     found = lax.fori_loop(0, pairs, functools.partial(enlist, meta=meta_own, base=0), jnp.int32(0))
     found = lax.fori_loop(0, pairs, functools.partial(enlist, meta=meta_peer, base=patches), found)
 
@@ -161,6 +195,9 @@
         table[2, found + extra] = 0
         table[3, found + extra] = 0
         table[4, found + extra] = 0
+
+    own_copy.wait()
+    lax.fori_loop(0, patches, prepare, 0)
 
     lane_k = iota((1, lanes), 1)
     lane_code = (lane_k // edge) * 4096 + lane_k % edge
@@ -193,18 +230,30 @@
 
 
 def fold_kernel(a, out):
-    total = a[0]
-    for s in range(1, a.shape[0]):
-        total = total + a[s]
-    out[...] = total
+    size = out.shape[0]
+    sources = a.shape[0] // size
+
+    def add(i, carry):
+        total = a[i]
+        for s in range(1, sources):
+            total = total + a[s * size + i]
+        out[i] = total
+        return carry
+
+    lax.fori_loop(0, size, add, 0)
 
 
 def gather_kernel(a, new_data, faces, *, count, fields, edge):
     rows = fields * edge
     lanes = edge * edge
-    whole = a[0]
-    for s in range(1, a.shape[0]):
-        whole = whole + a[s]
+    sources = a.shape[0] // count
+    sums = []
+    for q in range(count):
+        total = a[q]
+        for s in range(1, sources):
+            total = total + a[s * count + q]
+        sums.append(total)
+    whole = jnp.concatenate(sums, axis=0)
     new_data[...] = whole
     high, low = halves(whole)
     stacked = jnp.concatenate([high, low], axis=0)
@@ -279,46 +328,52 @@
     owners = size_x * chips_y * count
     smem = pl.BlockSpec(memory_space=SMEM)
     vmem = pl.BlockSpec(memory_space=VMEM)
+    hbm = pl.BlockSpec(memory_space=HBM)
     params = pltpu.CompilerParams(vmem_limit_bytes=24 * 1024 * 1024)
     mass = pl.pallas_call(
         functools.partial(
             mass_kernel, patches=patches, fields=fields, edge=edge, size_y=size_y,
             size_z=chips_y * cores, new_count=count, pairs=pairs,
         ),
-        out_shape=VMEM((size_x * chips_y, 8, half), F32),
-        in_specs=[smem, smem, smem, vmem],
+        out_shape=jax.ShapeDtypeStruct((size_y, 8, half), F32),
+        in_specs=[smem, smem, hbm, hbm],
         out_specs=vmem,
-        scratch_shapes=[pltpu.VMEM((patches, edge, lanes), F32)],
+        scratch_shapes=[
+            pltpu.SMEM(new_ratio.shape, I32),
+            pltpu.VMEM((patches, rows, lanes), F32),
+            pltpu.VMEM((patches, edge, lanes), F32),
+            DMA((2,)),
+        ],
         compiler_params=params,
         name="mass",
-    )(place, meta, new_ratio, own)
-    plane = lax.all_to_all(mass, PLANE, 0, 0, tiled=True)
+    )(place, meta, slow(new_ratio), slow(own))
+    column = lax.all_to_all(mass, "gy", 0, 0, tiled=True)
     partials = pl.pallas_call(
         functools.partial(
             partials_kernel, patches=patches, fields=fields, edge=edge, size_x=size_x,
             size_y=size_y, chips_y=chips_y, cores=cores, new_count=count, pairs=pairs,
         ),
-        out_shape=jax.ShapeDtypeStruct((owners, rows, lanes), F32),
-        in_specs=[smem, smem, smem, smem, vmem, vmem],
+        out_shape=HBM((owners, rows, lanes), F32),
+        in_specs=[smem, smem, smem, hbm, hbm, vmem],
         out_specs=vmem,
         scratch_shapes=[
+            pltpu.SMEM(new_ratio.shape, I32),
+            pltpu.VMEM((patches, rows, lanes), F32),
             pltpu.SMEM((5, 2 * pairs + UNROLL), I32),
             pltpu.VMEM((2 * patches, 2 * rows, lanes), BF16),
             pltpu.VMEM((lanes, lanes), I32),
             pltpu.VMEM((rows, 2 * rows), I32),
+            DMA((2,)),
         ],
         compiler_params=params,
         name="partials",
-    )(place, meta, peer_meta, new_ratio, own, fast(peer))
+    )(place, meta, peer_meta, slow(new_ratio), slow(own), fast(peer))
 
     first_groups, last_groups = mixed_groups(size_x, size_y, chips_y, cores)
     first = lax.all_to_all(partials, ALL_AXES, 0, 0, tiled=True, axis_index_groups=first_groups)
-    total = jnp.sum(plane, axis=0)
-    total = crossed(total, "gz_1", 1)
-    distance = 1
-    while distance < size_y:
-        total = crossed(total, "gy", distance)
-        distance = distance * 2
+    total = jnp.sum(column, axis=0)
+    for pairs_of in mixed_steps(size_x, size_y, chips_y, cores):
+        total = total + lax.ppermute(total, ALL_AXES, pairs_of)
     folded = pl.pallas_call(
         fold_kernel,
         out_shape=VMEM((owners // size_x, rows, lanes), F32),
@@ -326,7 +381,7 @@
         out_specs=vmem,
         compiler_params=params,
         name="fold",
-    )(fast(first.reshape(size_x, owners // size_x, rows, lanes)))
+    )(fast(first))
     last = lax.all_to_all(folded, ALL_AXES, 0, 0, tiled=True, axis_index_groups=last_groups)
     new_data, faces = pl.pallas_call(
         functools.partial(gather_kernel, count=count, fields=fields, edge=edge),
@@ -338,7 +393,7 @@
         out_specs=(vmem, vmem),
         compiler_params=params,
         name="gather",
-    )(fast(last.reshape(chips_y, count * rows, lanes)))
+    )(fast(last))
     before = shifted(faces, ALL_AXES, 1)
     after = shifted(faces, ALL_AXES, -1)
     interface_jump = pl.pallas_call(

time: 128 us -> 131 us (1.023)
  waiting for transfers between devices: 47.9 us -> 54.8 us
  starting transfers between devices: 57.6 us -> 53.7 us
  local copies, waits for them, and re-layouts: 4.49 us -> 0.74 us
  Pallas kernels: 16.2 us -> 19.1 us
    ppermute x5, starting transfers between devices: 25 us -> 16.9 us  [body(): total = total + lax.ppermute(total, ALL_AXES, pairs_of)]
    all_to_all x1, waiting for transfers between devices: 3.09 us -> 9.44 us  [body(): column = lax.all_to_all(mass, 'gy', 0, 0, tiled=True)]
    all_to_all x1, starting transfers between devices: 4.77 us -> 10.4 us  [body(): column = lax.all_to_all(mass, 'gy', 0, 0, tiled=True)]
    unnamed x13 -> x3, local copies, waits for them, and re-layouts: 4.41 us -> 0.65 us
    ppermute x2, starting transfers between devices: 9.74 us -> 7.36 us  [shifted(): return lax.ppermute(block, axis, route)]
    pallas_call x1, Pallas kernels: 8.23 us -> 10.5 us  [body(): pl.pallas_call(functools.partial(partials_kernel, patches=patches, fields...]
  transfers between devices with their start and end apart: 12 -> 12, of which waited for: 10 -> 10; matrix products, arithmetic and copies ran while one was open for 1% -> 1% of each run, Pallas kernels for 4% -> 5%
where the time goes in v4:
time: 131 us; the launch traced here: 130 us
  waiting for transfers between devices  54.8 us (42%)
  starting transfers between devices  53.7 us (41%)
  Pallas kernels  19.1 us (15%)
    all_to_all x1, waiting for transfers between devices, body(): lax.all_to_all(partials, ALL_AXES, 0, 0, tiled=True, axis_index_groups=fi...  21.9 us
    ppermute x5, starting transfers between devices, body(): total = total + lax.ppermute(total, ALL_AXES, pairs_of)  16.9 us
    ppermute x5, waiting for transfers between devices, body(): total = total + lax.ppermute(total, ALL_AXES, pairs_of)  14.7 us
    pallas_call x1, Pallas kernels, body(): pl.pallas_call(functools.partial(partials_kernel, patches=patches, fields...  10.5 us
    all_to_all x1, starting transfers between devices, body(): column = lax.all_to_all(mass, 'gy', 0, 0, tiled=True)  10.4 us
    all_to_all x1, starting transfers between devices, body(): lax.all_to_all(partials, ALL_AXES, 0, 0, tiled=True, axis_index_groups=fi...  10.1 us
    all_to_all x1, waiting for transfers between devices, body(): column = lax.all_to_all(mass, 'gy', 0, 0, tiled=True)  9.44 us
    ppermute x2, waiting for transfers between devices, shifted(): return lax.ppermute(block, axis, route)  8.09 us
  transfers between devices with their start and end apart: 12, of which 10 were waited for; matrix products, arithmetic and copies ran while one was open for 1% of the time, Pallas kernels for 5%

profile of v4, /device:TPU:2, one launch (start us, length us, event | category | flops | bytes accessed | tf_op | source)
XLA Modules:
  0.0 129.9 jit_solution(16979541509030948676)
XLA Ops:
  0.6 1.9 %collective-permute-start.1 = (f32[12,80,256]{2,1,0:T(8,128)}, f32[12,80,256]{2,1,0:T(8,128)S(1)}, u32[]{:S(2)}, u32[]{:S(2)}) collective-permute-start(f32[12,80,256]{2,1,0:T(8,128)} %bitcast.13), channel_id=1, source_target_pairs={{0,1},{1,0},{2,3},{3,2},{4,5},{5,4},{6,7},{7,6},{8,9},{9,8},{10,11... | collective-permute-start | bytes 2949128 | tf_op jit(solution)/shard_map/ppermute | solution.py:327
  2.6 0.7 pad_add_fusion.meta_own.meta
  3.3 2.4 %collective-permute-start = (s32[6,32]{1,0:T(8,128)S(1)}, s32[6,32]{1,0:T(8,128)S(1)}, u32[]{:S(2)}, u32[]{:S(2)}) collective-permute-start(s32[6,32]{1,0:T(8,128)S(1)} %pad_add_fusion.meta_own.meta), channel_id=1, source_target_pairs={{0,1},{1,0},{2,3},{3,2},{4,5},{5,4},{6,7},{7,6},{8,9},{9,8},{10,11... | collective-permute-start | bytes 2312 | tf_op jit(solution)/shard_map/ppermute | solution.py:326
  5.7 0.1 stack.23.place
  5.8 0.0 copy-start
  5.8 0.7 collective-permute-done.meta_peer
  6.5 0.0 collective-permute-done.1.peer
  6.5 10.5 %partials.1 = f32[48,80,256]{2,1,0:T(8,128)} custom-call(s32[5]{0:T(128)S(1)} %stack.23.place, s32[6,32]{1,0:T(8,128)S(1)} %pad_add_fusion.meta_own.meta, s32[6,32]{1,0:T(8,128)S(1)} %collective-permute-done.meta_peer, s32[1536]{0:T(1024)} %ratio_in.3, f32[12,80,256]{2,1,0:T(8,128)} %bitcast.14, f32[12,80,256]{2,1,0:T(8,128)S(1)} %collective-permute-done.1.peer), custom_call_target="tpu_custom_call" | custom-call | tf_op jit(solution)/shard_map/partials/pallas_call | solution.py:351
  17.0 10.1 %all-to-all-start = ((f32[48,80,256]{2,1,0:T(8,128)}), f32[48,80,256]{2,1,0:T(8,128)}, u32[]{:S(2)}, u32[]{:S(2)}) async-start(f32[48,80,256]{2,1,0:T(8,128)} %partials.1), calls=%async_computation | async-start | bytes 7864320 | tf_op jit(solution)/shard_map/all_to_all | solution.py:373
  27.1 0.0 copy-done
  27.1 3.1 %mass.1 = f32[16,8,128]{2,1,0:T(8,128)} custom-call(s32[5]{0:T(128)S(1)} %stack.23.place, s32[6,32]{1,0:T(8,128)S(1)} %pad_add_fusion.meta_own.meta, s32[1536]{0:T(1024)} %ratio_in.3, f32[12,80,256]{2,1,0:T(8,128)} %bitcast.15), custom_call_target="tpu_custom_call" | custom-call | tf_op jit(solution)/shard_map/mass/pallas_call | solution.py:333
  30.2 21.9 %all-to-all-done.a = f32[48,80,256]{2,1,0:T(8,128)} async-done(((f32[48,80,256]{2,1,0:T(8,128)}), f32[48,80,256]{2,1,0:T(8,128)}, u32[]{:S(2)}, u32[]{:S(2)}) %all-to-all-start) | async-done | bytes 3932192 | tf_op jit(solution)/shard_map/all_to_all | solution.py:373
  52.1 10.4 %all-to-all-start.2 = ((f32[16,8,128]{2,1,0:T(8,128)}), f32[16,8,128]{2,1,0:T(8,128)S(1)}, u32[]{:S(2)}, u32[]{:S(2)}) async-start(f32[16,8,128]{2,1,0:T(8,128)} %mass.1), calls=%async_computation.2 | async-start | bytes 131072 | tf_op jit(solution)/shard_map/all_to_all | solution.py:350
  62.5 3.3 %fold.1 = f32[12,80,256]{2,1,0:T(8,128)} custom-call(f32[48,80,256]{2,1,0:T(8,128)} %all-to-all-done.a), custom_call_target="tpu_custom_call" | custom-call | tf_op jit(solution)/shard_map/fold/pallas_call | solution.py:377
  65.8 9.4 %all-to-all-done.2 = f32[16,8,128]{2,1,0:T(8,128)S(1)} async-done(((f32[16,8,128]{2,1,0:T(8,128)}), f32[16,8,128]{2,1,0:T(8,128)S(1)}, u32[]{:S(2)}, u32[]{:S(2)}) %all-to-all-start.2) | async-done | bytes 65568 | tf_op jit(solution)/shard_map/all_to_all | solution.py:350
  75.2 4.6 %all-to-all-start.1 = ((f32[12,80,256]{2,1,0:T(8,128)}), f32[12,80,256]{2,1,0:T(8,128)S(1)}, u32[]{:S(2)}, u32[]{:S(2)}) async-start(f32[12,80,256]{2,1,0:T(8,128)} %fold.1), calls=%async_computation.1 | async-start | bytes 1966080 | tf_op jit(solution)/shard_map/all_to_all | solution.py:385
  79.8 3.9 %collective-permute-start.4 = (f32[8,128]{1,0:T(8,128)S(1)}, f32[8,128]{1,0:T(8,128)S(1)}, u32[]{:S(2)}, u32[]{:S(2)}) collective-permute-start(f32[8,128]{1,0:T(8,128)S(1)} %reduce_sum.9), channel_id=1, source_target_pairs={{0,2},{1,129},{2,0},{3,131},{4,6},{5,133},{6,4},{7,135},{8,10},{9,... | collective-permute-start | bytes 12296 | tf_op jit(solution)/shard_map/ppermute | solution.py:376
  83.8 5.1 %collective-permute-done.4 = f32[8,128]{1,0:T(8,128)S(1)} collective-permute-done((f32[8,128]{1,0:T(8,128)S(1)}, f32[8,128]{1,0:T(8,128)S(1)}, u32[]{:S(2)}, u32[]{:S(2)}) %collective-permute-start.4) | collective-permute-done | bytes 4128 | tf_op jit(solution)/shard_map/ppermute | solution.py:376
  88.9 4.6 %collective-permute-start.5 = (f32[8,128]{1,0:T(8,128)S(1)}, f32[8,128]{1,0:T(8,128)S(1)}, u32[]{:S(2)}, u32[]{:S(2)}) collective-permute-start(f32[8,128]{1,0:T(8,128)S(1)} %add.27), channel_id=1, source_target_pairs={{0,4},{1,257},{2,6},{3,259},{4,0},{5,261},{6,2},{7,263},{8,12},{9,... | collective-permute-start | bytes 12296 | tf_op jit(solution)/shard_map/ppermute | solution.py:376
  93.5 2.4 %collective-permute-done.5 = f32[8,128]{1,0:T(8,128)S(1)} collective-permute-done((f32[8,128]{1,0:T(8,128)S(1)}, f32[8,128]{1,0:T(8,128)S(1)}, u32[]{:S(2)}, u32[]{:S(2)}) %collective-permute-start.5) | collective-permute-done | bytes 4128 | tf_op jit(solution)/shard_map/ppermute | solution.py:376
  95.9 3.1 %collective-permute-start.6 = (f32[8,128]{1,0:T(8,128)S(1)}, f32[8,128]{1,0:T(8,128)S(1)}, u32[]{:S(2)}, u32[]{:S(2)}) collective-permute-start(f32[8,128]{1,0:T(8,128)S(1)} %add.28), channel_id=1, source_target_pairs={{0,128},{1,3},{2,130},{3,1},{4,132},{5,7},{6,134},{7,5},{8,136},{9... | collective-permute-start | bytes 12296 | tf_op jit(solution)/shard_map/ppermute | solution.py:376
  99.1 2.3 %collective-permute-done.6 = f32[8,128]{1,0:T(8,128)S(1)} collective-permute-done((f32[8,128]{1,0:T(8,128)S(1)}, f32[8,128]{1,0:T(8,128)S(1)}, u32[]{:S(2)}, u32[]{:S(2)}) %collective-permute-start.6) | collective-permute-done | bytes 4128 | tf_op jit(solution)/shard_map/ppermute | solution.py:376
  101.4 3.3 %collective-permute-start.7 = (f32[8,128]{1,0:T(8,128)S(1)}, f32[8,128]{1,0:T(8,128)S(1)}, u32[]{:S(2)}, u32[]{:S(2)}) collective-permute-start(f32[8,128]{1,0:T(8,128)S(1)} %add.29), channel_id=1, source_target_pairs={{0,256},{1,5},{2,258},{3,7},{4,260},{5,1},{6,262},{7,3},{8,264},{9... | collective-permute-start | bytes 12296 | tf_op jit(solution)/shard_map/ppermute | solution.py:376
  104.8 3.6 %collective-permute-done.7 = f32[8,128]{1,0:T(8,128)S(1)} collective-permute-done((f32[8,128]{1,0:T(8,128)S(1)}, f32[8,128]{1,0:T(8,128)S(1)}, u32[]{:S(2)}, u32[]{:S(2)}) %collective-permute-start.7) | collective-permute-done | bytes 4128 | tf_op jit(solution)/shard_map/ppermute | solution.py:376
  108.4 1.9 %collective-permute-start.8 = (f32[8,128]{1,0:T(8,128)S(1)}, f32[8,128]{1,0:T(8,128)S(1)}, u32[]{:S(2)}, u32[]{:S(2)}) collective-permute-start(f32[8,128]{1,0:T(8,128)S(1)} %add.30), channel_id=1, source_target_pairs={{0,1},{1,0},{2,3},{3,2},{4,5},{5,4},{6,7},{7,6},{8,9},{9,8},{10,11... | collective-permute-start | bytes 12296 | tf_op jit(solution)/shard_map/ppermute | solution.py:376
  110.3 1.1 collective-permute-done.8
  111.5 0.0 all-to-all-done.1.a
  111.5 0.8 gather.1
  112.2 5.4 %collective-permute-start.3 = (f32[3,6,5,256]{3,2,1,0:T(8,128)S(1)}, f32[3,6,5,256]{3,2,1,0:T(8,128)S(1)}, u32[]{:S(2)}, u32[]{:S(2)}) collective-permute-start(f32[3,6,5,256]{3,2,1,0:T(8,128)S(1)} %get-tuple-element.6.own), channel_id=1, source_target_pairs={{1,0},{2,1},{3,2},{4,3},{5,4},{6,5},{7,6},{8,7},{9,8},{10,9},{11,1... | collective-permute-start | bytes 276488 | tf_op jit(solution)/shard_map/ppermute | solution.py:26
  117.7 1.9 %collective-permute-start.2 = (f32[3,6,5,256]{3,2,1,0:T(8,128)S(1)}, f32[3,6,5,256]{3,2,1,0:T(8,128)S(1)}, u32[]{:S(2)}, u32[]{:S(2)}) collective-permute-start(f32[3,6,5,256]{3,2,1,0:T(8,128)S(1)} %get-tuple-element.6.own), channel_id=1, source_target_pairs={{0,1},{1,2},{2,3},{3,4},{4,5},{5,6},{6,7},{7,8},{8,9},{9,10},{10,1... | collective-permute-start | bytes 276488 | tf_op jit(solution)/shard_map/ppermute | solution.py:26
  119.6 0.6 copy.11
  120.3 0.1 collective-permute-done.3.after
  120.3 8.0 %collective-permute-done.2.before = f32[3,6,5,256]{3,2,1,0:T(8,128)S(1)} collective-permute-done((f32[3,6,5,256]{3,2,1,0:T(8,128)S(1)}, f32[3,6,5,256]{3,2,1,0:T(8,128)S(1)}, u32[]{:S(2)}, u32[]{:S(2)}) %collective-permute-start.2) | collective-permute-done | bytes 92192 | tf_op jit(solution)/shard_map/ppermute | solution.py:26
  128.3 1.5 %jump.1 = f32[3,5,6,256]{3,2,1,0:T(8,128)} custom-call(s32[5]{0:T(128)} %copy-done, s32[3,6]{1,0:T(4,128)} %side.1, s32[3,6]{1,0:T(4,128)} %patch.1, f32[3,6,5,256]{3,2,1,0:T(8,128)S(1)} %get-tuple-element.6.own, f32[3,6,5,256]{3,2,1,0:T(8,128)S(1)} %collective-permute-done.2.before, f32[3,6,5,256]{3,2,1,0:T(8,128)S(1)} %collective-permute-done.3.after), custom_call_target="tpu_custom_call" | custom-call | tf_op jit(solution)/shard_map/jump/pallas_call | solution.py:399
  (7 shorter events, 0.0 us)
Async XLA Ops:
  0.6 5.9 %collective-permute-start.1 = (f32[12,80,256]{2,1,0:T(8,128)}, f32[12,80,256]{2,1,0:T(8,128)S(1)}, u32[]{:S(2)}, u32[]{:S(2)}) collective-permute-start(f32[12,80,256]{2,1,0:T(8,128)} %bitcast.13), channel_id=1, source_target_pairs={{0,1},{1,0},{2,3},{3,2},{4,5},{5,4},{6,7},{7,6},{8,9},{9,8},{10,11... | collective-permute-start | bytes 2949128 | tf_op jit(solution)/shard_map/ppermute | solution.py:327
  3.3 3.2 %collective-permute-start = (s32[6,32]{1,0:T(8,128)S(1)}, s32[6,32]{1,0:T(8,128)S(1)}, u32[]{:S(2)}, u32[]{:S(2)}) collective-permute-start(s32[6,32]{1,0:T(8,128)S(1)} %pad_add_fusion.meta_own.meta), channel_id=1, source_target_pairs={{0,1},{1,0},{2,3},{3,2},{4,5},{5,4},{6,7},{7,6},{8,9},{9,8},{10,11... | collective-permute-start | bytes 2312 | tf_op jit(solution)/shard_map/ppermute | solution.py:326
  5.8 21.3 %copy-start = (s32[5]{0:T(128)}, s32[5]{0:T(128)S(1)}, u32[]{:S(2)}) copy-start(s32[5]{0:T(128)S(1)} %stack.23.place) | copy-start | bytes 64
  17.0 35.1 %all-to-all-start = ((f32[48,80,256]{2,1,0:T(8,128)}), f32[48,80,256]{2,1,0:T(8,128)}, u32[]{:S(2)}, u32[]{:S(2)}) async-start(f32[48,80,256]{2,1,0:T(8,128)} %partials.1), calls=%async_computation | async-start | bytes 7864320 | tf_op jit(solution)/shard_map/all_to_all | solution.py:373
  52.1 23.1 %all-to-all-start.2 = ((f32[16,8,128]{2,1,0:T(8,128)}), f32[16,8,128]{2,1,0:T(8,128)S(1)}, u32[]{:S(2)}, u32[]{:S(2)}) async-start(f32[16,8,128]{2,1,0:T(8,128)} %mass.1), calls=%async_computation.2 | async-start | bytes 131072 | tf_op jit(solution)/shard_map/all_to_all | solution.py:350
  75.2 36.3 %all-to-all-start.1 = ((f32[12,80,256]{2,1,0:T(8,128)}), f32[12,80,256]{2,1,0:T(8,128)S(1)}, u32[]{:S(2)}, u32[]{:S(2)}) async-start(f32[12,80,256]{2,1,0:T(8,128)} %fold.1), calls=%async_computation.1 | async-start | bytes 1966080 | tf_op jit(solution)/shard_map/all_to_all | solution.py:385
  79.8 9.1 %collective-permute-start.4 = (f32[8,128]{1,0:T(8,128)S(1)}, f32[8,128]{1,0:T(8,128)S(1)}, u32[]{:S(2)}, u32[]{:S(2)}) collective-permute-start(f32[8,128]{1,0:T(8,128)S(1)} %reduce_sum.9), channel_id=1, source_target_pairs={{0,2},{1,129},{2,0},{3,131},{4,6},{5,133},{6,4},{7,135},{8,10},{9,... | collective-permute-start | bytes 12296 | tf_op jit(solution)/shard_map/ppermute | solution.py:376
  88.9 7.0 %collective-permute-start.5 = (f32[8,128]{1,0:T(8,128)S(1)}, f32[8,128]{1,0:T(8,128)S(1)}, u32[]{:S(2)}, u32[]{:S(2)}) collective-permute-start(f32[8,128]{1,0:T(8,128)S(1)} %add.27), channel_id=1, source_target_pairs={{0,4},{1,257},{2,6},{3,259},{4,0},{5,261},{6,2},{7,263},{8,12},{9,... | collective-permute-start | bytes 12296 | tf_op jit(solution)/shard_map/ppermute | solution.py:376
  95.9 5.5 %collective-permute-start.6 = (f32[8,128]{1,0:T(8,128)S(1)}, f32[8,128]{1,0:T(8,128)S(1)}, u32[]{:S(2)}, u32[]{:S(2)}) collective-permute-start(f32[8,128]{1,0:T(8,128)S(1)} %add.28), channel_id=1, source_target_pairs={{0,128},{1,3},{2,130},{3,1},{4,132},{5,7},{6,134},{7,5},{8,136},{9... | collective-permute-start | bytes 12296 | tf_op jit(solution)/shard_map/ppermute | solution.py:376
  101.4 7.0 %collective-permute-start.7 = (f32[8,128]{1,0:T(8,128)S(1)}, f32[8,128]{1,0:T(8,128)S(1)}, u32[]{:S(2)}, u32[]{:S(2)}) collective-permute-start(f32[8,128]{1,0:T(8,128)S(1)} %add.29), channel_id=1, source_target_pairs={{0,256},{1,5},{2,258},{3,7},{4,260},{5,1},{6,262},{7,3},{8,264},{9... | collective-permute-start | bytes 12296 | tf_op jit(solution)/shard_map/ppermute | solution.py:376
  108.4 3.0 %collective-permute-start.8 = (f32[8,128]{1,0:T(8,128)S(1)}, f32[8,128]{1,0:T(8,128)S(1)}, u32[]{:S(2)}, u32[]{:S(2)}) collective-permute-start(f32[8,128]{1,0:T(8,128)S(1)} %add.30), channel_id=1, source_target_pairs={{0,1},{1,0},{2,3},{3,2},{4,5},{5,4},{6,7},{7,6},{8,9},{9,8},{10,11... | collective-permute-start | bytes 12296 | tf_op jit(solution)/shard_map/ppermute | solution.py:376
  112.2 8.1 %collective-permute-start.3 = (f32[3,6,5,256]{3,2,1,0:T(8,128)S(1)}, f32[3,6,5,256]{3,2,1,0:T(8,128)S(1)}, u32[]{:S(2)}, u32[]{:S(2)}) collective-permute-start(f32[3,6,5,256]{3,2,1,0:T(8,128)S(1)} %get-tuple-element.6.own), channel_id=1, source_target_pairs={{1,0},{2,1},{3,2},{4,3},{5,4},{6,5},{7,6},{8,7},{9,8},{10,9},{11,1... | collective-permute-start | bytes 276488 | tf_op jit(solution)/shard_map/ppermute | solution.py:26
  117.7 10.7 %collective-permute-start.2 = (f32[3,6,5,256]{3,2,1,0:T(8,128)S(1)}, f32[3,6,5,256]{3,2,1,0:T(8,128)S(1)}, u32[]{:S(2)}, u32[]{:S(2)}) collective-permute-start(f32[3,6,5,256]{3,2,1,0:T(8,128)S(1)} %get-tuple-element.6.own), channel_id=1, source_target_pairs={{0,1},{1,2},{2,3},{3,4},{4,5},{5,6},{6,7},{7,8},{8,9},{9,10},{10,1... | collective-permute-start | bytes 276488 | tf_op jit(solution)/shard_map/ppermute | solution.py:26

commit v5 on v4

--- a/solution.py
+++ b/solution.py
@@ -43,30 +43,6 @@
     return along_x, along_y
 
 
-def mixed_steps(size_x, size_y, chips_y, cores):
-    shape = (size_x, size_y, chips_y, cores)
-    spots = [
-        (x, z, y, c) for x in range(size_x) for z in range(size_y) for y in range(chips_y) for c in range(cores)
-    ]
-
-    def number(spot):
-        at = 0
-        for size, i in zip(shape, spot):
-            at = at * size + i
-        return at
-
-    def step(across, distance):
-        def other(spot):
-            axis = (2 if spot[3] == 0 else 0) if across else (0 if spot[3] == 0 else 2)
-            return tuple(i ^ distance if n == axis else i for n, i in enumerate(spot))
-
-        return [(number(spot), number(other(spot))) for spot in spots]
-
-    steps = [step(across, distance) for across in (True, False) for distance in (1, 2)]
-    steps.append([(number(spot), number((*spot[:3], spot[3] ^ 1))) for spot in spots])
-    return steps
-
-
 def slow(block):
     return pltpu.with_memory_space_constraint(block, HBM)
 
@@ -75,6 +51,14 @@
     high = block.astype(BF16)
     low = (block - high.astype(F32)).astype(BF16)
     return high, low
+
+
+def over(value, size):
+    return value >> (size.bit_length() - 1)
+
+
+def within(value, size):
+    return value & (size - 1)
 
 
 def iota(shape, dim):
@@ -91,12 +75,12 @@
     own_copy.start()
     counts[...] = jnp.zeros_like(counts)
     at_x = iota((edge, lanes), 0)
-    at_y = iota((edge, lanes), 1) // edge
-    at_z = iota((edge, lanes), 1) % edge
+    at_y = over(iota((edge, lanes), 1), edge)
+    at_z = within(iota((edge, lanes), 1), edge)
 
     def count(p, carry):
         dest = meta[5, p]
-        owner = ((dest // size_z) * size_y + index_y) * size_z + dest % size_z
+        owner = (over(dest, size_z) * size_y + index_y) * size_z + within(dest, size_z)
         reach = edge * ratio[owner * new_count + meta[1, p]]
         hit = jnp.full((edge, lanes), True)
         for a, at in enumerate((at_x, at_y, at_z)):
@@ -144,6 +128,8 @@
     index_y = place[0]
     core = place[1]
     size_z = chips_y * cores
+    for size in (edge, size_z, cores):
+        assert size & (size - 1) == 0
     ratio_copy = pltpu.make_async_copy(ratio_in, ratio, sems.at[0])
     own_copy = pltpu.make_async_copy(own_in, own, sems.at[1])
     ratio_copy.start()
@@ -160,26 +146,26 @@
 
     out[...] = jnp.zeros_like(out)
     cell = iota((lanes, lanes), 0)
-    code_k[...] = (cell // edge) * 4096 + cell % edge
+    code_k[...] = over(cell, edge) * 4096 + within(cell, edge)
     row = iota((rows, 2 * rows), 0)
     col = iota((rows, 2 * rows), 1) % rows
-    code_x[...] = (col // edge - row // edge) * 4096 + col % edge
+    code_x[...] = (over(col, edge) - over(row, edge)) * 4096 + within(col, edge)
 
     def enlist(p, found, meta, base):
         dest = meta[5, p]
-        mine = dest % cores == core
+        mine = within(dest, cores) == core
 
         @pl.when(mine)
         def _():
             table[0, found] = base + meta[0, p]
-            iz = dest % size_z
-            ix = dest // size_z
+            iz = within(dest, size_z)
+            ix = over(dest, size_z)
             slot = meta[1, p]
             owner = (ix * size_y + index_y) * size_z + iz
             table[1, found] = ratio[owner * new_count + slot]
             table[2, found] = meta[2, p]
             table[3, found] = meta[3, p] * 4096 + meta[4, p]
-            chip_y = iz // cores
+            chip_y = over(iz, cores)
             chip = jnp.where(core == 0, ix * chips_y + chip_y, chip_y * size_x + ix)
             table[4, found] = chip * new_count + slot
 
@@ -200,8 +186,8 @@
     lax.fori_loop(0, patches, prepare, 0)
 
     lane_k = iota((1, lanes), 1)
-    lane_code = (lane_k // edge) * 4096 + lane_k % edge
-    row_x = iota((rows, 1), 0) % edge
+    lane_code = over(lane_k, edge) * 4096 + within(lane_k, edge)
+    row_x = within(iota((rows, 1), 0), edge)
 
     def remap(step, carry):
         results = []
@@ -230,17 +216,10 @@
 
 
 def fold_kernel(a, out):
-    size = out.shape[0]
-    sources = a.shape[0] // size
-
-    def add(i, carry):
-        total = a[i]
-        for s in range(1, sources):
-            total = total + a[s * size + i]
-        out[i] = total
-        return carry
-
-    lax.fori_loop(0, size, add, 0)
+    total = a[0]
+    for s in range(1, a.shape[0]):
+        total = total + a[s]
+    out[...] = total
 
 
 def gather_kernel(a, new_data, faces, *, count, fields, edge):
@@ -258,8 +237,8 @@
     high, low = halves(whole)
     stacked = jnp.concatenate([high, low], axis=0)
     source = iota((lanes, lanes), 0)
-    target = iota((lanes, lanes), 1) % edge
-    here = (iota((edge, lanes), 1) // edge) == iota((edge, lanes), 0)
+    target = within(iota((lanes, lanes), 1), edge)
+    here = over(iota((edge, lanes), 1), edge) == iota((edge, lanes), 0)
     picks = (
         source == target,
         source == target + (lanes - edge),
@@ -335,7 +314,7 @@
             mass_kernel, patches=patches, fields=fields, edge=edge, size_y=size_y,
             size_z=chips_y * cores, new_count=count, pairs=pairs,
         ),
-        out_shape=jax.ShapeDtypeStruct((size_y, 8, half), F32),
+        out_shape=jax.ShapeDtypeStruct((size_x * chips_y, 8, half), F32),
         in_specs=[smem, smem, hbm, hbm],
         out_specs=vmem,
         scratch_shapes=[
@@ -347,7 +326,7 @@
         compiler_params=params,
         name="mass",
     )(place, meta, slow(new_ratio), slow(own))
-    column = lax.all_to_all(mass, "gy", 0, 0, tiled=True)
+    plane = lax.all_to_all(mass, ("gx", "gz_0"), 0, 0, tiled=True)
     partials = pl.pallas_call(
         functools.partial(
             partials_kernel, patches=patches, fields=fields, edge=edge, size_x=size_x,
@@ -371,17 +350,19 @@
 
     first_groups, last_groups = mixed_groups(size_x, size_y, chips_y, cores)
     first = lax.all_to_all(partials, ALL_AXES, 0, 0, tiled=True, axis_index_groups=first_groups)
-    total = jnp.sum(column, axis=0)
-    for pairs_of in mixed_steps(size_x, size_y, chips_y, cores):
-        total = total + lax.ppermute(total, ALL_AXES, pairs_of)
+    total = jnp.sum(plane, axis=0)
+    total = lax.psum(total, "gy")
+    total = total + lax.ppermute(total, "gz_1", swap)
+    kept = owners // size_x
     folded = pl.pallas_call(
         fold_kernel,
-        out_shape=VMEM((owners // size_x, rows, lanes), F32),
-        in_specs=[vmem],
-        out_specs=vmem,
+        out_shape=jax.ShapeDtypeStruct((kept, rows, lanes), F32),
+        grid=(kept // count,),
+        in_specs=[pl.BlockSpec((size_x, count, rows, lanes), lambda i: (0, i, 0, 0))],
+        out_specs=pl.BlockSpec((count, rows, lanes), lambda i: (i, 0, 0)),
         compiler_params=params,
         name="fold",
-    )(fast(first))
+    )(first.reshape(size_x, kept, rows, lanes))
     last = lax.all_to_all(folded, ALL_AXES, 0, 0, tiled=True, axis_index_groups=last_groups)
     new_data, faces = pl.pallas_call(
         functools.partial(gather_kernel, count=count, fields=fields, edge=edge),

time: 131 us -> 122 us (0.931)
  blocking collectives: 0 us -> 33.9 us
  starting transfers between devices: 53.7 us -> 31.5 us
  waiting for transfers between devices: 54.8 us -> 34.4 us
    psum x0 -> x1, blocking collectives: none -> 33.9 us  [body(): total = lax.psum(total, 'gy')]
    ppermute x5 -> x1, starting transfers between devices: 16.9 us -> 1.91 us  [body(): total = total + lax.ppermute(total, 'gz_1', swap)]
    ppermute x5 -> x1, waiting for transfers between devices: 14.7 us -> 1.13 us  [body(): total = total + lax.ppermute(total, 'gz_1', swap)]
    all_to_all x1, waiting for transfers between devices: 9.44 us -> 2.36 us  [body(): plane = lax.all_to_all(mass, ('gx', 'gz_0'), 0, 0, tiled=True)]
    all_to_all x1, starting transfers between devices: 10.4 us -> 4.77 us  [body(): plane = lax.all_to_all(mass, ('gx', 'gz_0'), 0, 0, tiled=True)]
  transfers between devices with their start and end apart: 12 -> 8, of which waited for: 10 -> 6; matrix products, arithmetic and copies ran while one was open for 1% -> 1% of each run, Pallas kernels for 5% -> 6%
where the time goes in v5:
time: 122 us; the launch traced here: 121 us
  waiting for transfers between devices  34.4 us (28%)
  blocking collectives  33.9 us (28%)
  starting transfers between devices  31.5 us (26%)
  Pallas kernels  19 us (16%)
    psum x1, blocking collectives, body(): total = lax.psum(total, 'gy')  33.9 us
    all_to_all x1, waiting for transfers between devices, body(): lax.all_to_all(partials, ALL_AXES, 0, 0, tiled=True, axis_index_groups=fi...  22.1 us
    all_to_all x1, starting transfers between devices, body(): lax.all_to_all(partials, ALL_AXES, 0, 0, tiled=True, axis_index_groups=fi...  10.1 us
    pallas_call x1, Pallas kernels, body(): pl.pallas_call(functools.partial(partials_kernel, patches=patches, fields...  9.84 us
    ppermute x2, waiting for transfers between devices, shifted(): return lax.ppermute(block, axis, route)  8.09 us
    ppermute x2, starting transfers between devices, shifted(): return lax.ppermute(block, axis, route)  6.87 us
    all_to_all x1, starting transfers between devices, body(): plane = lax.all_to_all(mass, ('gx', 'gz_0'), 0, 0, tiled=True)  4.77 us
    pallas_call x1, Pallas kernels, body(): pl.pallas_call(fold_kernel, out_shape=jax.ShapeDtypeStruct((kept, rows, l...  3.96 us
  transfers between devices with their start and end apart: 8, of which 6 were waited for; matrix products, arithmetic and copies ran while one was open for 1% of the time, Pallas kernels for 6%

profile of v5, /device:TPU:2, one launch (start us, length us, event | category | flops | bytes accessed | tf_op | source)
XLA Modules:
  0.0 121.0 jit_solution(3679299714564433893)
XLA Ops:
  0.6 1.9 %collective-permute-start.1 = (f32[12,80,256]{2,1,0:T(8,128)}, f32[12,80,256]{2,1,0:T(8,128)S(1)}, u32[]{:S(2)}, u32[]{:S(2)}) collective-permute-start(f32[12,80,256]{2,1,0:T(8,128)} %bitcast.14), channel_id=1, source_target_pairs={{0,1},{1,0},{2,3},{3,2},{4,5},{5,4},{6,7},{7,6},{8,9},{9,8},{10,11... | collective-permute-start | bytes 2949128 | tf_op jit(solution)/shard_map/ppermute | solution.py:306
  2.6 0.7 pad_add_fusion.meta_own.meta
  3.3 2.4 %collective-permute-start = (s32[6,32]{1,0:T(8,128)S(1)}, s32[6,32]{1,0:T(8,128)S(1)}, u32[]{:S(2)}, u32[]{:S(2)}) collective-permute-start(s32[6,32]{1,0:T(8,128)S(1)} %pad_add_fusion.meta_own.meta), channel_id=1, source_target_pairs={{0,1},{1,0},{2,3},{3,2},{4,5},{5,4},{6,7},{7,6},{8,9},{9,8},{10,11... | collective-permute-start | bytes 2312 | tf_op jit(solution)/shard_map/ppermute | solution.py:305
  5.7 0.1 stack.23.place
  5.8 0.0 copy-start
  5.8 0.7 collective-permute-done.meta_peer
  6.5 0.0 collective-permute-done.1.peer
  6.5 9.8 %partials.1 = f32[48,80,256]{2,1,0:T(8,128)} custom-call(s32[5]{0:T(128)S(1)} %stack.23.place, s32[6,32]{1,0:T(8,128)S(1)} %pad_add_fusion.meta_own.meta, s32[6,32]{1,0:T(8,128)S(1)} %collective-permute-done.meta_peer, s32[1536]{0:T(1024)} %ratio_in.3, f32[12,80,256]{2,1,0:T(8,128)} %bitcast.15, f32[12,80,256]{2,1,0:T(8,128)S(1)} %collective-permute-done.1.peer), custom_call_target="tpu_custom_call" | custom-call | tf_op jit(solution)/shard_map/partials/pallas_call | solution.py:330
  16.3 10.1 %all-to-all-start = ((f32[48,80,256]{2,1,0:T(8,128)}), f32[48,80,256]{2,1,0:T(8,128)}, u32[]{:S(2)}, u32[]{:S(2)}) async-start(f32[48,80,256]{2,1,0:T(8,128)} %partials.1), calls=%async_computation | async-start | bytes 7864320 | tf_op jit(solution)/shard_map/all_to_all | solution.py:352
  26.5 0.0 copy-done
  26.5 2.9 %mass.1 = f32[16,8,128]{2,1,0:T(8,128)} custom-call(s32[5]{0:T(128)S(1)} %stack.23.place, s32[6,32]{1,0:T(8,128)S(1)} %pad_add_fusion.meta_own.meta, s32[1536]{0:T(1024)} %ratio_in.3, f32[12,80,256]{2,1,0:T(8,128)} %bitcast.16), custom_call_target="tpu_custom_call" | custom-call | tf_op jit(solution)/shard_map/mass/pallas_call | solution.py:312
  29.4 22.1 %all-to-all-done = f32[48,80,256]{2,1,0:T(8,128)} async-done(((f32[48,80,256]{2,1,0:T(8,128)}), f32[48,80,256]{2,1,0:T(8,128)}, u32[]{:S(2)}, u32[]{:S(2)}) %all-to-all-start) | async-done | bytes 3932192 | tf_op jit(solution)/shard_map/all_to_all | solution.py:352
  51.5 4.8 %all-to-all-start.2 = ((f32[16,8,128]{2,1,0:T(8,128)}), f32[16,8,128]{2,1,0:T(8,128)S(1)}, u32[]{:S(2)}, u32[]{:S(2)}) async-start(f32[16,8,128]{2,1,0:T(8,128)} %mass.1), calls=%async_computation.2 | async-start | bytes 131072 | tf_op jit(solution)/shard_map/all_to_all | solution.py:329
  56.2 4.0 %fold.1 = f32[12,80,256]{2,1,0:T(8,128)} custom-call(f32[4,12,80,256]{3,2,1,0:T(8,128)} %bitcast.10.a), custom_call_target="tpu_custom_call" | custom-call | tf_op jit(solution)/shard_map/fold/pallas_call | solution.py:357
  60.2 2.4 %all-to-all-done.2 = f32[16,8,128]{2,1,0:T(8,128)S(1)} async-done(((f32[16,8,128]{2,1,0:T(8,128)}), f32[16,8,128]{2,1,0:T(8,128)S(1)}, u32[]{:S(2)}, u32[]{:S(2)}) %all-to-all-start.2) | async-done | bytes 65568 | tf_op jit(solution)/shard_map/all_to_all | solution.py:329
  62.6 3.5 %all-to-all-start.1 = ((f32[12,80,256]{2,1,0:T(8,128)}), f32[12,80,256]{2,1,0:T(8,128)S(1)}, u32[]{:S(2)}, u32[]{:S(2)}) async-start(f32[12,80,256]{2,1,0:T(8,128)} %fold.1), calls=%async_computation.1 | async-start | bytes 1966080 | tf_op jit(solution)/shard_map/all_to_all | solution.py:366
  66.1 33.9 %psum.7 = f32[8,128]{1,0:T(8,128)S(1)} all-reduce(f32[8,128]{1,0:T(8,128)S(1)} %reduce_sum.9), channel_id=1, replica_groups=mesh['gx'=4,'gy'=16,'gz_0'=4,'gz_1'=2] {'gy'}, use_global_device_ids=true, to_apply=%region_1.0 | all-reduce | flops 1024 | bytes 8192 | tf_op jit(solution)/shard_map/psum | solution.py:354
  100.0 1.9 %collective-permute-start.4 = (f32[8,128]{1,0:T(8,128)S(1)}, f32[8,128]{1,0:T(8,128)S(1)}, u32[]{:S(2)}, u32[]{:S(2)}) collective-permute-start(f32[8,128]{1,0:T(8,128)S(1)} %psum.7), channel_id=1, source_target_pairs={{0,1},{1,0},{2,3},{3,2},{4,5},{5,4},{6,7},{7,6},{8,9},{9,8},{10,11... | collective-permute-start | bytes 12296 | tf_op jit(solution)/shard_map/ppermute | solution.py:355
  102.0 1.1 collective-permute-done.4
  103.1 0.0 all-to-all-done.1.a
  103.1 0.8 gather.1
  103.9 5.0 %collective-permute-start.3 = (f32[3,6,5,256]{3,2,1,0:T(8,128)S(1)}, f32[3,6,5,256]{3,2,1,0:T(8,128)S(1)}, u32[]{:S(2)}, u32[]{:S(2)}) collective-permute-start(f32[3,6,5,256]{3,2,1,0:T(8,128)S(1)} %get-tuple-element.6.own), channel_id=1, source_target_pairs={{1,0},{2,1},{3,2},{4,3},{5,4},{6,5},{7,6},{8,7},{9,8},{10,9},{11,1... | collective-permute-start | bytes 276488 | tf_op jit(solution)/shard_map/ppermute | solution.py:26
  108.8 1.9 %collective-permute-start.2 = (f32[3,6,5,256]{3,2,1,0:T(8,128)S(1)}, f32[3,6,5,256]{3,2,1,0:T(8,128)S(1)}, u32[]{:S(2)}, u32[]{:S(2)}) collective-permute-start(f32[3,6,5,256]{3,2,1,0:T(8,128)S(1)} %get-tuple-element.6.own), channel_id=1, source_target_pairs={{0,1},{1,2},{2,3},{3,4},{4,5},{5,6},{6,7},{7,8},{8,9},{9,10},{10,1... | collective-permute-start | bytes 276488 | tf_op jit(solution)/shard_map/ppermute | solution.py:26
  110.8 0.6 copy.11
  111.4 0.1 collective-permute-done.3.after
  111.5 8.0 %collective-permute-done.2.before = f32[3,6,5,256]{3,2,1,0:T(8,128)S(1)} collective-permute-done((f32[3,6,5,256]{3,2,1,0:T(8,128)S(1)}, f32[3,6,5,256]{3,2,1,0:T(8,128)S(1)}, u32[]{:S(2)}, u32[]{:S(2)}) %collective-permute-start.2) | collective-permute-done | bytes 92192 | tf_op jit(solution)/shard_map/ppermute | solution.py:26
  119.5 1.5 %jump.1 = f32[3,5,6,256]{3,2,1,0:T(8,128)} custom-call(s32[5]{0:T(128)} %copy-done, s32[3,6]{1,0:T(4,128)} %side.1, s32[3,6]{1,0:T(4,128)} %patch.1, f32[3,6,5,256]{3,2,1,0:T(8,128)S(1)} %get-tuple-element.6.own, f32[3,6,5,256]{3,2,1,0:T(8,128)S(1)} %collective-permute-done.2.before, f32[3,6,5,256]{3,2,1,0:T(8,128)S(1)} %collective-permute-done.3.after), custom_call_target="tpu_custom_call" | custom-call | tf_op jit(solution)/shard_map/jump/pallas_call | solution.py:380
  (3 shorter events, 0.0 us)
Async XLA Ops:
  0.6 5.9 %collective-permute-start.1 = (f32[12,80,256]{2,1,0:T(8,128)}, f32[12,80,256]{2,1,0:T(8,128)S(1)}, u32[]{:S(2)}, u32[]{:S(2)}) collective-permute-start(f32[12,80,256]{2,1,0:T(8,128)} %bitcast.14), channel_id=1, source_target_pairs={{0,1},{1,0},{2,3},{3,2},{4,5},{5,4},{6,7},{7,6},{8,9},{9,8},{10,11... | collective-permute-start | bytes 2949128 | tf_op jit(solution)/shard_map/ppermute | solution.py:306
  3.3 3.2 %collective-permute-start = (s32[6,32]{1,0:T(8,128)S(1)}, s32[6,32]{1,0:T(8,128)S(1)}, u32[]{:S(2)}, u32[]{:S(2)}) collective-permute-start(s32[6,32]{1,0:T(8,128)S(1)} %pad_add_fusion.meta_own.meta), channel_id=1, source_target_pairs={{0,1},{1,0},{2,3},{3,2},{4,5},{5,4},{6,7},{7,6},{8,9},{9,8},{10,11... | collective-permute-start | bytes 2312 | tf_op jit(solution)/shard_map/ppermute | solution.py:305
  5.8 20.7 %copy-start = (s32[5]{0:T(128)}, s32[5]{0:T(128)S(1)}, u32[]{:S(2)}) copy-start(s32[5]{0:T(128)S(1)} %stack.23.place) | copy-start | bytes 64
  16.3 35.1 %all-to-all-start = ((f32[48,80,256]{2,1,0:T(8,128)}), f32[48,80,256]{2,1,0:T(8,128)}, u32[]{:S(2)}, u32[]{:S(2)}) async-start(f32[48,80,256]{2,1,0:T(8,128)} %partials.1), calls=%async_computation | async-start | bytes 7864320 | tf_op jit(solution)/shard_map/all_to_all | solution.py:352
  51.5 11.1 %all-to-all-start.2 = ((f32[16,8,128]{2,1,0:T(8,128)}), f32[16,8,128]{2,1,0:T(8,128)S(1)}, u32[]{:S(2)}, u32[]{:S(2)}) async-start(f32[16,8,128]{2,1,0:T(8,128)} %mass.1), calls=%async_computation.2 | async-start | bytes 131072 | tf_op jit(solution)/shard_map/all_to_all | solution.py:329
  62.6 40.5 %all-to-all-start.1 = ((f32[12,80,256]{2,1,0:T(8,128)}), f32[12,80,256]{2,1,0:T(8,128)S(1)}, u32[]{:S(2)}, u32[]{:S(2)}) async-start(f32[12,80,256]{2,1,0:T(8,128)} %fold.1), calls=%async_computation.1 | async-start | bytes 1966080 | tf_op jit(solution)/shard_map/all_to_all | solution.py:366
  100.0 3.0 %collective-permute-start.4 = (f32[8,128]{1,0:T(8,128)S(1)}, f32[8,128]{1,0:T(8,128)S(1)}, u32[]{:S(2)}, u32[]{:S(2)}) collective-permute-start(f32[8,128]{1,0:T(8,128)S(1)} %psum.7), channel_id=1, source_target_pairs={{0,1},{1,0},{2,3},{3,2},{4,5},{5,4},{6,7},{7,6},{8,9},{9,8},{10,11... | collective-permute-start | bytes 12296 | tf_op jit(solution)/shard_map/ppermute | solution.py:355
  103.9 7.6 %collective-permute-start.3 = (f32[3,6,5,256]{3,2,1,0:T(8,128)S(1)}, f32[3,6,5,256]{3,2,1,0:T(8,128)S(1)}, u32[]{:S(2)}, u32[]{:S(2)}) collective-permute-start(f32[3,6,5,256]{3,2,1,0:T(8,128)S(1)} %get-tuple-element.6.own), channel_id=1, source_target_pairs={{1,0},{2,1},{3,2},{4,3},{5,4},{6,5},{7,6},{8,7},{9,8},{10,9},{11,1... | collective-permute-start | bytes 276488 | tf_op jit(solution)/shard_map/ppermute | solution.py:26
  108.8 10.7 %collective-permute-start.2 = (f32[3,6,5,256]{3,2,1,0:T(8,128)S(1)}, f32[3,6,5,256]{3,2,1,0:T(8,128)S(1)}, u32[]{:S(2)}, u32[]{:S(2)}) collective-permute-start(f32[3,6,5,256]{3,2,1,0:T(8,128)S(1)} %get-tuple-element.6.own), channel_id=1, source_target_pairs={{0,1},{1,2},{2,3},{3,4},{4,5},{5,6},{6,7},{7,8},{8,9},{9,10},{10,1... | collective-permute-start | bytes 276488 | tf_op jit(solution)/shard_map/ppermute | solution.py:26

commit v6 on v5

--- a/solution.py
+++ b/solution.py
@@ -10,6 +10,7 @@
 
 
 ALL_AXES = ("gx", "gy", "gz_0", "gz_1")
+PLANE = ("gx", "gz_0", "gz_1")
 UNROLL = 4
 BF16 = jnp.bfloat16
 F32 = jnp.float32
@@ -215,11 +216,34 @@
     lax.fori_loop(0, steps, remap, 0)
 
 
-def fold_kernel(a, out):
-    total = a[0]
-    for s in range(1, a.shape[0]):
-        total = total + a[s]
-    out[...] = total
+def fold_kernel(a, out, parts, sums, in_sems, out_sems, *, sources, chunk):
+    kept = out.shape[0]
+    chunks = kept // chunk
+    copies = [
+        [
+            pltpu.make_async_copy(
+                a.at[pl.ds(s * kept + j * chunk, chunk)], parts.at[pl.ds(s * kept + j * chunk, chunk)], in_sems.at[j, s]
+            )
+            for s in range(sources)
+        ]
+        for j in range(chunks)
+    ]
+    for row in copies:
+        for copy in row:
+            copy.start()
+    outs = []
+    for j in range(chunks):
+        for copy in copies[j]:
+            copy.wait()
+        at = j * chunk
+        total = parts[at:at + chunk]
+        for s in range(1, sources):
+            total = total + parts[s * kept + at:s * kept + at + chunk]
+        sums[at:at + chunk] = total
+        outs.append(pltpu.make_async_copy(sums.at[pl.ds(at, chunk)], out.at[pl.ds(at, chunk)], out_sems.at[j]))
+        outs[-1].start()
+    for copy in outs:
+        copy.wait()
 
 
 def gather_kernel(a, new_data, faces, *, count, fields, edge):
@@ -314,7 +338,7 @@
             mass_kernel, patches=patches, fields=fields, edge=edge, size_y=size_y,
             size_z=chips_y * cores, new_count=count, pairs=pairs,
         ),
-        out_shape=jax.ShapeDtypeStruct((size_x * chips_y, 8, half), F32),
+        out_shape=jax.ShapeDtypeStruct((size_x * chips_y * cores, 8, half), F32),
         in_specs=[smem, smem, hbm, hbm],
         out_specs=vmem,
         scratch_shapes=[
@@ -326,7 +350,7 @@
         compiler_params=params,
         name="mass",
     )(place, meta, slow(new_ratio), slow(own))
-    plane = lax.all_to_all(mass, ("gx", "gz_0"), 0, 0, tiled=True)
+    plane = lax.all_to_all(mass, PLANE, 0, 0, tiled=True)
     partials = pl.pallas_call(
         functools.partial(
             partials_kernel, patches=patches, fields=fields, edge=edge, size_x=size_x,
@@ -351,18 +375,29 @@
     first_groups, last_groups = mixed_groups(size_x, size_y, chips_y, cores)
     first = lax.all_to_all(partials, ALL_AXES, 0, 0, tiled=True, axis_index_groups=first_groups)
     total = jnp.sum(plane, axis=0)
-    total = lax.psum(total, "gy")
-    total = total + lax.ppermute(total, "gz_1", swap)
+
+    def crossed(value, distance):
+        return value + lax.ppermute(value, "gy", [(i, i ^ distance) for i in range(size_y)])
+
+    total = crossed(total, 8)
+    total = crossed(total, 4)
+    total = crossed(total, 2)
+    total = crossed(total, 1)
     kept = owners // size_x
     folded = pl.pallas_call(
-        fold_kernel,
-        out_shape=jax.ShapeDtypeStruct((kept, rows, lanes), F32),
-        grid=(kept // count,),
-        in_specs=[pl.BlockSpec((size_x, count, rows, lanes), lambda i: (0, i, 0, 0))],
-        out_specs=pl.BlockSpec((count, rows, lanes), lambda i: (i, 0, 0)),
+        functools.partial(fold_kernel, sources=size_x, chunk=count),
+        out_shape=HBM((kept, rows, lanes), F32),
+        in_specs=[hbm],
+        out_specs=hbm,
+        scratch_shapes=[
+            pltpu.VMEM((owners, rows, lanes), F32),
+            pltpu.VMEM((kept, rows, lanes), F32),
+            DMA((kept // count, size_x)),
+            DMA((kept // count,)),
+        ],
         compiler_params=params,
         name="fold",
-    )(first.reshape(size_x, kept, rows, lanes))
+    )(slow(first))
     last = lax.all_to_all(folded, ALL_AXES, 0, 0, tiled=True, axis_index_groups=last_groups)
     new_data, faces = pl.pallas_call(
         functools.partial(gather_kernel, count=count, fields=fields, edge=edge),

time: 122 us -> 122 us (level)
  blocking collectives: 33.9 us -> 0 us
  starting transfers between devices: 31.5 us -> 54.9 us
  waiting for transfers between devices: 34.4 us -> 46.1 us
    psum x1 -> x0, blocking collectives: 33.9 us -> none  [body(): total = lax.psum(total, 'gy')]
    ppermute x1 -> x4, starting transfers between devices: 1.91 us -> 24.7 us  [crossed(): lax.ppermute(value, 'gy', [(i, i ^ distance) for i in range(size_y)])]
    ppermute x1 -> x4, waiting for transfers between devices: 1.13 us -> 10.7 us  [crossed(): lax.ppermute(value, 'gy', [(i, i ^ distance) for i in range(size_y)])]
  transfers between devices with their start and end apart: 8 -> 11, of which waited for: 6 -> 9; matrix products, arithmetic and copies ran while one was open for 1% -> 1% of each run, Pallas kernels for 6% -> 5%
where the time goes in v6:
time: 122 us
  starting transfers between devices  54.9 us (45%)
  waiting for transfers between devices  46.1 us (38%)
  Pallas kernels  18.2 us (15%)
    ppermute x4, starting transfers between devices, crossed(): lax.ppermute(value, 'gy', [(i, i ^ distance) for i in range(size_y)])  24.7 us
    all_to_all x1, waiting for transfers between devices, body(): lax.all_to_all(partials, ALL_AXES, 0, 0, tiled=True, axis_index_groups=fi...  22 us
    ppermute x4, waiting for transfers between devices, crossed(): lax.ppermute(value, 'gy', [(i, i ^ distance) for i in range(size_y)])  10.7 us
    all_to_all x1, starting transfers between devices, body(): lax.all_to_all(partials, ALL_AXES, 0, 0, tiled=True, axis_index_groups=fi...  10.1 us
    pallas_call x1, Pallas kernels, body(): pl.pallas_call(functools.partial(partials_kernel, patches=patches, fields...  9.84 us
    ppermute x2, waiting for transfers between devices, shifted(): return lax.ppermute(block, axis, route)  9.12 us
    ppermute x2, starting transfers between devices, shifted(): return lax.ppermute(block, axis, route)  7.25 us
    all_to_all x1, starting transfers between devices, body(): plane = lax.all_to_all(mass, PLANE, 0, 0, tiled=True)  5.02 us
  transfers between devices with their start and end apart: 11, of which 9 were waited for; matrix products, arithmetic and copies ran while one was open for 1% of the time, Pallas kernels for 5%

profile of v6, /device:TPU:2, one launch (start us, length us, event | category | flops | bytes accessed | tf_op | source)
XLA Modules:
  0.0 121.5 jit_solution(2428021301633931596)
XLA Ops:
  0.6 1.9 %collective-permute-start.1 = (f32[12,80,256]{2,1,0:T(8,128)}, f32[12,80,256]{2,1,0:T(8,128)S(1)}, u32[]{:S(2)}, u32[]{:S(2)}) collective-permute-start(f32[12,80,256]{2,1,0:T(8,128)} %bitcast.13), channel_id=1, source_target_pairs={{0,1},{1,0},{2,3},{3,2},{4,5},{5,4},{6,7},{7,6},{8,9},{9,8},{10,11... | collective-permute-start | bytes 2949128 | tf_op jit(solution)/shard_map/ppermute | solution.py:330
  2.6 0.7 pad_add_fusion.meta_own.meta
  3.3 2.4 %collective-permute-start = (s32[6,32]{1,0:T(8,128)S(1)}, s32[6,32]{1,0:T(8,128)S(1)}, u32[]{:S(2)}, u32[]{:S(2)}) collective-permute-start(s32[6,32]{1,0:T(8,128)S(1)} %pad_add_fusion.meta_own.meta), channel_id=1, source_target_pairs={{0,1},{1,0},{2,3},{3,2},{4,5},{5,4},{6,7},{7,6},{8,9},{9,8},{10,11... | collective-permute-start | bytes 2312 | tf_op jit(solution)/shard_map/ppermute | solution.py:329
  5.7 0.1 stack.23.place
  5.8 0.0 copy-start
  5.8 0.7 collective-permute-done.meta_peer
  6.5 0.0 collective-permute-done.1.peer
  6.5 9.8 %partials.1 = f32[48,80,256]{2,1,0:T(8,128)} custom-call(s32[5]{0:T(128)S(1)} %stack.23.place, s32[6,32]{1,0:T(8,128)S(1)} %pad_add_fusion.meta_own.meta, s32[6,32]{1,0:T(8,128)S(1)} %collective-permute-done.meta_peer, s32[1536]{0:T(1024)} %ratio_in.3, f32[12,80,256]{2,1,0:T(8,128)} %bitcast.14, f32[12,80,256]{2,1,0:T(8,128)S(1)} %collective-permute-done.1.peer), custom_call_target="tpu_custom_call" | custom-call | tf_op jit(solution)/shard_map/partials/pallas_call | solution.py:354
  16.3 10.1 %all-to-all-start = ((f32[48,80,256]{2,1,0:T(8,128)}), f32[48,80,256]{2,1,0:T(8,128)}, u32[]{:S(2)}, u32[]{:S(2)}) async-start(f32[48,80,256]{2,1,0:T(8,128)} %partials.1), calls=%async_computation | async-start | bytes 7864320 | tf_op jit(solution)/shard_map/all_to_all | solution.py:376
  26.5 0.0 copy-done
  26.5 2.9 %mass.1 = f32[32,8,128]{2,1,0:T(8,128)} custom-call(s32[5]{0:T(128)S(1)} %stack.23.place, s32[6,32]{1,0:T(8,128)S(1)} %pad_add_fusion.meta_own.meta, s32[1536]{0:T(1024)} %ratio_in.3, f32[12,80,256]{2,1,0:T(8,128)} %bitcast.15), custom_call_target="tpu_custom_call" | custom-call | tf_op jit(solution)/shard_map/mass/pallas_call | solution.py:336
  29.4 22.0 %all-to-all-done.a = f32[48,80,256]{2,1,0:T(8,128)} async-done(((f32[48,80,256]{2,1,0:T(8,128)}), f32[48,80,256]{2,1,0:T(8,128)}, u32[]{:S(2)}, u32[]{:S(2)}) %all-to-all-start) | async-done | bytes 3932192 | tf_op jit(solution)/shard_map/all_to_all | solution.py:376
  51.5 5.0 %all-to-all-start.2 = ((f32[32,8,128]{2,1,0:T(8,128)}), f32[32,8,128]{2,1,0:T(8,128)S(1)}, u32[]{:S(2)}, u32[]{:S(2)}) async-start(f32[32,8,128]{2,1,0:T(8,128)} %mass.1), calls=%async_computation.2 | async-start | bytes 262144 | tf_op jit(solution)/shard_map/all_to_all | solution.py:353
  56.5 3.1 %fold.1 = f32[12,80,256]{2,1,0:T(8,128)} custom-call(f32[48,80,256]{2,1,0:T(8,128)} %all-to-all-done.a), custom_call_target="tpu_custom_call" | custom-call | tf_op jit(solution)/shard_map/fold/pallas_call | solution.py:387
  59.6 3.6 %all-to-all-done.2 = f32[32,8,128]{2,1,0:T(8,128)S(1)} async-done(((f32[32,8,128]{2,1,0:T(8,128)}), f32[32,8,128]{2,1,0:T(8,128)S(1)}, u32[]{:S(2)}, u32[]{:S(2)}) %all-to-all-start.2) | async-done | bytes 131104 | tf_op jit(solution)/shard_map/all_to_all | solution.py:353
  63.2 3.5 %all-to-all-start.1 = ((f32[12,80,256]{2,1,0:T(8,128)}), f32[12,80,256]{2,1,0:T(8,128)S(1)}, u32[]{:S(2)}, u32[]{:S(2)}) async-start(f32[12,80,256]{2,1,0:T(8,128)} %fold.1), calls=%async_computation.1 | async-start | bytes 1966080 | tf_op jit(solution)/shard_map/all_to_all | solution.py:401
  66.7 12.5 %collective-permute-start.4 = (f32[8,128]{1,0:T(8,128)S(1)}, f32[8,128]{1,0:T(8,128)S(1)}, u32[]{:S(2)}, u32[]{:S(2)}) collective-permute-start(f32[8,128]{1,0:T(8,128)S(1)} %reduce_sum.9), channel_id=1, source_target_pairs={{0,64},{8,72},{16,80},{24,88},{32,96},{40,104},{48,112},{56,120},{... | collective-permute-start | bytes 12296 | tf_op jit(solution)/shard_map/ppermute | solution.py:380
  79.2 1.7 %collective-permute-done.4 = f32[8,128]{1,0:T(8,128)S(1)} collective-permute-done((f32[8,128]{1,0:T(8,128)S(1)}, f32[8,128]{1,0:T(8,128)S(1)}, u32[]{:S(2)}, u32[]{:S(2)}) %collective-permute-start.4) | collective-permute-done | bytes 4128 | tf_op jit(solution)/shard_map/ppermute | solution.py:380
  80.9 5.9 %collective-permute-start.5 = (f32[8,128]{1,0:T(8,128)S(1)}, f32[8,128]{1,0:T(8,128)S(1)}, u32[]{:S(2)}, u32[]{:S(2)}) collective-permute-start(f32[8,128]{1,0:T(8,128)S(1)} %add.24), channel_id=1, source_target_pairs={{0,32},{8,40},{16,48},{24,56},{32,0},{40,8},{48,16},{56,24},{64,96... | collective-permute-start | bytes 12296 | tf_op jit(solution)/shard_map/ppermute | solution.py:380
  86.8 3.5 %collective-permute-done.5 = f32[8,128]{1,0:T(8,128)S(1)} collective-permute-done((f32[8,128]{1,0:T(8,128)S(1)}, f32[8,128]{1,0:T(8,128)S(1)}, u32[]{:S(2)}, u32[]{:S(2)}) %collective-permute-start.5) | collective-permute-done | bytes 4128 | tf_op jit(solution)/shard_map/ppermute | solution.py:380
  90.3 3.6 %collective-permute-start.6 = (f32[8,128]{1,0:T(8,128)S(1)}, f32[8,128]{1,0:T(8,128)S(1)}, u32[]{:S(2)}, u32[]{:S(2)}) collective-permute-start(f32[8,128]{1,0:T(8,128)S(1)} %add.25), channel_id=1, source_target_pairs={{0,16},{8,24},{16,0},{24,8},{32,48},{40,56},{48,32},{56,40},{64,80... | collective-permute-start | bytes 12296 | tf_op jit(solution)/shard_map/ppermute | solution.py:380
  93.9 2.8 %collective-permute-done.6 = f32[8,128]{1,0:T(8,128)S(1)} collective-permute-done((f32[8,128]{1,0:T(8,128)S(1)}, f32[8,128]{1,0:T(8,128)S(1)}, u32[]{:S(2)}, u32[]{:S(2)}) %collective-permute-start.6) | collective-permute-done | bytes 4128 | tf_op jit(solution)/shard_map/ppermute | solution.py:380
  96.7 2.8 %collective-permute-start.7 = (f32[8,128]{1,0:T(8,128)S(1)}, f32[8,128]{1,0:T(8,128)S(1)}, u32[]{:S(2)}, u32[]{:S(2)}) collective-permute-start(f32[8,128]{1,0:T(8,128)S(1)} %add.26), channel_id=1, source_target_pairs={{0,8},{8,0},{16,24},{24,16},{32,40},{40,32},{48,56},{56,48},{64,72... | collective-permute-start | bytes 12296 | tf_op jit(solution)/shard_map/ppermute | solution.py:380
  99.6 2.7 %collective-permute-done.7 = f32[8,128]{1,0:T(8,128)S(1)} collective-permute-done((f32[8,128]{1,0:T(8,128)S(1)}, f32[8,128]{1,0:T(8,128)S(1)}, u32[]{:S(2)}, u32[]{:S(2)}) %collective-permute-start.7) | collective-permute-done | bytes 4128 | tf_op jit(solution)/shard_map/ppermute | solution.py:380
  102.2 0.0 all-to-all-done.1.a
  102.2 0.8 gather.1
  103.0 5.3 %collective-permute-start.3 = (f32[3,6,5,256]{3,2,1,0:T(8,128)S(1)}, f32[3,6,5,256]{3,2,1,0:T(8,128)S(1)}, u32[]{:S(2)}, u32[]{:S(2)}) collective-permute-start(f32[3,6,5,256]{3,2,1,0:T(8,128)S(1)} %get-tuple-element.6.own), channel_id=1, source_target_pairs={{1,0},{2,1},{3,2},{4,3},{5,4},{6,5},{7,6},{8,7},{9,8},{10,9},{11,1... | collective-permute-start | bytes 276488 | tf_op jit(solution)/shard_map/ppermute | solution.py:27
  108.3 1.9 %collective-permute-start.2 = (f32[3,6,5,256]{3,2,1,0:T(8,128)S(1)}, f32[3,6,5,256]{3,2,1,0:T(8,128)S(1)}, u32[]{:S(2)}, u32[]{:S(2)}) collective-permute-start(f32[3,6,5,256]{3,2,1,0:T(8,128)S(1)} %get-tuple-element.6.own), channel_id=1, source_target_pairs={{0,1},{1,2},{2,3},{3,4},{4,5},{5,6},{6,7},{7,8},{8,9},{9,10},{10,1... | collective-permute-start | bytes 276488 | tf_op jit(solution)/shard_map/ppermute | solution.py:27
  110.3 0.6 copy.11
  110.9 0.1 collective-permute-done.3.after
  111.0 9.1 %collective-permute-done.2.before = f32[3,6,5,256]{3,2,1,0:T(8,128)S(1)} collective-permute-done((f32[3,6,5,256]{3,2,1,0:T(8,128)S(1)}, f32[3,6,5,256]{3,2,1,0:T(8,128)S(1)}, u32[]{:S(2)}, u32[]{:S(2)}) %collective-permute-start.2) | collective-permute-done | bytes 92192 | tf_op jit(solution)/shard_map/ppermute | solution.py:27
  120.0 1.5 %jump.1 = f32[3,5,6,256]{3,2,1,0:T(8,128)} custom-call(s32[5]{0:T(128)} %copy-done, s32[3,6]{1,0:T(4,128)} %side.1, s32[3,6]{1,0:T(4,128)} %patch.1, f32[3,6,5,256]{3,2,1,0:T(8,128)S(1)} %get-tuple-element.6.own, f32[3,6,5,256]{3,2,1,0:T(8,128)S(1)} %collective-permute-done.2.before, f32[3,6,5,256]{3,2,1,0:T(8,128)S(1)} %collective-permute-done.3.after), custom_call_target="tpu_custom_call" | custom-call | tf_op jit(solution)/shard_map/jump/pallas_call | solution.py:415
  (6 shorter events, 0.1 us)
Async XLA Ops:
  0.6 5.9 %collective-permute-start.1 = (f32[12,80,256]{2,1,0:T(8,128)}, f32[12,80,256]{2,1,0:T(8,128)S(1)}, u32[]{:S(2)}, u32[]{:S(2)}) collective-permute-start(f32[12,80,256]{2,1,0:T(8,128)} %bitcast.13), channel_id=1, source_target_pairs={{0,1},{1,0},{2,3},{3,2},{4,5},{5,4},{6,7},{7,6},{8,9},{9,8},{10,11... | collective-permute-start | bytes 2949128 | tf_op jit(solution)/shard_map/ppermute | solution.py:330
  3.3 3.2 %collective-permute-start = (s32[6,32]{1,0:T(8,128)S(1)}, s32[6,32]{1,0:T(8,128)S(1)}, u32[]{:S(2)}, u32[]{:S(2)}) collective-permute-start(s32[6,32]{1,0:T(8,128)S(1)} %pad_add_fusion.meta_own.meta), channel_id=1, source_target_pairs={{0,1},{1,0},{2,3},{3,2},{4,5},{5,4},{6,7},{7,6},{8,9},{9,8},{10,11... | collective-permute-start | bytes 2312 | tf_op jit(solution)/shard_map/ppermute | solution.py:329
  5.8 20.7 %copy-start = (s32[5]{0:T(128)}, s32[5]{0:T(128)S(1)}, u32[]{:S(2)}) copy-start(s32[5]{0:T(128)S(1)} %stack.23.place) | copy-start | bytes 64
  16.3 35.1 %all-to-all-start = ((f32[48,80,256]{2,1,0:T(8,128)}), f32[48,80,256]{2,1,0:T(8,128)}, u32[]{:S(2)}, u32[]{:S(2)}) async-start(f32[48,80,256]{2,1,0:T(8,128)} %partials.1), calls=%async_computation | async-start | bytes 7864320 | tf_op jit(solution)/shard_map/all_to_all | solution.py:376
  51.5 11.7 %all-to-all-start.2 = ((f32[32,8,128]{2,1,0:T(8,128)}), f32[32,8,128]{2,1,0:T(8,128)S(1)}, u32[]{:S(2)}, u32[]{:S(2)}) async-start(f32[32,8,128]{2,1,0:T(8,128)} %mass.1), calls=%async_computation.2 | async-start | bytes 262144 | tf_op jit(solution)/shard_map/all_to_all | solution.py:353
  63.2 39.1 %all-to-all-start.1 = ((f32[12,80,256]{2,1,0:T(8,128)}), f32[12,80,256]{2,1,0:T(8,128)S(1)}, u32[]{:S(2)}, u32[]{:S(2)}) async-start(f32[12,80,256]{2,1,0:T(8,128)} %fold.1), calls=%async_computation.1 | async-start | bytes 1966080 | tf_op jit(solution)/shard_map/all_to_all | solution.py:401
  66.7 14.2 %collective-permute-start.4 = (f32[8,128]{1,0:T(8,128)S(1)}, f32[8,128]{1,0:T(8,128)S(1)}, u32[]{:S(2)}, u32[]{:S(2)}) collective-permute-start(f32[8,128]{1,0:T(8,128)S(1)} %reduce_sum.9), channel_id=1, source_target_pairs={{0,64},{8,72},{16,80},{24,88},{32,96},{40,104},{48,112},{56,120},{... | collective-permute-start | bytes 12296 | tf_op jit(solution)/shard_map/ppermute | solution.py:380
  80.9 9.4 %collective-permute-start.5 = (f32[8,128]{1,0:T(8,128)S(1)}, f32[8,128]{1,0:T(8,128)S(1)}, u32[]{:S(2)}, u32[]{:S(2)}) collective-permute-start(f32[8,128]{1,0:T(8,128)S(1)} %add.24), channel_id=1, source_target_pairs={{0,32},{8,40},{16,48},{24,56},{32,0},{40,8},{48,16},{56,24},{64,96... | collective-permute-start | bytes 12296 | tf_op jit(solution)/shard_map/ppermute | solution.py:380
  90.3 6.4 %collective-permute-start.6 = (f32[8,128]{1,0:T(8,128)S(1)}, f32[8,128]{1,0:T(8,128)S(1)}, u32[]{:S(2)}, u32[]{:S(2)}) collective-permute-start(f32[8,128]{1,0:T(8,128)S(1)} %add.25), channel_id=1, source_target_pairs={{0,16},{8,24},{16,0},{24,8},{32,48},{40,56},{48,32},{56,40},{64,80... | collective-permute-start | bytes 12296 | tf_op jit(solution)/shard_map/ppermute | solution.py:380
  96.7 5.5 %collective-permute-start.7 = (f32[8,128]{1,0:T(8,128)S(1)}, f32[8,128]{1,0:T(8,128)S(1)}, u32[]{:S(2)}, u32[]{:S(2)}) collective-permute-start(f32[8,128]{1,0:T(8,128)S(1)} %add.26), channel_id=1, source_target_pairs={{0,8},{8,0},{16,24},{24,16},{32,40},{40,32},{48,56},{56,48},{64,72... | collective-permute-start | bytes 12296 | tf_op jit(solution)/shard_map/ppermute | solution.py:380
  103.0 8.0 %collective-permute-start.3 = (f32[3,6,5,256]{3,2,1,0:T(8,128)S(1)}, f32[3,6,5,256]{3,2,1,0:T(8,128)S(1)}, u32[]{:S(2)}, u32[]{:S(2)}) collective-permute-start(f32[3,6,5,256]{3,2,1,0:T(8,128)S(1)} %get-tuple-element.6.own), channel_id=1, source_target_pairs={{1,0},{2,1},{3,2},{4,3},{5,4},{6,5},{7,6},{8,7},{9,8},{10,9},{11,1... | collective-permute-start | bytes 276488 | tf_op jit(solution)/shard_map/ppermute | solution.py:27
  108.3 11.7 %collective-permute-start.2 = (f32[3,6,5,256]{3,2,1,0:T(8,128)S(1)}, f32[3,6,5,256]{3,2,1,0:T(8,128)S(1)}, u32[]{:S(2)}, u32[]{:S(2)}) collective-permute-start(f32[3,6,5,256]{3,2,1,0:T(8,128)S(1)} %get-tuple-element.6.own), channel_id=1, source_target_pairs={{0,1},{1,2},{2,3},{3,4},{4,5},{5,6},{6,7},{7,8},{8,9},{9,10},{10,1... | collective-permute-start | bytes 276488 | tf_op jit(solution)/shard_map/ppermute | solution.py:27

commit v7 on v6

--- a/solution.py
+++ b/solution.py
@@ -12,6 +12,7 @@
 ALL_AXES = ("gx", "gy", "gz_0", "gz_1")
 PLANE = ("gx", "gz_0", "gz_1")
 UNROLL = 4
+META_ROWS = 40
 BF16 = jnp.bfloat16
 F32 = jnp.float32
 I32 = jnp.int32
@@ -21,10 +22,10 @@
 DMA = pltpu.SemaphoreType.DMA
 
 
-def shifted(block, axis, distance):
-    devices = range(lax.axis_size(axis))
-    route = [(i - distance, i) for i in devices if i - distance in devices]
-    return lax.ppermute(block, axis, route)
+def swapped(block, first):
+    devices = lax.axis_size(ALL_AXES)
+    pairs = [(i, i + 1) for i in range(first, devices - 1, 2)]
+    return lax.ppermute(block, ALL_AXES, pairs + [(j, i) for i, j in pairs])
 
 
 def fast(block):
@@ -66,28 +67,43 @@
     return lax.broadcasted_iota(I32, shape, dim)
 
 
-def mass_kernel(place, meta, ratio_in, own_in, out, ratio, own, counts, sems, *, patches, fields, edge, size_y, size_z, new_count, pairs):
+def head_kernel(
+    place, pair_old, pair_slot, pair_shift, pair_dest, old_row, slot_row, shift_col, dest_col, ratio_in, own_in,
+    out, packed, ratio, counts, sems,
+    *, patches, fields, edge, size_y, size_z, new_count, pairs,
+):
     lanes = edge * edge
     half = lanes // 2
     index_y = place[0]
     ratio_copy = pltpu.make_async_copy(ratio_in, ratio, sems.at[0])
-    own_copy = pltpu.make_async_copy(own_in, own, sems.at[1])
+    rows = fields * edge
+    cells = patches * rows
+    own_copy = pltpu.make_async_copy(own_in, packed.at[pl.ds(0, cells)], sems.at[1])
     ratio_copy.start()
     own_copy.start()
+    lane = iota((pairs, lanes), 1)
+    shift = shift_col[...].astype(F32)
+    table = jnp.where(lane == 3, dest_col[...].astype(F32), 0.0)
+    for a in range(3):
+        table = jnp.where(lane == a, shift[:, a:a + 1], table)
+    packed[cells:cells + pairs] = table
+    packed[cells + pairs:] = jnp.zeros((META_ROWS - pairs, lanes), F32)
+    packed[cells + pairs:cells + pairs + 1, 0:pairs] = old_row[...].astype(F32)
+    packed[cells + pairs + 1:cells + pairs + 2, 0:pairs] = slot_row[...].astype(F32)
     counts[...] = jnp.zeros_like(counts)
     at_x = iota((edge, lanes), 0)
     at_y = over(iota((edge, lanes), 1), edge)
     at_z = within(iota((edge, lanes), 1), edge)
 
     def count(p, carry):
-        dest = meta[5, p]
+        dest = pair_dest[p, 0]
         owner = (over(dest, size_z) * size_y + index_y) * size_z + within(dest, size_z)
-        reach = edge * ratio[owner * new_count + meta[1, p]]
+        reach = edge * ratio[owner * new_count + pair_slot[p]]
         hit = jnp.full((edge, lanes), True)
         for a, at in enumerate((at_x, at_y, at_z)):
-            distance = at - meta[2 + a, p]
+            distance = at - pair_shift[p, a]
             hit = hit & (distance >= 0) & (distance < reach)
-        o = meta[0, p]
+        o = pair_old[p]
         counts[o] = counts[o] + jnp.where(hit, 1.0, 0.0)
         return carry
 
@@ -100,7 +116,7 @@
         olds, news = sums
         old_list, new_list = [], []
         for f in range(fields):
-            block = own[o, f * edge:(f + 1) * edge]
+            block = packed[pl.ds(o * rows + f * edge, edge)]
             scaled = block * weight
             old_list.append(olds[f] + (block[:, :half] + block[:, half:]))
             new_list.append(news[f] + (scaled[:, :half] + scaled[:, half:]))
@@ -120,8 +136,8 @@
 
 
 def partials_kernel(
-    place, meta_own, meta_peer, ratio_in, own_in, peer,
-    out, ratio, own, table, split, code_k, code_x, sems,
+    place, pair_old, pair_slot, pair_shift, pair_dest, ratio_in, own_in, peer,
+    out, ratio, own, meta_v, meta, table, split, code_k, code_x, sems,
     *, patches, fields, edge, size_x, size_y, chips_y, cores, new_count, pairs,
 ):
     rows = fields * edge
@@ -135,12 +151,16 @@
     own_copy = pltpu.make_async_copy(own_in, own, sems.at[1])
     ratio_copy.start()
     own_copy.start()
+    cells = patches * rows
+    meta_v[...] = peer[cells:cells + META_ROWS, 0:meta_v.shape[1]].astype(I32)
+    meta_copy = pltpu.make_async_copy(meta_v, meta, sems.at[2])
+    meta_copy.start()
 
     def prepare(o, carry):
         high, low = halves(own[o])
         split[o, 0:rows] = high
         split[o, rows:2 * rows] = low
-        high, low = halves(peer[o])
+        high, low = halves(peer[pl.ds(o * rows, rows)])
         split[patches + o, 0:rows] = high
         split[patches + o, rows:2 * rows] = low
         return carry
@@ -152,29 +172,36 @@
     col = iota((rows, 2 * rows), 1) % rows
     code_x[...] = (over(col, edge) - over(row, edge)) * 4096 + within(col, edge)
 
-    def enlist(p, found, meta, base):
-        dest = meta[5, p]
+    def enlist(found, base, old, slot, shift, dest):
         mine = within(dest, cores) == core
 
         @pl.when(mine)
         def _():
-            table[0, found] = base + meta[0, p]
+            table[0, found] = base + old
             iz = within(dest, size_z)
             ix = over(dest, size_z)
-            slot = meta[1, p]
             owner = (ix * size_y + index_y) * size_z + iz
             table[1, found] = ratio[owner * new_count + slot]
-            table[2, found] = meta[2, p]
-            table[3, found] = meta[3, p] * 4096 + meta[4, p]
+            table[2, found] = shift[0]
+            table[3, found] = shift[1] * 4096 + shift[2]
             chip_y = over(iz, cores)
             chip = jnp.where(core == 0, ix * chips_y + chip_y, chip_y * size_x + ix)
             table[4, found] = chip * new_count + slot
 
         return found + mine.astype(I32)
 
+    def enlist_own(p, found):
+        shift = [pair_shift[p, a] for a in range(3)]
+        return enlist(found, 0, pair_old[p], pair_slot[p], shift, pair_dest[p, 0])
+
+    def enlist_peer(p, found):
+        shift = [meta[p, a] for a in range(3)]
+        return enlist(found, patches, meta[pairs, p], meta[pairs + 1, p], shift, meta[p, 3])
+
     ratio_copy.wait()
-    found = lax.fori_loop(0, pairs, functools.partial(enlist, meta=meta_own, base=0), jnp.int32(0))
-    found = lax.fori_loop(0, pairs, functools.partial(enlist, meta=meta_peer, base=patches), found)
+    found = lax.fori_loop(0, pairs, enlist_own, jnp.int32(0))
+    meta_copy.wait()
+    found = lax.fori_loop(0, pairs, enlist_peer, found)
 
     for extra in range(UNROLL - 1):
         table[0, found + extra] = 0
@@ -285,8 +312,9 @@
                 faces[q, 2 + e, f:f + 1, :] = line
 
 
-def jump_kernel(place, side, patch, own, before, after, jump, *, count, fields, devices):
+def jump_kernel(place, side, patch, own, near, cross, jump, *, count, fields, devices):
     linear = place[2]
+    even = within(linear, 2) == 0
     for q in range(count):
         for e in range(6):
             u = side[q, e]
@@ -294,8 +322,9 @@
             at = linear + u - 1
             present = (u < 3) & (at >= 0) & (at < devices)
             other = e ^ 1
+            inside = (u == 2) == even
             ghost = jnp.where(
-                u == 0, before[n, other], jnp.where(u == 1, own[n, other], after[n, other])
+                u == 1, own[n, other], jnp.where(inside, near[n, other], cross[n, other])
             )
             line = jnp.where(present, ghost - own[q, e], 0.0)
             for f in range(fields):
@@ -321,35 +350,37 @@
     chip_y = lax.axis_index("gz_0")
     linear = ((index_x * size_y + index_y) * chips_y + chip_y) * cores + core
     place = jnp.stack([index_y, core, linear, index_x, chip_y]).astype(I32)
-    meta = jnp.concatenate(
-        [pair_old[None], pair_slot[None], pair_shift.T, pair_dest.T], axis=0
-    )
     own = old_data.reshape(patches, rows, lanes)
     swap = [(i, cores - 1 - i) for i in range(cores)]
-    peer_meta = lax.ppermute(meta, "gz_1", swap)
-    peer = lax.ppermute(own, "gz_1", swap)
     owners = size_x * chips_y * count
     smem = pl.BlockSpec(memory_space=SMEM)
     vmem = pl.BlockSpec(memory_space=VMEM)
     hbm = pl.BlockSpec(memory_space=HBM)
     params = pltpu.CompilerParams(vmem_limit_bytes=24 * 1024 * 1024)
-    mass = pl.pallas_call(
+    mass, packed = pl.pallas_call(
         functools.partial(
-            mass_kernel, patches=patches, fields=fields, edge=edge, size_y=size_y,
+            head_kernel, patches=patches, fields=fields, edge=edge, size_y=size_y,
             size_z=chips_y * cores, new_count=count, pairs=pairs,
         ),
-        out_shape=jax.ShapeDtypeStruct((size_x * chips_y * cores, 8, half), F32),
-        in_specs=[smem, smem, hbm, hbm],
-        out_specs=vmem,
+        out_shape=(
+            jax.ShapeDtypeStruct((size_x * chips_y * cores, 8, half), F32),
+            VMEM((patches * rows + META_ROWS, lanes), F32),
+        ),
+        in_specs=[smem] * 5 + [vmem] * 4 + [hbm, hbm],
+        out_specs=(vmem, vmem),
         scratch_shapes=[
             pltpu.SMEM(new_ratio.shape, I32),
-            pltpu.VMEM((patches, rows, lanes), F32),
             pltpu.VMEM((patches, edge, lanes), F32),
             DMA((2,)),
         ],
         compiler_params=params,
-        name="mass",
-    )(place, meta, slow(new_ratio), slow(own))
+        name="head",
+    )(
+        place, pair_old, pair_slot, pair_shift, pair_dest,
+        pair_old.reshape(1, pairs), pair_slot.reshape(1, pairs), pair_shift, pair_dest,
+        slow(new_ratio), slow(old_data.reshape(patches * rows, lanes)),
+    )
+    peer = lax.ppermute(packed, "gz_1", swap)
     plane = lax.all_to_all(mass, PLANE, 0, 0, tiled=True)
     partials = pl.pallas_call(
         functools.partial(
@@ -357,20 +388,22 @@
             size_y=size_y, chips_y=chips_y, cores=cores, new_count=count, pairs=pairs,
         ),
         out_shape=HBM((owners, rows, lanes), F32),
-        in_specs=[smem, smem, smem, hbm, hbm, vmem],
+        in_specs=[smem] * 5 + [hbm, hbm, vmem],
         out_specs=vmem,
         scratch_shapes=[
             pltpu.SMEM(new_ratio.shape, I32),
             pltpu.VMEM((patches, rows, lanes), F32),
+            pltpu.VMEM((META_ROWS, half), I32),
+            pltpu.SMEM((META_ROWS, half), I32),
             pltpu.SMEM((5, 2 * pairs + UNROLL), I32),
             pltpu.VMEM((2 * patches, 2 * rows, lanes), BF16),
             pltpu.VMEM((lanes, lanes), I32),
             pltpu.VMEM((rows, 2 * rows), I32),
-            DMA((2,)),
+            DMA((3,)),
         ],
         compiler_params=params,
         name="partials",
-    )(place, meta, peer_meta, slow(new_ratio), slow(own), fast(peer))
+    )(place, pair_old, pair_slot, pair_shift, pair_dest, slow(new_ratio), slow(own), fast(peer))
 
     first_groups, last_groups = mixed_groups(size_x, size_y, chips_y, cores)
     first = lax.all_to_all(partials, ALL_AXES, 0, 0, tiled=True, axis_index_groups=first_groups)
@@ -410,15 +443,15 @@
         compiler_params=params,
         name="gather",
     )(fast(last))
-    before = shifted(faces, ALL_AXES, 1)
-    after = shifted(faces, ALL_AXES, -1)
+    cross = swapped(faces, 1)
+    near = swapped(faces, 0)
     interface_jump = pl.pallas_call(
         functools.partial(jump_kernel, count=count, fields=fields, devices=devices),
         out_shape=jax.ShapeDtypeStruct((count, fields, 6, lanes), F32),
         in_specs=[smem, smem, smem, vmem, vmem, vmem],
         out_specs=vmem,
         name="jump",
-    )(place, neighbor_side, neighbor_patch, fast(faces), fast(before), fast(after))
+    )(place, neighbor_side, neighbor_patch, fast(faces), fast(near), fast(cross))
     total_cells = patches * devices * edge * lanes
     mass_totals = total[:fields, :2].T / total_cells
     return (new_data.reshape(count, fields, edge, lanes), interface_jump, mass_totals)

time: 122 us -> 122 us (level)
  blocking collectives: 0 us -> 35.8 us
  waiting for transfers between devices: 46.1 us -> 19.6 us
  starting transfers between devices: 54.9 us -> 42.4 us
  local copies, waits for them, and re-layouts: 0.74 us -> 3.55 us
    all_to_all x0 -> x1, blocking collectives: none -> 35.8 us  [body(): lax.all_to_all(partials, ALL_AXES, 0, 0, tiled=True, axis_index_groups=fi...]
    all_to_all x1 -> x0, waiting for transfers between devices: 22 us -> none  [body(): lax.all_to_all(partials, ALL_AXES, 0, 0, tiled=True, axis_index_groups=fi...]
    all_to_all x1 -> x0, starting transfers between devices: 10.1 us -> none  [body(): lax.all_to_all(partials, ALL_AXES, 0, 0, tiled=True, axis_index_groups=fi...]
    ppermute x4 -> x3, waiting for transfers between devices: 9.82 us -> 5.33 us  [the longest x2 2.74 us: swapped(): return lax.ppermute(block, ALL_AXES, pairs + [(j, i) for i, j in pairs])]
    unnamed x3 -> x9, local copies, waits for them, and re-layouts: 0.65 us -> 3.46 us
    ppermute x4 -> x3, starting transfers between devices: 11.6 us -> 9.18 us  [the longest x2 7.26 us: swapped(): return lax.ppermute(block, ALL_AXES, pairs + [(j, i) for i, j in pairs])]
  transfers between devices with their start and end apart: 11 -> 9, of which waited for: 9 -> 7; matrix products, arithmetic and copies ran while one was open for 1% -> 1% of each run, Pallas kernels for 5% -> 3%
where the time goes in v7:
time: 122 us; the launch traced here: 121 us
  starting transfers between devices  42.4 us (35%)
  blocking collectives  35.8 us (29%)
  waiting for transfers between devices  19.6 us (16%)
  Pallas kernels  18.7 us (15%)
  local copies, waits for them, and re-layouts  3.55 us (3%)
    all_to_all x1, blocking collectives, body(): lax.all_to_all(partials, ALL_AXES, 0, 0, tiled=True, axis_index_groups=fi...  35.8 us
    ppermute x4, starting transfers between devices, crossed(): lax.ppermute(value, 'gy', [(i, i ^ distance) for i in range(size_y)])  24.7 us
    ppermute x4, waiting for transfers between devices, crossed(): lax.ppermute(value, 'gy', [(i, i ^ distance) for i in range(size_y)])  10.8 us
    pallas_call x1, Pallas kernels, body(): pl.pallas_call(functools.partial(partials_kernel, patches=patches, fields...  9.9 us
    ppermute x2, starting transfers between devices, swapped(): return lax.ppermute(block, ALL_AXES, pairs + [(j, i) for i, j in pairs])  7.26 us
    all_to_all x1, starting transfers between devices, body(): plane = lax.all_to_all(mass, PLANE, 0, 0, tiled=True)  5.02 us
    all_to_all x1, waiting for transfers between devices, body(): plane = lax.all_to_all(mass, PLANE, 0, 0, tiled=True)  3.55 us
    all_to_all x1, starting transfers between devices, body(): lax.all_to_all(folded, ALL_AXES, 0, 0, tiled=True, axis_index_groups=last...  3.51 us
  transfers between devices with their start and end apart: 9, of which 7 were waited for; matrix products, arithmetic and copies ran while one was open for 1% of the time, Pallas kernels for 3%

profile of v7, /device:TPU:2, one launch (start us, length us, event | category | flops | bytes accessed | tf_op | source)
XLA Modules:
  0.0 120.9 jit_solution(13698500837728154047)
XLA Ops:
  0.6 0.8 copy.21.pair_shift.shift_col
  1.4 0.7 copy.22.pair_dest.dest_col
  2.1 0.1 stack.23.place
  2.2 0.0 copy-start
  2.2 0.0 copy-start.1
  2.2 0.7 copy-done.1
  2.9 0.0 copy-start.2
  2.9 0.7 copy-done.2
  3.5 3.4 %head.1 = (f32[32,8,128]{2,1,0:T(8,128)}, f32[1000,256]{1,0:T(8,128)S(1)}) custom-call(s32[5]{0:T(128)S(1)} %stack.23.place, s32[32]{0:T(128)S(1)} %copy-done.1, s32[32]{0:T(128)S(1)} %copy-done.2, s32[32,3]{1,0:T(8,128)S(1)} %copy.21.pair_shift.shift_col, s32[32,1]{1,0:T(8,128)S(1)} %copy.22.pair_dest.dest_col, s32[1,32]{1,0:T(1,128)S(1)} %bitcast.12, ...), custom_call_target="tpu_custom_call" | custom-call | tf_op jit(solution)/shard_map/head/pallas_call | solution.py:360
  6.9 1.9 %collective-permute-start = (f32[1000,256]{1,0:T(8,128)S(1)}, f32[1000,256]{1,0:T(8,128)S(1)}, u32[]{:S(2)}, u32[]{:S(2)}) collective-permute-start(f32[1000,256]{1,0:T(8,128)S(1)} %get-tuple-element.7), channel_id=1, source_target_pairs={{0,1},{1,0},{2,3},{3,2},{4,5},{5,4},{6,7},{7,6},{8,9},{9,8},{10,11... | collective-permute-start | bytes 3072008 | tf_op jit(solution)/shard_map/ppermute | solution.py:383
  8.9 2.6 %collective-permute-done.peer = f32[1000,256]{1,0:T(8,128)S(1)} collective-permute-done((f32[1000,256]{1,0:T(8,128)S(1)}, f32[1000,256]{1,0:T(8,128)S(1)}, u32[]{:S(2)}, u32[]{:S(2)}) %collective-permute-start) | collective-permute-done | bytes 1024032 | tf_op jit(solution)/shard_map/ppermute | solution.py:383
  11.5 9.9 %partials.1 = f32[48,80,256]{2,1,0:T(8,128)} custom-call(s32[5]{0:T(128)S(1)} %stack.23.place, s32[32]{0:T(128)S(1)} %copy-done.1, s32[32]{0:T(128)S(1)} %copy-done.2, s32[32,3]{1,0:T(8,128)S(1)} %copy.21.pair_shift.shift_col, s32[32,1]{1,0:T(8,128)S(1)} %copy.22.pair_dest.dest_col, s32[1536]{0:T(1024)} %ratio_in.3, f32[12,80,256]{2,1,0:T(8,128)} %bitcast.15, ...), custom_call_target="tpu_custom_call" | custom-call | tf_op jit(solution)/shard_map/partials/pallas_call | solution.py:385
  21.4 35.8 %all_to_all.15.a = f32[48,80,256]{2,1,0:T(8,128)} all-to-all(f32[48,80,256]{2,1,0:T(8,128)} %partials.1), channel_id=1, replica_groups={{0,128,256,384},{2,130,258,386},{4,132,260,388},{6,134,262,390},{8,136,..., dimensions={0} | all-to-all | bytes 7864320 | tf_op jit(solution)/shard_map/all_to_all | solution.py:409
  57.2 0.0 copy-done
  57.2 5.0 %all-to-all-start.2 = ((f32[32,8,128]{2,1,0:T(8,128)}), f32[32,8,128]{2,1,0:T(8,128)S(1)}, u32[]{:S(2)}, u32[]{:S(2)}) async-start(f32[32,8,128]{2,1,0:T(8,128)} %get-tuple-element.10), calls=%async_computation.2 | async-start | bytes 262144 | tf_op jit(solution)/shard_map/all_to_all | solution.py:384
  62.2 3.1 %fold.1 = f32[12,80,256]{2,1,0:T(8,128)} custom-call(f32[48,80,256]{2,1,0:T(8,128)} %all_to_all.15.a), custom_call_target="tpu_custom_call" | custom-call | tf_op jit(solution)/shard_map/fold/pallas_call | solution.py:420
  65.3 3.6 %all-to-all-done.2 = f32[32,8,128]{2,1,0:T(8,128)S(1)} async-done(((f32[32,8,128]{2,1,0:T(8,128)}), f32[32,8,128]{2,1,0:T(8,128)S(1)}, u32[]{:S(2)}, u32[]{:S(2)}) %all-to-all-start.2) | async-done | bytes 131104 | tf_op jit(solution)/shard_map/all_to_all | solution.py:384
  68.9 3.5 %all-to-all-start.1 = ((f32[12,80,256]{2,1,0:T(8,128)}), f32[12,80,256]{2,1,0:T(8,128)S(1)}, u32[]{:S(2)}, u32[]{:S(2)}) async-start(f32[12,80,256]{2,1,0:T(8,128)} %fold.1), calls=%async_computation.1 | async-start | bytes 1966080 | tf_op jit(solution)/shard_map/all_to_all | solution.py:434
  72.5 12.5 %collective-permute-start.3 = (f32[8,128]{1,0:T(8,128)S(1)}, f32[8,128]{1,0:T(8,128)S(1)}, u32[]{:S(2)}, u32[]{:S(2)}) collective-permute-start(f32[8,128]{1,0:T(8,128)S(1)} %reduce_sum.9), channel_id=1, source_target_pairs={{0,64},{8,72},{16,80},{24,88},{32,96},{40,104},{48,112},{56,120},{... | collective-permute-start | bytes 12296 | tf_op jit(solution)/shard_map/ppermute | solution.py:413
  85.0 1.7 %collective-permute-done.3 = f32[8,128]{1,0:T(8,128)S(1)} collective-permute-done((f32[8,128]{1,0:T(8,128)S(1)}, f32[8,128]{1,0:T(8,128)S(1)}, u32[]{:S(2)}, u32[]{:S(2)}) %collective-permute-start.3) | collective-permute-done | bytes 4128 | tf_op jit(solution)/shard_map/ppermute | solution.py:413
  86.7 5.9 %collective-permute-start.4 = (f32[8,128]{1,0:T(8,128)S(1)}, f32[8,128]{1,0:T(8,128)S(1)}, u32[]{:S(2)}, u32[]{:S(2)}) collective-permute-start(f32[8,128]{1,0:T(8,128)S(1)} %add.24), channel_id=1, source_target_pairs={{0,32},{8,40},{16,48},{24,56},{32,0},{40,8},{48,16},{56,24},{64,96... | collective-permute-start | bytes 12296 | tf_op jit(solution)/shard_map/ppermute | solution.py:413
  92.5 3.5 %collective-permute-done.4 = f32[8,128]{1,0:T(8,128)S(1)} collective-permute-done((f32[8,128]{1,0:T(8,128)S(1)}, f32[8,128]{1,0:T(8,128)S(1)}, u32[]{:S(2)}, u32[]{:S(2)}) %collective-permute-start.4) | collective-permute-done | bytes 4128 | tf_op jit(solution)/shard_map/ppermute | solution.py:413
  96.1 3.6 %collective-permute-start.5 = (f32[8,128]{1,0:T(8,128)S(1)}, f32[8,128]{1,0:T(8,128)S(1)}, u32[]{:S(2)}, u32[]{:S(2)}) collective-permute-start(f32[8,128]{1,0:T(8,128)S(1)} %add.25), channel_id=1, source_target_pairs={{0,16},{8,24},{16,0},{24,8},{32,48},{40,56},{48,32},{56,40},{64,80... | collective-permute-start | bytes 12296 | tf_op jit(solution)/shard_map/ppermute | solution.py:413
  99.6 2.8 %collective-permute-done.5 = f32[8,128]{1,0:T(8,128)S(1)} collective-permute-done((f32[8,128]{1,0:T(8,128)S(1)}, f32[8,128]{1,0:T(8,128)S(1)}, u32[]{:S(2)}, u32[]{:S(2)}) %collective-permute-start.5) | collective-permute-done | bytes 4128 | tf_op jit(solution)/shard_map/ppermute | solution.py:413
  102.5 2.8 %collective-permute-start.6 = (f32[8,128]{1,0:T(8,128)S(1)}, f32[8,128]{1,0:T(8,128)S(1)}, u32[]{:S(2)}, u32[]{:S(2)}) collective-permute-start(f32[8,128]{1,0:T(8,128)S(1)} %add.26), channel_id=1, source_target_pairs={{0,8},{8,0},{16,24},{24,16},{32,40},{40,32},{48,56},{56,48},{64,72... | collective-permute-start | bytes 12296 | tf_op jit(solution)/shard_map/ppermute | solution.py:413
  105.3 2.7 %collective-permute-done.6 = f32[8,128]{1,0:T(8,128)S(1)} collective-permute-done((f32[8,128]{1,0:T(8,128)S(1)}, f32[8,128]{1,0:T(8,128)S(1)}, u32[]{:S(2)}, u32[]{:S(2)}) %collective-permute-start.6) | collective-permute-done | bytes 4128 | tf_op jit(solution)/shard_map/ppermute | solution.py:413
  108.0 0.0 all-to-all-done.1.a
  108.0 0.8 gather.1
  108.7 5.3 %collective-permute-start.2 = (f32[3,6,5,256]{3,2,1,0:T(8,128)S(1)}, f32[3,6,5,256]{3,2,1,0:T(8,128)S(1)}, u32[]{:S(2)}, u32[]{:S(2)}) collective-permute-start(f32[3,6,5,256]{3,2,1,0:T(8,128)S(1)} %get-tuple-element.9.own), channel_id=1, source_target_pairs={{1,2},{3,4},{5,6},{7,8},{9,10},{11,12},{13,14},{15,16},{17,18},{19... | collective-permute-start | bytes 276488 | tf_op jit(solution)/shard_map/ppermute | solution.py:28
  114.1 1.9 %collective-permute-start.1 = (f32[3,6,5,256]{3,2,1,0:T(8,128)S(1)}, f32[3,6,5,256]{3,2,1,0:T(8,128)S(1)}, u32[]{:S(2)}, u32[]{:S(2)}) collective-permute-start(f32[3,6,5,256]{3,2,1,0:T(8,128)S(1)} %get-tuple-element.9.own), channel_id=1, source_target_pairs={{0,1},{2,3},{4,5},{6,7},{8,9},{10,11},{12,13},{14,15},{16,17},{18,... | collective-permute-start | bytes 276488 | tf_op jit(solution)/shard_map/ppermute | solution.py:28
  116.0 0.6 copy.23
  116.7 2.7 %collective-permute-done.2.cross = f32[3,6,5,256]{3,2,1,0:T(8,128)S(1)} collective-permute-done((f32[3,6,5,256]{3,2,1,0:T(8,128)S(1)}, f32[3,6,5,256]{3,2,1,0:T(8,128)S(1)}, u32[]{:S(2)}, u32[]{:S(2)}) %collective-permute-start.2) | collective-permute-done | bytes 92192 | tf_op jit(solution)/shard_map/ppermute | solution.py:28
  119.4 0.0 collective-permute-done.1.near
  119.4 1.5 %jump.1 = f32[3,5,6,256]{3,2,1,0:T(8,128)} custom-call(s32[5]{0:T(128)} %copy-done, s32[3,6]{1,0:T(4,128)} %side.1, s32[3,6]{1,0:T(4,128)} %patch.1, f32[3,6,5,256]{3,2,1,0:T(8,128)S(1)} %get-tuple-element.9.own, f32[3,6,5,256]{3,2,1,0:T(8,128)S(1)} %collective-permute-done.1.near, f32[3,6,5,256]{3,2,1,0:T(8,128)S(1)} %collective-permute-done.2.cross), custom_call_target="tpu_custom_call" | custom-call | tf_op jit(solution)/shard_map/jump/pallas_call | solution.py:448
  (6 shorter events, 0.1 us)
Async XLA Ops:
  2.2 55.0 %copy-start = (s32[5]{0:T(128)}, s32[5]{0:T(128)S(1)}, u32[]{:S(2)}) copy-start(s32[5]{0:T(128)S(1)} %stack.23.place) | copy-start | bytes 64
  2.2 0.7 copy-start.1
  2.9 0.7 copy-start.2
  6.9 4.5 %collective-permute-start = (f32[1000,256]{1,0:T(8,128)S(1)}, f32[1000,256]{1,0:T(8,128)S(1)}, u32[]{:S(2)}, u32[]{:S(2)}) collective-permute-start(f32[1000,256]{1,0:T(8,128)S(1)} %get-tuple-element.7), channel_id=1, source_target_pairs={{0,1},{1,0},{2,3},{3,2},{4,5},{5,4},{6,7},{7,6},{8,9},{9,8},{10,11... | collective-permute-start | bytes 3072008 | tf_op jit(solution)/shard_map/ppermute | solution.py:383
  57.2 11.7 %all-to-all-start.2 = ((f32[32,8,128]{2,1,0:T(8,128)}), f32[32,8,128]{2,1,0:T(8,128)S(1)}, u32[]{:S(2)}, u32[]{:S(2)}) async-start(f32[32,8,128]{2,1,0:T(8,128)} %get-tuple-element.10), calls=%async_computation.2 | async-start | bytes 262144 | tf_op jit(solution)/shard_map/all_to_all | solution.py:384
  68.9 39.1 %all-to-all-start.1 = ((f32[12,80,256]{2,1,0:T(8,128)}), f32[12,80,256]{2,1,0:T(8,128)S(1)}, u32[]{:S(2)}, u32[]{:S(2)}) async-start(f32[12,80,256]{2,1,0:T(8,128)} %fold.1), calls=%async_computation.1 | async-start | bytes 1966080 | tf_op jit(solution)/shard_map/all_to_all | solution.py:434
  72.5 14.2 %collective-permute-start.3 = (f32[8,128]{1,0:T(8,128)S(1)}, f32[8,128]{1,0:T(8,128)S(1)}, u32[]{:S(2)}, u32[]{:S(2)}) collective-permute-start(f32[8,128]{1,0:T(8,128)S(1)} %reduce_sum.9), channel_id=1, source_target_pairs={{0,64},{8,72},{16,80},{24,88},{32,96},{40,104},{48,112},{56,120},{... | collective-permute-start | bytes 12296 | tf_op jit(solution)/shard_map/ppermute | solution.py:413
  86.7 9.4 %collective-permute-start.4 = (f32[8,128]{1,0:T(8,128)S(1)}, f32[8,128]{1,0:T(8,128)S(1)}, u32[]{:S(2)}, u32[]{:S(2)}) collective-permute-start(f32[8,128]{1,0:T(8,128)S(1)} %add.24), channel_id=1, source_target_pairs={{0,32},{8,40},{16,48},{24,56},{32,0},{40,8},{48,16},{56,24},{64,96... | collective-permute-start | bytes 12296 | tf_op jit(solution)/shard_map/ppermute | solution.py:413
  96.1 6.4 %collective-permute-start.5 = (f32[8,128]{1,0:T(8,128)S(1)}, f32[8,128]{1,0:T(8,128)S(1)}, u32[]{:S(2)}, u32[]{:S(2)}) collective-permute-start(f32[8,128]{1,0:T(8,128)S(1)} %add.25), channel_id=1, source_target_pairs={{0,16},{8,24},{16,0},{24,8},{32,48},{40,56},{48,32},{56,40},{64,80... | collective-permute-start | bytes 12296 | tf_op jit(solution)/shard_map/ppermute | solution.py:413
  102.5 5.5 %collective-permute-start.6 = (f32[8,128]{1,0:T(8,128)S(1)}, f32[8,128]{1,0:T(8,128)S(1)}, u32[]{:S(2)}, u32[]{:S(2)}) collective-permute-start(f32[8,128]{1,0:T(8,128)S(1)} %add.26), channel_id=1, source_target_pairs={{0,8},{8,0},{16,24},{24,16},{32,40},{40,32},{48,56},{56,48},{64,72... | collective-permute-start | bytes 12296 | tf_op jit(solution)/shard_map/ppermute | solution.py:413
  108.7 10.7 %collective-permute-start.2 = (f32[3,6,5,256]{3,2,1,0:T(8,128)S(1)}, f32[3,6,5,256]{3,2,1,0:T(8,128)S(1)}, u32[]{:S(2)}, u32[]{:S(2)}) collective-permute-start(f32[3,6,5,256]{3,2,1,0:T(8,128)S(1)} %get-tuple-element.9.own), channel_id=1, source_target_pairs={{1,2},{3,4},{5,6},{7,8},{9,10},{11,12},{13,14},{15,16},{17,18},{19... | collective-permute-start | bytes 276488 | tf_op jit(solution)/shard_map/ppermute | solution.py:28
  114.1 5.3 %collective-permute-start.1 = (f32[3,6,5,256]{3,2,1,0:T(8,128)S(1)}, f32[3,6,5,256]{3,2,1,0:T(8,128)S(1)}, u32[]{:S(2)}, u32[]{:S(2)}) collective-permute-start(f32[3,6,5,256]{3,2,1,0:T(8,128)S(1)} %get-tuple-element.9.own), channel_id=1, source_target_pairs={{0,1},{2,3},{4,5},{6,7},{8,9},{10,11},{12,13},{14,15},{16,17},{18,... | collective-permute-start | bytes 276488 | tf_op jit(solution)/shard_map/ppermute | solution.py:28

commit v8 on v7

--- a/solution.py
+++ b/solution.py
@@ -11,8 +11,8 @@
 
 ALL_AXES = ("gx", "gy", "gz_0", "gz_1")
 PLANE = ("gx", "gz_0", "gz_1")
-UNROLL = 4
-META_ROWS = 40
+UNROLL = 8
+META_ROWS = 8
 BF16 = jnp.bfloat16
 F32 = jnp.float32
 I32 = jnp.int32
@@ -68,7 +68,7 @@
 
 
 def head_kernel(
-    place, pair_old, pair_slot, pair_shift, pair_dest, old_row, slot_row, shift_col, dest_col, ratio_in, own_in,
+    place, pair_old, pair_slot, pair_shift, pair_dest, old_row, slot_row, dest_row, shift_rows, ratio_in, own_in,
     out, packed, ratio, counts, sems,
     *, patches, fields, edge, size_y, size_z, new_count, pairs,
 ):
@@ -81,27 +81,24 @@
     own_copy = pltpu.make_async_copy(own_in, packed.at[pl.ds(0, cells)], sems.at[1])
     ratio_copy.start()
     own_copy.start()
-    lane = iota((pairs, lanes), 1)
-    shift = shift_col[...].astype(F32)
-    table = jnp.where(lane == 3, dest_col[...].astype(F32), 0.0)
-    for a in range(3):
-        table = jnp.where(lane == a, shift[:, a:a + 1], table)
-    packed[cells:cells + pairs] = table
-    packed[cells + pairs:] = jnp.zeros((META_ROWS - pairs, lanes), F32)
-    packed[cells + pairs:cells + pairs + 1, 0:pairs] = old_row[...].astype(F32)
-    packed[cells + pairs + 1:cells + pairs + 2, 0:pairs] = slot_row[...].astype(F32)
+    packed[cells:] = jnp.zeros((META_ROWS, lanes), F32)
+    at = cells
+    for rows_in in (old_row, slot_row, dest_row, shift_rows):
+        size = rows_in.shape[0]
+        packed[at:at + size, 0:pairs] = rows_in[...].astype(F32)
+        at += size
     counts[...] = jnp.zeros_like(counts)
     at_x = iota((edge, lanes), 0)
     at_y = over(iota((edge, lanes), 1), edge)
     at_z = within(iota((edge, lanes), 1), edge)
 
     def count(p, carry):
-        dest = pair_dest[p, 0]
+        dest = pair_dest[0, p]
         owner = (over(dest, size_z) * size_y + index_y) * size_z + within(dest, size_z)
         reach = edge * ratio[owner * new_count + pair_slot[p]]
         hit = jnp.full((edge, lanes), True)
         for a, at in enumerate((at_x, at_y, at_z)):
-            distance = at - pair_shift[p, a]
+            distance = at - pair_shift[a, p]
             hit = hit & (distance >= 0) & (distance < reach)
         o = pair_old[p]
         counts[o] = counts[o] + jnp.where(hit, 1.0, 0.0)
@@ -137,8 +134,8 @@
 
 def partials_kernel(
     place, pair_old, pair_slot, pair_shift, pair_dest, ratio_in, own_in, peer,
-    out, ratio, own, meta_v, meta, table, split, code_k, code_x, sems,
-    *, patches, fields, edge, size_x, size_y, chips_y, cores, new_count, pairs,
+    out, ratio, own, meta_v, meta, table, order, ends, sums, split, code_k, code_x, sems, out_sems,
+    *, patches, fields, edge, size_y, chips_y, cores, new_count, pairs,
 ):
     rows = fields * edge
     lanes = edge * edge
@@ -165,7 +162,10 @@
         split[patches + o, rows:2 * rows] = low
         return carry
 
-    out[...] = jnp.zeros_like(out)
+    sums[...] = jnp.zeros_like(sums)
+    chunks = ends.shape[0]
+    chunk_size = out.shape[0] // chunks
+    spare = out.shape[0]
     cell = iota((lanes, lanes), 0)
     code_k[...] = over(cell, edge) * 4096 + within(cell, edge)
     row = iota((rows, 2 * rows), 0)
@@ -185,30 +185,59 @@
             table[2, found] = shift[0]
             table[3, found] = shift[1] * 4096 + shift[2]
             chip_y = over(iz, cores)
-            chip = jnp.where(core == 0, ix * chips_y + chip_y, chip_y * size_x + ix)
-            table[4, found] = chip * new_count + slot
+            chunk = jnp.where(core == 0, ix, chip_y)
+            table[4, found] = (chunk * chips_y + jnp.where(core == 0, chip_y, ix)) * new_count + slot
+            rank = ends[chunk]
+            table[5, found] = chunk
+            table[6, found] = rank
+            ends[chunk] = rank + 1
 
         return found + mine.astype(I32)
 
     def enlist_own(p, found):
-        shift = [pair_shift[p, a] for a in range(3)]
-        return enlist(found, 0, pair_old[p], pair_slot[p], shift, pair_dest[p, 0])
+        shift = [pair_shift[a, p] for a in range(3)]
+        return enlist(found, 0, pair_old[p], pair_slot[p], shift, pair_dest[0, p])
 
     def enlist_peer(p, found):
-        shift = [meta[p, a] for a in range(3)]
-        return enlist(found, patches, meta[pairs, p], meta[pairs + 1, p], shift, meta[p, 3])
-
+        shift = [meta[3 + a, p] for a in range(3)]
+        return enlist(found, patches, meta[0, p], meta[1, p], shift, meta[2, p])
+
+    for k in range(chunks):
+        ends[k] = 0
     ratio_copy.wait()
     found = lax.fori_loop(0, pairs, enlist_own, jnp.int32(0))
     meta_copy.wait()
     found = lax.fori_loop(0, pairs, enlist_peer, found)
 
+    before = jnp.int32(0)
+    starts = []
+    for k in range(chunks):
+        starts.append(before)
+        before = before + ends[k]
+        ends[k] = starts[k]
+
+    def place_in_order(p, carry):
+        order[ends[table[5, p]] + table[6, p]] = p
+        return carry
+
+    lax.fori_loop(0, found, place_in_order, 0)
+    stops = starts[1:] + [found]
+    blank = table.shape[1] - 1
+    for field, value in enumerate((0, 1, 0, 0, spare)):
+        table[field, blank] = value
     for extra in range(UNROLL - 1):
-        table[0, found + extra] = 0
-        table[1, found + extra] = 1
-        table[2, found + extra] = 0
-        table[3, found + extra] = 0
-        table[4, found + extra] = 0
+        order[found + extra] = blank
+
+    def copy_out(k):
+        at = pl.ds(k * chunk_size, chunk_size)
+        return pltpu.make_async_copy(sums.at[at], out.at[at], out_sems.at[k])
+
+    def send(low, high):
+        for k in range(chunks):
+
+            @pl.when((stops[k] > low) & (stops[k] <= high))
+            def _():
+                copy_out(k).start()
 
     own_copy.wait()
     lax.fori_loop(0, patches, prepare, 0)
@@ -220,8 +249,7 @@
     def remap(step, carry):
         results = []
         for u in range(UNROLL):
-            p = step * UNROLL + u
-            live = (p < found).astype(F32)
+            p = order[step * UNROLL + u]
             r = table[1, p]
             inverse = jnp.where(r == 2, 0.5, 1.0).astype(F32)
             spread = code_x[...] - (row_x * r + table[2, p])
@@ -232,15 +260,19 @@
             high, low = halves(section)
             stacked = jnp.concatenate([high, low], axis=0)
             product = jnp.dot(stacked, weight_k, preferred_element_type=F32)
-            part = (product[:rows] + product[rows:]) * live
+            part = product[:rows] + product[rows:]
             results.append((p, part))
         for p, part in results:
             to = table[4, p]
-            out[to] = out[to] + part
+            sums[to] = sums[to] + part
+        send(step * UNROLL, (step + 1) * UNROLL)
         return carry
 
     steps = (found + UNROLL - 1) // UNROLL
+    send(-1, 0)
     lax.fori_loop(0, steps, remap, 0)
+    for k in range(chunks):
+        copy_out(k).wait()
 
 
 def fold_kernel(a, out, parts, sums, in_sems, out_sems, *, sources, chunk):
@@ -351,6 +383,7 @@
     linear = ((index_x * size_y + index_y) * chips_y + chip_y) * cores + core
     place = jnp.stack([index_y, core, linear, index_x, chip_y]).astype(I32)
     own = old_data.reshape(patches, rows, lanes)
+    table = [slow(pair_old), slow(pair_slot), slow(pair_shift.T), slow(pair_dest.T)]
     swap = [(i, cores - 1 - i) for i in range(cores)]
     owners = size_x * chips_y * count
     smem = pl.BlockSpec(memory_space=SMEM)
@@ -376,34 +409,37 @@
         compiler_params=params,
         name="head",
     )(
-        place, pair_old, pair_slot, pair_shift, pair_dest,
-        pair_old.reshape(1, pairs), pair_slot.reshape(1, pairs), pair_shift, pair_dest,
+        place, *table, slow(pair_old.reshape(1, pairs)), slow(pair_slot.reshape(1, pairs)), *table[:1:-1],
         slow(new_ratio), slow(old_data.reshape(patches * rows, lanes)),
     )
     peer = lax.ppermute(packed, "gz_1", swap)
     plane = lax.all_to_all(mass, PLANE, 0, 0, tiled=True)
     partials = pl.pallas_call(
         functools.partial(
-            partials_kernel, patches=patches, fields=fields, edge=edge, size_x=size_x,
+            partials_kernel, patches=patches, fields=fields, edge=edge,
             size_y=size_y, chips_y=chips_y, cores=cores, new_count=count, pairs=pairs,
         ),
         out_shape=HBM((owners, rows, lanes), F32),
         in_specs=[smem] * 5 + [hbm, hbm, vmem],
-        out_specs=vmem,
+        out_specs=hbm,
         scratch_shapes=[
             pltpu.SMEM(new_ratio.shape, I32),
             pltpu.VMEM((patches, rows, lanes), F32),
             pltpu.VMEM((META_ROWS, half), I32),
             pltpu.SMEM((META_ROWS, half), I32),
-            pltpu.SMEM((5, 2 * pairs + UNROLL), I32),
+            pltpu.SMEM((7, 2 * pairs + 1), I32),
+            pltpu.SMEM((2 * pairs + UNROLL,), I32),
+            pltpu.SMEM((size_x,), I32),
+            pltpu.VMEM((owners + 1, rows, lanes), F32),
             pltpu.VMEM((2 * patches, 2 * rows, lanes), BF16),
             pltpu.VMEM((lanes, lanes), I32),
             pltpu.VMEM((rows, 2 * rows), I32),
             DMA((3,)),
+            DMA((size_x,)),
         ],
         compiler_params=params,
         name="partials",
-    )(place, pair_old, pair_slot, pair_shift, pair_dest, slow(new_ratio), slow(own), fast(peer))
+    )(place, *table, slow(new_ratio), slow(own), fast(peer))
 
     first_groups, last_groups = mixed_groups(size_x, size_y, chips_y, cores)
     first = lax.all_to_all(partials, ALL_AXES, 0, 0, tiled=True, axis_index_groups=first_groups)

time: 122 us -> 117 us (0.959)
  local copies, waits for them, and re-layouts: 3.55 us -> 0.74 us
    unnamed x9 -> x3, local copies, waits for them, and re-layouts: 3.46 us -> 0.65 us
where the time goes in v8:
time: 117 us
  starting transfers between devices  42.6 us (36%)
  blocking collectives  35.4 us (30%)
  waiting for transfers between devices  19.6 us (17%)
  Pallas kernels  17.7 us (15%)
    all_to_all x1, blocking collectives, body(): lax.all_to_all(partials, ALL_AXES, 0, 0, tiled=True, axis_index_groups=fi...  35.4 us
    ppermute x4, starting transfers between devices, crossed(): lax.ppermute(value, 'gy', [(i, i ^ distance) for i in range(size_y)])  25.2 us
    ppermute x4, waiting for transfers between devices, crossed(): lax.ppermute(value, 'gy', [(i, i ^ distance) for i in range(size_y)])  10.5 us
    pallas_call x1, Pallas kernels, body(): pl.pallas_call(functools.partial(partials_kernel, patches=patches, fields...  9.1 us
    ppermute x2, starting transfers between devices, swapped(): return lax.ppermute(block, ALL_AXES, pairs + [(j, i) for i, j in pairs])  6.93 us
    all_to_all x1, starting transfers between devices, body(): plane = lax.all_to_all(mass, PLANE, 0, 0, tiled=True)  5.02 us
    all_to_all x1, waiting for transfers between devices, body(): plane = lax.all_to_all(mass, PLANE, 0, 0, tiled=True)  3.53 us
    all_to_all x1, starting transfers between devices, body(): lax.all_to_all(folded, ALL_AXES, 0, 0, tiled=True, axis_index_groups=last...  3.51 us
  transfers between devices with their start and end apart: 9, of which 7 were waited for; matrix products, arithmetic and copies ran while one was open for 1% of the time, Pallas kernels for 3%

profile of v8, /device:TPU:2, one launch (start us, length us, event | category | flops | bytes accessed | tf_op | source)
XLA Modules:
  0.0 116.8 jit_solution(12648345435444839496)
XLA Ops:
  0.6 0.1 stack.23.place
  0.7 0.0 copy-start
  0.7 3.2 %head.1 = (f32[32,8,128]{2,1,0:T(8,128)}, f32[968,256]{1,0:T(8,128)S(1)}) custom-call(s32[5]{0:T(128)S(1)} %stack.23.place, s32[32]{0:T(128)} %pair_old.3, s32[32]{0:T(128)} %pair_slot.3, s32[3,32]{1,0:T(4,128)} %bitcast.16, s32[1,32]{1,0:T(1,128)} %bitcast.21, s32[1,32]{1,0:T(1,128)} %bitcast.19, s32[1,32]{1,0:T(1,128)} %bitcast.20, s32[1,32]{1,0:T(1,128)} %bitcast.22, ...), custom_call_target="tpu_custom_call" | custom-call | tf_op jit(solution)/shard_map/head/pallas_call | solution.py:393
  3.9 1.9 %collective-permute-start = (f32[968,256]{1,0:T(8,128)S(1)}, f32[968,256]{1,0:T(8,128)S(1)}, u32[]{:S(2)}, u32[]{:S(2)}) collective-permute-start(f32[968,256]{1,0:T(8,128)S(1)} %get-tuple-element.7), channel_id=1, source_target_pairs={{0,1},{1,0},{2,3},{3,2},{4,5},{5,4},{6,7},{7,6},{8,9},{9,8},{10,11... | collective-permute-start | bytes 2973704 | tf_op jit(solution)/shard_map/ppermute | solution.py:415
  5.8 2.5 %collective-permute-done.peer = f32[968,256]{1,0:T(8,128)S(1)} collective-permute-done((f32[968,256]{1,0:T(8,128)S(1)}, f32[968,256]{1,0:T(8,128)S(1)}, u32[]{:S(2)}, u32[]{:S(2)}) %collective-permute-start) | collective-permute-done | bytes 991264 | tf_op jit(solution)/shard_map/ppermute | solution.py:415
  8.4 9.1 %partials.1 = f32[48,80,256]{2,1,0:T(8,128)} custom-call(s32[5]{0:T(128)S(1)} %stack.23.place, s32[32]{0:T(128)} %pair_old.3, s32[32]{0:T(128)} %pair_slot.3, s32[3,32]{1,0:T(4,128)} %bitcast.18, s32[1,32]{1,0:T(1,128)} %bitcast.23, s32[1536]{0:T(1024)} %ratio_in.3, f32[12,80,256]{2,1,0:T(8,128)} %bitcast.15, f32[968,256]{1,0:T(8,128)S(1)} %collective-permute-done.peer), custom_call_target="tpu_custom_call" | custom-call | tf_op jit(solution)/shard_map/partials/pallas_call | solution.py:417
  17.5 35.4 %all_to_all.15.a = f32[48,80,256]{2,1,0:T(8,128)} all-to-all(f32[48,80,256]{2,1,0:T(8,128)} %partials.1), channel_id=1, replica_groups={{0,128,256,384},{2,130,258,386},{4,132,260,388},{6,134,262,390},{8,136,..., dimensions={0} | all-to-all | bytes 7864320 | tf_op jit(solution)/shard_map/all_to_all | solution.py:445
  52.9 0.0 copy-done
  52.9 5.0 %all-to-all-start.2 = ((f32[32,8,128]{2,1,0:T(8,128)}), f32[32,8,128]{2,1,0:T(8,128)S(1)}, u32[]{:S(2)}, u32[]{:S(2)}) async-start(f32[32,8,128]{2,1,0:T(8,128)} %get-tuple-element.10), calls=%async_computation.2 | async-start | bytes 262144 | tf_op jit(solution)/shard_map/all_to_all | solution.py:416
  57.9 3.1 %fold.1 = f32[12,80,256]{2,1,0:T(8,128)} custom-call(f32[48,80,256]{2,1,0:T(8,128)} %all_to_all.15.a), custom_call_target="tpu_custom_call" | custom-call | tf_op jit(solution)/shard_map/fold/pallas_call | solution.py:456
  61.0 3.5 %all-to-all-done.2 = f32[32,8,128]{2,1,0:T(8,128)S(1)} async-done(((f32[32,8,128]{2,1,0:T(8,128)}), f32[32,8,128]{2,1,0:T(8,128)S(1)}, u32[]{:S(2)}, u32[]{:S(2)}) %all-to-all-start.2) | async-done | bytes 131104 | tf_op jit(solution)/shard_map/all_to_all | solution.py:416
  64.6 3.5 %all-to-all-start.1 = ((f32[12,80,256]{2,1,0:T(8,128)}), f32[12,80,256]{2,1,0:T(8,128)S(1)}, u32[]{:S(2)}, u32[]{:S(2)}) async-start(f32[12,80,256]{2,1,0:T(8,128)} %fold.1), calls=%async_computation.1 | async-start | bytes 1966080 | tf_op jit(solution)/shard_map/all_to_all | solution.py:470
  68.1 12.9 %collective-permute-start.3 = (f32[8,128]{1,0:T(8,128)S(1)}, f32[8,128]{1,0:T(8,128)S(1)}, u32[]{:S(2)}, u32[]{:S(2)}) collective-permute-start(f32[8,128]{1,0:T(8,128)S(1)} %reduce_sum.9), channel_id=1, source_target_pairs={{0,64},{8,72},{16,80},{24,88},{32,96},{40,104},{48,112},{56,120},{... | collective-permute-start | bytes 12296 | tf_op jit(solution)/shard_map/ppermute | solution.py:449
  81.0 1.6 %collective-permute-done.3 = f32[8,128]{1,0:T(8,128)S(1)} collective-permute-done((f32[8,128]{1,0:T(8,128)S(1)}, f32[8,128]{1,0:T(8,128)S(1)}, u32[]{:S(2)}, u32[]{:S(2)}) %collective-permute-start.3) | collective-permute-done | bytes 4128 | tf_op jit(solution)/shard_map/ppermute | solution.py:449
  82.6 6.0 %collective-permute-start.4 = (f32[8,128]{1,0:T(8,128)S(1)}, f32[8,128]{1,0:T(8,128)S(1)}, u32[]{:S(2)}, u32[]{:S(2)}) collective-permute-start(f32[8,128]{1,0:T(8,128)S(1)} %add.24), channel_id=1, source_target_pairs={{0,32},{8,40},{16,48},{24,56},{32,0},{40,8},{48,16},{56,24},{64,96... | collective-permute-start | bytes 12296 | tf_op jit(solution)/shard_map/ppermute | solution.py:449
  88.6 3.4 %collective-permute-done.4 = f32[8,128]{1,0:T(8,128)S(1)} collective-permute-done((f32[8,128]{1,0:T(8,128)S(1)}, f32[8,128]{1,0:T(8,128)S(1)}, u32[]{:S(2)}, u32[]{:S(2)}) %collective-permute-start.4) | collective-permute-done | bytes 4128 | tf_op jit(solution)/shard_map/ppermute | solution.py:449
  92.0 3.4 %collective-permute-start.5 = (f32[8,128]{1,0:T(8,128)S(1)}, f32[8,128]{1,0:T(8,128)S(1)}, u32[]{:S(2)}, u32[]{:S(2)}) collective-permute-start(f32[8,128]{1,0:T(8,128)S(1)} %add.25), channel_id=1, source_target_pairs={{0,16},{8,24},{16,0},{24,8},{32,48},{40,56},{48,32},{56,40},{64,80... | collective-permute-start | bytes 12296 | tf_op jit(solution)/shard_map/ppermute | solution.py:449
  95.4 3.0 %collective-permute-done.5 = f32[8,128]{1,0:T(8,128)S(1)} collective-permute-done((f32[8,128]{1,0:T(8,128)S(1)}, f32[8,128]{1,0:T(8,128)S(1)}, u32[]{:S(2)}, u32[]{:S(2)}) %collective-permute-start.5) | collective-permute-done | bytes 4128 | tf_op jit(solution)/shard_map/ppermute | solution.py:449
  98.4 2.9 %collective-permute-start.6 = (f32[8,128]{1,0:T(8,128)S(1)}, f32[8,128]{1,0:T(8,128)S(1)}, u32[]{:S(2)}, u32[]{:S(2)}) collective-permute-start(f32[8,128]{1,0:T(8,128)S(1)} %add.26), channel_id=1, source_target_pairs={{0,8},{8,0},{16,24},{24,16},{32,40},{40,32},{48,56},{56,48},{64,72... | collective-permute-start | bytes 12296 | tf_op jit(solution)/shard_map/ppermute | solution.py:449
  101.3 2.6 %collective-permute-done.6 = f32[8,128]{1,0:T(8,128)S(1)} collective-permute-done((f32[8,128]{1,0:T(8,128)S(1)}, f32[8,128]{1,0:T(8,128)S(1)}, u32[]{:S(2)}, u32[]{:S(2)}) %collective-permute-start.6) | collective-permute-done | bytes 4128 | tf_op jit(solution)/shard_map/ppermute | solution.py:449
  103.9 0.0 all-to-all-done.1.a
  103.9 0.8 gather.1
  104.6 5.0 %collective-permute-start.2 = (f32[3,6,5,256]{3,2,1,0:T(8,128)S(1)}, f32[3,6,5,256]{3,2,1,0:T(8,128)S(1)}, u32[]{:S(2)}, u32[]{:S(2)}) collective-permute-start(f32[3,6,5,256]{3,2,1,0:T(8,128)S(1)} %get-tuple-element.9.own), channel_id=1, source_target_pairs={{1,2},{3,4},{5,6},{7,8},{9,10},{11,12},{13,14},{15,16},{17,18},{19... | collective-permute-start | bytes 276488 | tf_op jit(solution)/shard_map/ppermute | solution.py:28
  109.7 1.9 %collective-permute-start.1 = (f32[3,6,5,256]{3,2,1,0:T(8,128)S(1)}, f32[3,6,5,256]{3,2,1,0:T(8,128)S(1)}, u32[]{:S(2)}, u32[]{:S(2)}) collective-permute-start(f32[3,6,5,256]{3,2,1,0:T(8,128)S(1)} %get-tuple-element.9.own), channel_id=1, source_target_pairs={{0,1},{2,3},{4,5},{6,7},{8,9},{10,11},{12,13},{14,15},{16,17},{18,... | collective-permute-start | bytes 276488 | tf_op jit(solution)/shard_map/ppermute | solution.py:28
  111.6 0.6 copy.11
  112.3 3.1 %collective-permute-done.2.cross = f32[3,6,5,256]{3,2,1,0:T(8,128)S(1)} collective-permute-done((f32[3,6,5,256]{3,2,1,0:T(8,128)S(1)}, f32[3,6,5,256]{3,2,1,0:T(8,128)S(1)}, u32[]{:S(2)}, u32[]{:S(2)}) %collective-permute-start.2) | collective-permute-done | bytes 92192 | tf_op jit(solution)/shard_map/ppermute | solution.py:28
  115.3 0.0 collective-permute-done.1.near
  115.3 1.5 %jump.1 = f32[3,5,6,256]{3,2,1,0:T(8,128)} custom-call(s32[5]{0:T(128)} %copy-done, s32[3,6]{1,0:T(4,128)} %side.1, s32[3,6]{1,0:T(4,128)} %patch.1, f32[3,6,5,256]{3,2,1,0:T(8,128)S(1)} %get-tuple-element.9.own, f32[3,6,5,256]{3,2,1,0:T(8,128)S(1)} %collective-permute-done.1.near, f32[3,6,5,256]{3,2,1,0:T(8,128)S(1)} %collective-permute-done.2.cross), custom_call_target="tpu_custom_call" | custom-call | tf_op jit(solution)/shard_map/jump/pallas_call | solution.py:484
  (6 shorter events, 0.1 us)
Async XLA Ops:
  0.7 52.1 %copy-start = (s32[5]{0:T(128)}, s32[5]{0:T(128)S(1)}, u32[]{:S(2)}) copy-start(s32[5]{0:T(128)S(1)} %stack.23.place) | copy-start | bytes 64
  3.9 4.5 %collective-permute-start = (f32[968,256]{1,0:T(8,128)S(1)}, f32[968,256]{1,0:T(8,128)S(1)}, u32[]{:S(2)}, u32[]{:S(2)}) collective-permute-start(f32[968,256]{1,0:T(8,128)S(1)} %get-tuple-element.7), channel_id=1, source_target_pairs={{0,1},{1,0},{2,3},{3,2},{4,5},{5,4},{6,7},{7,6},{8,9},{9,8},{10,11... | collective-permute-start | bytes 2973704 | tf_op jit(solution)/shard_map/ppermute | solution.py:415
  52.9 11.7 %all-to-all-start.2 = ((f32[32,8,128]{2,1,0:T(8,128)}), f32[32,8,128]{2,1,0:T(8,128)S(1)}, u32[]{:S(2)}, u32[]{:S(2)}) async-start(f32[32,8,128]{2,1,0:T(8,128)} %get-tuple-element.10), calls=%async_computation.2 | async-start | bytes 262144 | tf_op jit(solution)/shard_map/all_to_all | solution.py:416
  64.6 39.3 %all-to-all-start.1 = ((f32[12,80,256]{2,1,0:T(8,128)}), f32[12,80,256]{2,1,0:T(8,128)S(1)}, u32[]{:S(2)}, u32[]{:S(2)}) async-start(f32[12,80,256]{2,1,0:T(8,128)} %fold.1), calls=%async_computation.1 | async-start | bytes 1966080 | tf_op jit(solution)/shard_map/all_to_all | solution.py:470
  68.1 14.5 %collective-permute-start.3 = (f32[8,128]{1,0:T(8,128)S(1)}, f32[8,128]{1,0:T(8,128)S(1)}, u32[]{:S(2)}, u32[]{:S(2)}) collective-permute-start(f32[8,128]{1,0:T(8,128)S(1)} %reduce_sum.9), channel_id=1, source_target_pairs={{0,64},{8,72},{16,80},{24,88},{32,96},{40,104},{48,112},{56,120},{... | collective-permute-start | bytes 12296 | tf_op jit(solution)/shard_map/ppermute | solution.py:449
  82.6 9.4 %collective-permute-start.4 = (f32[8,128]{1,0:T(8,128)S(1)}, f32[8,128]{1,0:T(8,128)S(1)}, u32[]{:S(2)}, u32[]{:S(2)}) collective-permute-start(f32[8,128]{1,0:T(8,128)S(1)} %add.24), channel_id=1, source_target_pairs={{0,32},{8,40},{16,48},{24,56},{32,0},{40,8},{48,16},{56,24},{64,96... | collective-permute-start | bytes 12296 | tf_op jit(solution)/shard_map/ppermute | solution.py:449
  92.0 6.4 %collective-permute-start.5 = (f32[8,128]{1,0:T(8,128)S(1)}, f32[8,128]{1,0:T(8,128)S(1)}, u32[]{:S(2)}, u32[]{:S(2)}) collective-permute-start(f32[8,128]{1,0:T(8,128)S(1)} %add.25), channel_id=1, source_target_pairs={{0,16},{8,24},{16,0},{24,8},{32,48},{40,56},{48,32},{56,40},{64,80... | collective-permute-start | bytes 12296 | tf_op jit(solution)/shard_map/ppermute | solution.py:449
  98.4 5.5 %collective-permute-start.6 = (f32[8,128]{1,0:T(8,128)S(1)}, f32[8,128]{1,0:T(8,128)S(1)}, u32[]{:S(2)}, u32[]{:S(2)}) collective-permute-start(f32[8,128]{1,0:T(8,128)S(1)} %add.26), channel_id=1, source_target_pairs={{0,8},{8,0},{16,24},{24,16},{32,40},{40,32},{48,56},{56,48},{64,72... | collective-permute-start | bytes 12296 | tf_op jit(solution)/shard_map/ppermute | solution.py:449
  104.6 10.7 %collective-permute-start.2 = (f32[3,6,5,256]{3,2,1,0:T(8,128)S(1)}, f32[3,6,5,256]{3,2,1,0:T(8,128)S(1)}, u32[]{:S(2)}, u32[]{:S(2)}) collective-permute-start(f32[3,6,5,256]{3,2,1,0:T(8,128)S(1)} %get-tuple-element.9.own), channel_id=1, source_target_pairs={{1,2},{3,4},{5,6},{7,8},{9,10},{11,12},{13,14},{15,16},{17,18},{19... | collective-permute-start | bytes 276488 | tf_op jit(solution)/shard_map/ppermute | solution.py:28
  109.7 5.7 %collective-permute-start.1 = (f32[3,6,5,256]{3,2,1,0:T(8,128)S(1)}, f32[3,6,5,256]{3,2,1,0:T(8,128)S(1)}, u32[]{:S(2)}, u32[]{:S(2)}) collective-permute-start(f32[3,6,5,256]{3,2,1,0:T(8,128)S(1)} %get-tuple-element.9.own), channel_id=1, source_target_pairs={{0,1},{2,3},{4,5},{6,7},{8,9},{10,11},{12,13},{14,15},{16,17},{18,... | collective-permute-start | bytes 276488 | tf_op jit(solution)/shard_map/ppermute | solution.py:28

commit v9 on v8

--- a/solution.py
+++ b/solution.py
@@ -13,6 +13,7 @@
 PLANE = ("gx", "gz_0", "gz_1")
 UNROLL = 8
 META_ROWS = 8
+FACE_ROWS = 32
 BF16 = jnp.bfloat16
 F32 = jnp.float32
 I32 = jnp.int32
@@ -173,26 +174,22 @@
     code_x[...] = (over(col, edge) - over(row, edge)) * 4096 + within(col, edge)
 
     def enlist(found, base, old, slot, shift, dest):
-        mine = within(dest, cores) == core
-
-        @pl.when(mine)
-        def _():
-            table[0, found] = base + old
-            iz = within(dest, size_z)
-            ix = over(dest, size_z)
-            owner = (ix * size_y + index_y) * size_z + iz
-            table[1, found] = ratio[owner * new_count + slot]
-            table[2, found] = shift[0]
-            table[3, found] = shift[1] * 4096 + shift[2]
-            chip_y = over(iz, cores)
-            chunk = jnp.where(core == 0, ix, chip_y)
-            table[4, found] = (chunk * chips_y + jnp.where(core == 0, chip_y, ix)) * new_count + slot
-            rank = ends[chunk]
-            table[5, found] = chunk
-            table[6, found] = rank
-            ends[chunk] = rank + 1
-
-        return found + mine.astype(I32)
+        mine = jnp.where(within(dest, cores) == core, 1, 0)
+        iz = within(dest, size_z)
+        ix = over(dest, size_z)
+        owner = (ix * size_y + index_y) * size_z + iz
+        chip_y = over(iz, cores)
+        chunk = jnp.where(core == 0, ix, chip_y)
+        rank = ends[chunk]
+        table[0, found] = base + old
+        table[1, found] = ratio[owner * new_count + slot]
+        table[2, found] = shift[0]
+        table[3, found] = shift[1] * 4096 + shift[2]
+        table[4, found] = (chunk * chips_y + jnp.where(core == 0, chip_y, ix)) * new_count + slot
+        table[5, found] = chunk
+        table[6, found] = rank
+        ends[chunk] = rank + mine
+        return found + mine
 
     def enlist_own(p, found):
         shift = [pair_shift[a, p] for a in range(3)]
@@ -205,9 +202,9 @@
     for k in range(chunks):
         ends[k] = 0
     ratio_copy.wait()
-    found = lax.fori_loop(0, pairs, enlist_own, jnp.int32(0))
+    found = lax.fori_loop(0, pairs, enlist_own, jnp.int32(0), unroll=4)
     meta_copy.wait()
-    found = lax.fori_loop(0, pairs, enlist_peer, found)
+    found = lax.fori_loop(0, pairs, enlist_peer, found, unroll=4)
 
     before = jnp.int32(0)
     starts = []
@@ -329,10 +326,11 @@
         source == target * edge + (edge - 1),
     )
     for q in range(count):
+        faces[q, 6 * fields:, :] = jnp.zeros((FACE_ROWS - 6 * fields, lanes), F32)
         for f in range(fields):
             start = q * rows + f * edge
-            faces[q, 0, f:f + 1, :] = whole[start:start + 1]
-            faces[q, 1, f:f + 1, :] = whole[start + edge - 1:start + edge]
+            faces[q, f:f + 1, :] = whole[start:start + 1]
+            faces[q, fields + f:fields + f + 1, :] = whole[start + edge - 1:start + edge]
     for e, pick in enumerate(picks):
         weight = jnp.where(pick, 1.0, 0.0).astype(BF16)
         product = jnp.dot(stacked, weight, preferred_element_type=F32)
@@ -341,7 +339,8 @@
             for f in range(fields):
                 start = q * rows + f * edge
                 line = jnp.sum(jnp.where(here, layer[start:start + edge], 0.0), axis=0, keepdims=True)
-                faces[q, 2 + e, f:f + 1, :] = line
+                at = (2 + e) * fields + f
+                faces[q, at:at + 1, :] = line
 
 
 def jump_kernel(place, side, patch, own, near, cross, jump, *, count, fields, devices):
@@ -353,12 +352,12 @@
             n = patch[q, e]
             at = linear + u - 1
             present = (u < 3) & (at >= 0) & (at < devices)
-            other = e ^ 1
+            other = pl.ds((e ^ 1) * fields, fields)
             inside = (u == 2) == even
             ghost = jnp.where(
                 u == 1, own[n, other], jnp.where(inside, near[n, other], cross[n, other])
             )
-            line = jnp.where(present, ghost - own[q, e], 0.0)
+            line = jnp.where(present, ghost - own[q, pl.ds(e * fields, fields)], 0.0)
             for f in range(fields):
                 jump[q, f, e:e + 1, :] = line[f:f + 1]
 
@@ -472,7 +471,7 @@
         functools.partial(gather_kernel, count=count, fields=fields, edge=edge),
         out_shape=(
             jax.ShapeDtypeStruct((count * rows, lanes), F32),
-            VMEM((count, 6, fields, lanes), F32),
+            VMEM((count, FACE_ROWS, lanes), F32),
         ),
         in_specs=[vmem],
         out_specs=(vmem, vmem),
@@ -486,6 +485,7 @@
         out_shape=jax.ShapeDtypeStruct((count, fields, 6, lanes), F32),
         in_specs=[smem, smem, smem, vmem, vmem, vmem],
         out_specs=vmem,
+        compiler_params=params,
         name="jump",
     )(place, neighbor_side, neighbor_patch, fast(faces), fast(near), fast(cross))
     total_cells = patches * devices * edge * lanes

time: 117 us -> 117 us (level)
  no operation moved by 1% of the time
where the time goes in v9:
time: 117 us; the launch traced here: 116 us
  starting transfers between devices  42.6 us (36%)
  blocking collectives  35.4 us (30%)
  waiting for transfers between devices  19.1 us (16%)
  Pallas kernels  17.3 us (15%)
    all_to_all x1, blocking collectives, body(): lax.all_to_all(partials, ALL_AXES, 0, 0, tiled=True, axis_index_groups=fi...  35.4 us
    ppermute x4, starting transfers between devices, crossed(): lax.ppermute(value, 'gy', [(i, i ^ distance) for i in range(size_y)])  25.2 us
    ppermute x4, waiting for transfers between devices, crossed(): lax.ppermute(value, 'gy', [(i, i ^ distance) for i in range(size_y)])  10.5 us
    pallas_call x1, Pallas kernels, body(): pl.pallas_call(functools.partial(partials_kernel, patches=patches, fields...  8.83 us
    ppermute x2, starting transfers between devices, swapped(): return lax.ppermute(block, ALL_AXES, pairs + [(j, i) for i, j in pairs])  6.93 us
    all_to_all x1, starting transfers between devices, body(): plane = lax.all_to_all(mass, PLANE, 0, 0, tiled=True)  5.02 us
    all_to_all x1, waiting for transfers between devices, body(): plane = lax.all_to_all(mass, PLANE, 0, 0, tiled=True)  3.52 us
    all_to_all x1, starting transfers between devices, body(): lax.all_to_all(folded, ALL_AXES, 0, 0, tiled=True, axis_index_groups=last...  3.51 us
  transfers between devices with their start and end apart: 9, of which 7 were waited for; matrix products, arithmetic and copies ran while one was open for 1% of the time, Pallas kernels for 3%

profile of v9, /device:TPU:2, one launch (start us, length us, event | category | flops | bytes accessed | tf_op | source)
XLA Modules:
  0.0 115.9 jit_solution(2777982382534315448)
XLA Ops:
  0.6 0.1 stack.23.place
  0.7 3.2 %head.1 = (f32[32,8,128]{2,1,0:T(8,128)}, f32[968,256]{1,0:T(8,128)S(1)}) custom-call(s32[5]{0:T(128)S(1)} %stack.23.place, s32[32]{0:T(128)} %pair_old.3, s32[32]{0:T(128)} %pair_slot.3, s32[3,32]{1,0:T(4,128)} %bitcast.16, s32[1,32]{1,0:T(1,128)} %bitcast.21, s32[1,32]{1,0:T(1,128)} %bitcast.19, s32[1,32]{1,0:T(1,128)} %bitcast.20, s32[1,32]{1,0:T(1,128)} %bitcast.22, ...), custom_call_target="tpu_custom_call" | custom-call | tf_op jit(solution)/shard_map/head/pallas_call | solution.py:392
  3.9 1.9 %collective-permute-start = (f32[968,256]{1,0:T(8,128)S(1)}, f32[968,256]{1,0:T(8,128)S(1)}, u32[]{:S(2)}, u32[]{:S(2)}) collective-permute-start(f32[968,256]{1,0:T(8,128)S(1)} %get-tuple-element.7), channel_id=1, source_target_pairs={{0,1},{1,0},{2,3},{3,2},{4,5},{5,4},{6,7},{7,6},{8,9},{9,8},{10,11... | collective-permute-start | bytes 2973704 | tf_op jit(solution)/shard_map/ppermute | solution.py:414
  5.8 2.5 %collective-permute-done.peer = f32[968,256]{1,0:T(8,128)S(1)} collective-permute-done((f32[968,256]{1,0:T(8,128)S(1)}, f32[968,256]{1,0:T(8,128)S(1)}, u32[]{:S(2)}, u32[]{:S(2)}) %collective-permute-start) | collective-permute-done | bytes 991264 | tf_op jit(solution)/shard_map/ppermute | solution.py:414
  8.4 8.8 %partials.1 = f32[48,80,256]{2,1,0:T(8,128)} custom-call(s32[5]{0:T(128)S(1)} %stack.23.place, s32[32]{0:T(128)} %pair_old.3, s32[32]{0:T(128)} %pair_slot.3, s32[3,32]{1,0:T(4,128)} %bitcast.18, s32[1,32]{1,0:T(1,128)} %bitcast.23, s32[1536]{0:T(1024)} %ratio_in.3, f32[12,80,256]{2,1,0:T(8,128)} %bitcast.15, f32[968,256]{1,0:T(8,128)S(1)} %collective-permute-done.peer), custom_call_target="tpu_custom_call" | custom-call | tf_op jit(solution)/shard_map/partials/pallas_call | solution.py:416
  17.2 35.4 %all_to_all.15.a = f32[48,80,256]{2,1,0:T(8,128)} all-to-all(f32[48,80,256]{2,1,0:T(8,128)} %partials.1), channel_id=1, replica_groups={{0,128,256,384},{2,130,258,386},{4,132,260,388},{6,134,262,390},{8,136,..., dimensions={0} | all-to-all | bytes 7864320 | tf_op jit(solution)/shard_map/all_to_all | solution.py:444
  52.6 5.0 %all-to-all-start.2 = ((f32[32,8,128]{2,1,0:T(8,128)}), f32[32,8,128]{2,1,0:T(8,128)S(1)}, u32[]{:S(2)}, u32[]{:S(2)}) async-start(f32[32,8,128]{2,1,0:T(8,128)} %get-tuple-element.10), calls=%async_computation.2 | async-start | bytes 262144 | tf_op jit(solution)/shard_map/all_to_all | solution.py:415
  57.6 0.0 copy-start
  57.6 0.0 copy-start.1
  57.7 3.1 %fold.1 = f32[12,80,256]{2,1,0:T(8,128)} custom-call(f32[48,80,256]{2,1,0:T(8,128)} %all_to_all.15.a), custom_call_target="tpu_custom_call" | custom-call | tf_op jit(solution)/shard_map/fold/pallas_call | solution.py:455
  60.8 3.5 %all-to-all-done.2 = f32[32,8,128]{2,1,0:T(8,128)S(1)} async-done(((f32[32,8,128]{2,1,0:T(8,128)}), f32[32,8,128]{2,1,0:T(8,128)S(1)}, u32[]{:S(2)}, u32[]{:S(2)}) %all-to-all-start.2) | async-done | bytes 131104 | tf_op jit(solution)/shard_map/all_to_all | solution.py:415
  64.3 3.5 %all-to-all-start.1 = ((f32[12,80,256]{2,1,0:T(8,128)}), f32[12,80,256]{2,1,0:T(8,128)S(1)}, u32[]{:S(2)}, u32[]{:S(2)}) async-start(f32[12,80,256]{2,1,0:T(8,128)} %fold.1), calls=%async_computation.1 | async-start | bytes 1966080 | tf_op jit(solution)/shard_map/all_to_all | solution.py:469
  67.9 12.9 %collective-permute-start.3 = (f32[8,128]{1,0:T(8,128)S(1)}, f32[8,128]{1,0:T(8,128)S(1)}, u32[]{:S(2)}, u32[]{:S(2)}) collective-permute-start(f32[8,128]{1,0:T(8,128)S(1)} %reduce_sum.9), channel_id=1, source_target_pairs={{0,64},{8,72},{16,80},{24,88},{32,96},{40,104},{48,112},{56,120},{... | collective-permute-start | bytes 12296 | tf_op jit(solution)/shard_map/ppermute | solution.py:448
  80.7 1.6 %collective-permute-done.3 = f32[8,128]{1,0:T(8,128)S(1)} collective-permute-done((f32[8,128]{1,0:T(8,128)S(1)}, f32[8,128]{1,0:T(8,128)S(1)}, u32[]{:S(2)}, u32[]{:S(2)}) %collective-permute-start.3) | collective-permute-done | bytes 4128 | tf_op jit(solution)/shard_map/ppermute | solution.py:448
  82.3 6.0 %collective-permute-start.4 = (f32[8,128]{1,0:T(8,128)S(1)}, f32[8,128]{1,0:T(8,128)S(1)}, u32[]{:S(2)}, u32[]{:S(2)}) collective-permute-start(f32[8,128]{1,0:T(8,128)S(1)} %add.24), channel_id=1, source_target_pairs={{0,32},{8,40},{16,48},{24,56},{32,0},{40,8},{48,16},{56,24},{64,96... | collective-permute-start | bytes 12296 | tf_op jit(solution)/shard_map/ppermute | solution.py:448
  88.4 3.4 %collective-permute-done.4 = f32[8,128]{1,0:T(8,128)S(1)} collective-permute-done((f32[8,128]{1,0:T(8,128)S(1)}, f32[8,128]{1,0:T(8,128)S(1)}, u32[]{:S(2)}, u32[]{:S(2)}) %collective-permute-start.4) | collective-permute-done | bytes 4128 | tf_op jit(solution)/shard_map/ppermute | solution.py:448
  91.7 3.4 %collective-permute-start.5 = (f32[8,128]{1,0:T(8,128)S(1)}, f32[8,128]{1,0:T(8,128)S(1)}, u32[]{:S(2)}, u32[]{:S(2)}) collective-permute-start(f32[8,128]{1,0:T(8,128)S(1)} %add.25), channel_id=1, source_target_pairs={{0,16},{8,24},{16,0},{24,8},{32,48},{40,56},{48,32},{56,40},{64,80... | collective-permute-start | bytes 12296 | tf_op jit(solution)/shard_map/ppermute | solution.py:448
  95.1 3.0 %collective-permute-done.5 = f32[8,128]{1,0:T(8,128)S(1)} collective-permute-done((f32[8,128]{1,0:T(8,128)S(1)}, f32[8,128]{1,0:T(8,128)S(1)}, u32[]{:S(2)}, u32[]{:S(2)}) %collective-permute-start.5) | collective-permute-done | bytes 4128 | tf_op jit(solution)/shard_map/ppermute | solution.py:448
  98.1 2.9 %collective-permute-start.6 = (f32[8,128]{1,0:T(8,128)S(1)}, f32[8,128]{1,0:T(8,128)S(1)}, u32[]{:S(2)}, u32[]{:S(2)}) collective-permute-start(f32[8,128]{1,0:T(8,128)S(1)} %add.26), channel_id=1, source_target_pairs={{0,8},{8,0},{16,24},{24,16},{32,40},{40,32},{48,56},{56,48},{64,72... | collective-permute-start | bytes 12296 | tf_op jit(solution)/shard_map/ppermute | solution.py:448
  101.1 2.5 %collective-permute-done.6 = f32[8,128]{1,0:T(8,128)S(1)} collective-permute-done((f32[8,128]{1,0:T(8,128)S(1)}, f32[8,128]{1,0:T(8,128)S(1)}, u32[]{:S(2)}, u32[]{:S(2)}) %collective-permute-start.6) | collective-permute-done | bytes 4128 | tf_op jit(solution)/shard_map/ppermute | solution.py:448
  103.6 0.0 all-to-all-done.1.a
  103.6 0.8 gather.1
  104.4 5.0 %collective-permute-start.2 = (f32[3,32,256]{2,1,0:T(8,128)S(1)}, f32[3,32,256]{2,1,0:T(8,128)S(1)}, u32[]{:S(2)}, u32[]{:S(2)}) collective-permute-start(f32[3,32,256]{2,1,0:T(8,128)S(1)} %get-tuple-element.9.own), channel_id=1, source_target_pairs={{1,2},{3,4},{5,6},{7,8},{9,10},{11,12},{13,14},{15,16},{17,18},{19... | collective-permute-start | bytes 294920 | tf_op jit(solution)/shard_map/ppermute | solution.py:29
  109.4 1.9 %collective-permute-start.1 = (f32[3,32,256]{2,1,0:T(8,128)S(1)}, f32[3,32,256]{2,1,0:T(8,128)S(1)}, u32[]{:S(2)}, u32[]{:S(2)}) collective-permute-start(f32[3,32,256]{2,1,0:T(8,128)S(1)} %get-tuple-element.9.own), channel_id=1, source_target_pairs={{0,1},{2,3},{4,5},{6,7},{8,9},{10,11},{12,13},{14,15},{16,17},{18,... | collective-permute-start | bytes 294920 | tf_op jit(solution)/shard_map/ppermute | solution.py:29
  111.3 0.6 copy.11
  112.0 2.5 %collective-permute-done.2.cross = f32[3,32,256]{2,1,0:T(8,128)S(1)} collective-permute-done((f32[3,32,256]{2,1,0:T(8,128)S(1)}, f32[3,32,256]{2,1,0:T(8,128)S(1)}, u32[]{:S(2)}, u32[]{:S(2)}) %collective-permute-start.2) | collective-permute-done | bytes 98336 | tf_op jit(solution)/shard_map/ppermute | solution.py:29
  114.5 0.0 collective-permute-done.1.near
  114.5 0.0 copy-done
  114.5 0.0 copy-done.1
  114.5 1.4 %jump.1 = f32[3,5,6,256]{3,2,1,0:T(8,128)} custom-call(s32[5]{0:T(128)S(1)} %stack.23.place, s32[3,6]{1,0:T(4,128)S(1)} %copy-done, s32[3,6]{1,0:T(4,128)S(1)} %copy-done.1, f32[3,32,256]{2,1,0:T(8,128)S(1)} %get-tuple-element.9.own, f32[3,32,256]{2,1,0:T(8,128)S(1)} %collective-permute-done.1.near, f32[3,32,256]{2,1,0:T(8,128)S(1)} %collective-permute-done.2.cross), custom_call_target="tpu_custom_call" | custom-call | tf_op jit(solution)/shard_map/jump/pallas_call | solution.py:483
  (6 shorter events, 0.1 us)
Async XLA Ops:
  3.9 4.5 %collective-permute-start = (f32[968,256]{1,0:T(8,128)S(1)}, f32[968,256]{1,0:T(8,128)S(1)}, u32[]{:S(2)}, u32[]{:S(2)}) collective-permute-start(f32[968,256]{1,0:T(8,128)S(1)} %get-tuple-element.7), channel_id=1, source_target_pairs={{0,1},{1,0},{2,3},{3,2},{4,5},{5,4},{6,7},{7,6},{8,9},{9,8},{10,11... | collective-permute-start | bytes 2973704 | tf_op jit(solution)/shard_map/ppermute | solution.py:414
  52.6 11.7 %all-to-all-start.2 = ((f32[32,8,128]{2,1,0:T(8,128)}), f32[32,8,128]{2,1,0:T(8,128)S(1)}, u32[]{:S(2)}, u32[]{:S(2)}) async-start(f32[32,8,128]{2,1,0:T(8,128)} %get-tuple-element.10), calls=%async_computation.2 | async-start | bytes 262144 | tf_op jit(solution)/shard_map/all_to_all | solution.py:415
  57.6 56.9 %copy-start = (s32[3,6]{1,0:T(4,128)S(1)}, s32[3,6]{1,0:T(4,128)}, u32[]{:S(2)}) copy-start(s32[3,6]{1,0:T(4,128)} %side.1) | copy-start | bytes 220
  57.6 56.9 %copy-start.1 = (s32[3,6]{1,0:T(4,128)S(1)}, s32[3,6]{1,0:T(4,128)}, u32[]{:S(2)}) copy-start(s32[3,6]{1,0:T(4,128)} %patch.1) | copy-start | bytes 220
  64.3 39.3 %all-to-all-start.1 = ((f32[12,80,256]{2,1,0:T(8,128)}), f32[12,80,256]{2,1,0:T(8,128)S(1)}, u32[]{:S(2)}, u32[]{:S(2)}) async-start(f32[12,80,256]{2,1,0:T(8,128)} %fold.1), calls=%async_computation.1 | async-start | bytes 1966080 | tf_op jit(solution)/shard_map/all_to_all | solution.py:469
  67.9 14.4 %collective-permute-start.3 = (f32[8,128]{1,0:T(8,128)S(1)}, f32[8,128]{1,0:T(8,128)S(1)}, u32[]{:S(2)}, u32[]{:S(2)}) collective-permute-start(f32[8,128]{1,0:T(8,128)S(1)} %reduce_sum.9), channel_id=1, source_target_pairs={{0,64},{8,72},{16,80},{24,88},{32,96},{40,104},{48,112},{56,120},{... | collective-permute-start | bytes 12296 | tf_op jit(solution)/shard_map/ppermute | solution.py:448
  82.3 9.4 %collective-permute-start.4 = (f32[8,128]{1,0:T(8,128)S(1)}, f32[8,128]{1,0:T(8,128)S(1)}, u32[]{:S(2)}, u32[]{:S(2)}) collective-permute-start(f32[8,128]{1,0:T(8,128)S(1)} %add.24), channel_id=1, source_target_pairs={{0,32},{8,40},{16,48},{24,56},{32,0},{40,8},{48,16},{56,24},{64,96... | collective-permute-start | bytes 12296 | tf_op jit(solution)/shard_map/ppermute | solution.py:448
  91.7 6.4 %collective-permute-start.5 = (f32[8,128]{1,0:T(8,128)S(1)}, f32[8,128]{1,0:T(8,128)S(1)}, u32[]{:S(2)}, u32[]{:S(2)}) collective-permute-start(f32[8,128]{1,0:T(8,128)S(1)} %add.25), channel_id=1, source_target_pairs={{0,16},{8,24},{16,0},{24,8},{32,48},{40,56},{48,32},{56,40},{64,80... | collective-permute-start | bytes 12296 | tf_op jit(solution)/shard_map/ppermute | solution.py:448
  98.1 5.5 %collective-permute-start.6 = (f32[8,128]{1,0:T(8,128)S(1)}, f32[8,128]{1,0:T(8,128)S(1)}, u32[]{:S(2)}, u32[]{:S(2)}) collective-permute-start(f32[8,128]{1,0:T(8,128)S(1)} %add.26), channel_id=1, source_target_pairs={{0,8},{8,0},{16,24},{24,16},{32,40},{40,32},{48,56},{56,48},{64,72... | collective-permute-start | bytes 12296 | tf_op jit(solution)/shard_map/ppermute | solution.py:448
  104.4 10.1 %collective-permute-start.2 = (f32[3,32,256]{2,1,0:T(8,128)S(1)}, f32[3,32,256]{2,1,0:T(8,128)S(1)}, u32[]{:S(2)}, u32[]{:S(2)}) collective-permute-start(f32[3,32,256]{2,1,0:T(8,128)S(1)} %get-tuple-element.9.own), channel_id=1, source_target_pairs={{1,2},{3,4},{5,6},{7,8},{9,10},{11,12},{13,14},{15,16},{17,18},{19... | collective-permute-start | bytes 294920 | tf_op jit(solution)/shard_map/ppermute | solution.py:29
  109.4 5.1 %collective-permute-start.1 = (f32[3,32,256]{2,1,0:T(8,128)S(1)}, f32[3,32,256]{2,1,0:T(8,128)S(1)}, u32[]{:S(2)}, u32[]{:S(2)}) collective-permute-start(f32[3,32,256]{2,1,0:T(8,128)S(1)} %get-tuple-element.9.own), channel_id=1, source_target_pairs={{0,1},{2,3},{4,5},{6,7},{8,9},{10,11},{12,13},{14,15},{16,17},{18,... | collective-permute-start | bytes 294920 | tf_op jit(solution)/shard_map/ppermute | solution.py:29

commit v10 on v9

--- a/solution.py
+++ b/solution.py
@@ -106,7 +106,7 @@
         return carry
 
     ratio_copy.wait()
-    lax.fori_loop(0, pairs, count, 0)
+    lax.fori_loop(0, pairs, count, 0, unroll=4)
     own_copy.wait()
 
     def add(o, sums):
@@ -121,21 +121,20 @@
         return tuple(old_list), tuple(new_list)
 
     zero = tuple(jnp.zeros((edge, half), F32) for _ in range(fields))
-    olds, news = lax.fori_loop(0, patches, add, (zero, zero))
-    lane = iota((1, half), 1)
-    lines = []
-    for f in range(fields):
-        old_f = jnp.sum(olds[f], keepdims=True)
-        new_f = jnp.sum(news[f], keepdims=True)
-        lines.append(jnp.where(lane == 0, old_f, jnp.where(lane == 1, new_f, 0.0)))
-    lines.append(jnp.zeros((8 - fields, half), F32))
-    packed = jnp.concatenate(lines, axis=0)
-    out[...] = jnp.broadcast_to(packed[None], out.shape)
+    olds, news = lax.fori_loop(0, patches, add, (zero, zero), unroll=2)
+    lane = iota((8, half), 1)
+    blank = [jnp.zeros((8 - fields, half), F32)]
+    old_rows = jnp.concatenate([jnp.sum(block, axis=0, keepdims=True) for block in olds] + blank, axis=0)
+    new_rows = jnp.concatenate([jnp.sum(block, axis=0, keepdims=True) for block in news] + blank, axis=0)
+    old_mass = jnp.sum(old_rows, axis=1, keepdims=True)
+    new_mass = jnp.sum(new_rows, axis=1, keepdims=True)
+    both = jnp.where(lane == 0, old_mass, jnp.where(lane == 1, new_mass, 0.0))
+    out[...] = jnp.broadcast_to(both[None], out.shape)
 
 
 def partials_kernel(
     place, pair_old, pair_slot, pair_shift, pair_dest, ratio_in, own_in, peer,
-    out, ratio, own, meta_v, meta, table, order, ends, sums, split, code_k, code_x, sems, out_sems,
+    out, ratio, own, meta_v, meta, table, order, ends, sums, split, code_x, sems, out_sems,
     *, patches, fields, edge, size_y, chips_y, cores, new_count, pairs,
 ):
     rows = fields * edge
@@ -167,8 +166,6 @@
     chunks = ends.shape[0]
     chunk_size = out.shape[0] // chunks
     spare = out.shape[0]
-    cell = iota((lanes, lanes), 0)
-    code_k[...] = over(cell, edge) * 4096 + within(cell, edge)
     row = iota((rows, 2 * rows), 0)
     col = iota((rows, 2 * rows), 1) % rows
     code_x[...] = (over(col, edge) - over(row, edge)) * 4096 + within(col, edge)
@@ -184,7 +181,8 @@
         table[0, found] = base + old
         table[1, found] = ratio[owner * new_count + slot]
         table[2, found] = shift[0]
-        table[3, found] = shift[1] * 4096 + shift[2]
+        table[3, found] = shift[1]
+        table[7, found] = shift[2]
         table[4, found] = (chunk * chips_y + jnp.where(core == 0, chip_y, ix)) * new_count + slot
         table[5, found] = chunk
         table[6, found] = rank
@@ -220,7 +218,7 @@
     lax.fori_loop(0, found, place_in_order, 0)
     stops = starts[1:] + [found]
     blank = table.shape[1] - 1
-    for field, value in enumerate((0, 1, 0, 0, spare)):
+    for field, value in enumerate((0, 1, 0, 0, spare, 0, 0, 0)):
         table[field, blank] = value
     for extra in range(UNROLL - 1):
         order[found + extra] = blank
@@ -240,7 +238,9 @@
     lax.fori_loop(0, patches, prepare, 0)
 
     lane_k = iota((1, lanes), 1)
-    lane_code = over(lane_k, edge) * 4096 + within(lane_k, edge)
+    lane_y = over(lane_k, edge)
+    lane_z = within(lane_k, edge)
+    near_row = iota((edge, lanes), 0)
     row_x = within(iota((rows, 1), 0), edge)
 
     def remap(step, carry):
@@ -252,8 +252,13 @@
             spread = code_x[...] - (row_x * r + table[2, p])
             weight_x = jnp.where((spread & ~(r - 1)) == 0, inverse, 0.0).astype(BF16)
             section = jnp.dot(weight_x, split[table[0, p]], preferred_element_type=F32)
-            spread = code_k[...] - (lane_code * r + table[3, p])
-            weight_k = jnp.where((spread & ~((r - 1) * 4097)) == 0, inverse * inverse, 0.0).astype(BF16)
+            spread = near_row - (lane_y * r + table[3, p])
+            weight_y = jnp.where((spread & ~(r - 1)) == 0, inverse, 0.0)
+            spread = near_row - (lane_z * r + table[7, p])
+            weight_z = jnp.where((spread & ~(r - 1)) == 0, inverse, 0.0)
+            weight_k = jnp.concatenate(
+                [(weight_y[n:n + 1] * weight_z).astype(BF16) for n in range(edge)], axis=0
+            )
             high, low = halves(section)
             stacked = jnp.concatenate([high, low], axis=0)
             product = jnp.dot(stacked, weight_k, preferred_element_type=F32)
@@ -426,12 +431,11 @@
             pltpu.VMEM((patches, rows, lanes), F32),
             pltpu.VMEM((META_ROWS, half), I32),
             pltpu.SMEM((META_ROWS, half), I32),
-            pltpu.SMEM((7, 2 * pairs + 1), I32),
+            pltpu.SMEM((8, 2 * pairs + 1), I32),
             pltpu.SMEM((2 * pairs + UNROLL,), I32),
             pltpu.SMEM((size_x,), I32),
             pltpu.VMEM((owners + 1, rows, lanes), F32),
             pltpu.VMEM((2 * patches, 2 * rows, lanes), BF16),
-            pltpu.VMEM((lanes, lanes), I32),
             pltpu.VMEM((rows, 2 * rows), I32),
             DMA((3,)),
             DMA((size_x,)),

time: 117 us -> 116 us (level)
  no operation moved by 1% of the time
where the time goes in v10:
time: 116 us
  starting transfers between devices  42.6 us (37%)
  blocking collectives  35.4 us (31%)
  waiting for transfers between devices  19.1 us (16%)
  Pallas kernels  17.1 us (15%)
    all_to_all x1, blocking collectives, body(): lax.all_to_all(partials, ALL_AXES, 0, 0, tiled=True, axis_index_groups=fi...  35.4 us
    ppermute x4, starting transfers between devices, crossed(): lax.ppermute(value, 'gy', [(i, i ^ distance) for i in range(size_y)])  25.3 us
    ppermute x4, waiting for transfers between devices, crossed(): lax.ppermute(value, 'gy', [(i, i ^ distance) for i in range(size_y)])  10.4 us
    pallas_call x1, Pallas kernels, body(): pl.pallas_call(functools.partial(partials_kernel, patches=patches, fields...  8.86 us
    ppermute x2, starting transfers between devices, swapped(): return lax.ppermute(block, ALL_AXES, pairs + [(j, i) for i, j in pairs])  6.93 us
    all_to_all x1, starting transfers between devices, body(): plane = lax.all_to_all(mass, PLANE, 0, 0, tiled=True)  5.02 us
    all_to_all x1, waiting for transfers between devices, body(): plane = lax.all_to_all(mass, PLANE, 0, 0, tiled=True)  3.52 us
    all_to_all x1, starting transfers between devices, body(): lax.all_to_all(folded, ALL_AXES, 0, 0, tiled=True, axis_index_groups=last...  3.51 us
  transfers between devices with their start and end apart: 9, of which 7 were waited for; matrix products, arithmetic and copies ran while one was open for 1% of the time, Pallas kernels for 3%

profile of v10, /device:TPU:2, one launch (start us, length us, event | category | flops | bytes accessed | tf_op | source)
XLA Modules:
  0.0 115.8 jit_solution(15678901283869957646)
XLA Ops:
  0.6 0.1 stack.23.place
  0.7 3.0 %head.1 = (f32[32,8,128]{2,1,0:T(8,128)}, f32[968,256]{1,0:T(8,128)S(1)}) custom-call(s32[5]{0:T(128)S(1)} %stack.23.place, s32[32]{0:T(128)} %pair_old.3, s32[32]{0:T(128)} %pair_slot.3, s32[3,32]{1,0:T(4,128)} %bitcast.16, s32[1,32]{1,0:T(1,128)} %bitcast.21, s32[1,32]{1,0:T(1,128)} %bitcast.19, s32[1,32]{1,0:T(1,128)} %bitcast.20, s32[1,32]{1,0:T(1,128)} %bitcast.22, ...), custom_call_target="tpu_custom_call" | custom-call | tf_op jit(solution)/shard_map/head/pallas_call | solution.py:397
  3.7 1.9 %collective-permute-start = (f32[968,256]{1,0:T(8,128)S(1)}, f32[968,256]{1,0:T(8,128)S(1)}, u32[]{:S(2)}, u32[]{:S(2)}) collective-permute-start(f32[968,256]{1,0:T(8,128)S(1)} %get-tuple-element.7), channel_id=1, source_target_pairs={{0,1},{1,0},{2,3},{3,2},{4,5},{5,4},{6,7},{7,6},{8,9},{9,8},{10,11... | collective-permute-start | bytes 2973704 | tf_op jit(solution)/shard_map/ppermute | solution.py:419
  5.6 2.5 %collective-permute-done.peer = f32[968,256]{1,0:T(8,128)S(1)} collective-permute-done((f32[968,256]{1,0:T(8,128)S(1)}, f32[968,256]{1,0:T(8,128)S(1)}, u32[]{:S(2)}, u32[]{:S(2)}) %collective-permute-start) | collective-permute-done | bytes 991264 | tf_op jit(solution)/shard_map/ppermute | solution.py:419
  8.2 8.9 %partials.1 = f32[48,80,256]{2,1,0:T(8,128)} custom-call(s32[5]{0:T(128)S(1)} %stack.23.place, s32[32]{0:T(128)} %pair_old.3, s32[32]{0:T(128)} %pair_slot.3, s32[3,32]{1,0:T(4,128)} %bitcast.18, s32[1,32]{1,0:T(1,128)} %bitcast.23, s32[1536]{0:T(1024)} %ratio_in.3, f32[12,80,256]{2,1,0:T(8,128)} %bitcast.15, f32[968,256]{1,0:T(8,128)S(1)} %collective-permute-done.peer), custom_call_target="tpu_custom_call" | custom-call | tf_op jit(solution)/shard_map/partials/pallas_call | solution.py:421
  17.0 35.4 %all_to_all.15.a = f32[48,80,256]{2,1,0:T(8,128)} all-to-all(f32[48,80,256]{2,1,0:T(8,128)} %partials.1), channel_id=1, replica_groups={{0,128,256,384},{2,130,258,386},{4,132,260,388},{6,134,262,390},{8,136,..., dimensions={0} | all-to-all | bytes 7864320 | tf_op jit(solution)/shard_map/all_to_all | solution.py:448
  52.4 5.0 %all-to-all-start.2 = ((f32[32,8,128]{2,1,0:T(8,128)}), f32[32,8,128]{2,1,0:T(8,128)S(1)}, u32[]{:S(2)}, u32[]{:S(2)}) async-start(f32[32,8,128]{2,1,0:T(8,128)} %get-tuple-element.10), calls=%async_computation.2 | async-start | bytes 262144 | tf_op jit(solution)/shard_map/all_to_all | solution.py:420
  57.5 0.0 copy-start
  57.5 0.0 copy-start.1
  57.5 3.1 %fold.1 = f32[12,80,256]{2,1,0:T(8,128)} custom-call(f32[48,80,256]{2,1,0:T(8,128)} %all_to_all.15.a), custom_call_target="tpu_custom_call" | custom-call | tf_op jit(solution)/shard_map/fold/pallas_call | solution.py:459
  60.6 3.5 %all-to-all-done.2 = f32[32,8,128]{2,1,0:T(8,128)S(1)} async-done(((f32[32,8,128]{2,1,0:T(8,128)}), f32[32,8,128]{2,1,0:T(8,128)S(1)}, u32[]{:S(2)}, u32[]{:S(2)}) %all-to-all-start.2) | async-done | bytes 131104 | tf_op jit(solution)/shard_map/all_to_all | solution.py:420
  64.2 3.5 %all-to-all-start.1 = ((f32[12,80,256]{2,1,0:T(8,128)}), f32[12,80,256]{2,1,0:T(8,128)S(1)}, u32[]{:S(2)}, u32[]{:S(2)}) async-start(f32[12,80,256]{2,1,0:T(8,128)} %fold.1), calls=%async_computation.1 | async-start | bytes 1966080 | tf_op jit(solution)/shard_map/all_to_all | solution.py:473
  67.7 12.9 %collective-permute-start.3 = (f32[8,128]{1,0:T(8,128)S(1)}, f32[8,128]{1,0:T(8,128)S(1)}, u32[]{:S(2)}, u32[]{:S(2)}) collective-permute-start(f32[8,128]{1,0:T(8,128)S(1)} %reduce_sum.9), channel_id=1, source_target_pairs={{0,64},{8,72},{16,80},{24,88},{32,96},{40,104},{48,112},{56,120},{... | collective-permute-start | bytes 12296 | tf_op jit(solution)/shard_map/ppermute | solution.py:452
  80.6 1.6 %collective-permute-done.3 = f32[8,128]{1,0:T(8,128)S(1)} collective-permute-done((f32[8,128]{1,0:T(8,128)S(1)}, f32[8,128]{1,0:T(8,128)S(1)}, u32[]{:S(2)}, u32[]{:S(2)}) %collective-permute-start.3) | collective-permute-done | bytes 4128 | tf_op jit(solution)/shard_map/ppermute | solution.py:452
  82.2 6.0 %collective-permute-start.4 = (f32[8,128]{1,0:T(8,128)S(1)}, f32[8,128]{1,0:T(8,128)S(1)}, u32[]{:S(2)}, u32[]{:S(2)}) collective-permute-start(f32[8,128]{1,0:T(8,128)S(1)} %add.24), channel_id=1, source_target_pairs={{0,32},{8,40},{16,48},{24,56},{32,0},{40,8},{48,16},{56,24},{64,96... | collective-permute-start | bytes 12296 | tf_op jit(solution)/shard_map/ppermute | solution.py:452
  88.2 3.3 %collective-permute-done.4 = f32[8,128]{1,0:T(8,128)S(1)} collective-permute-done((f32[8,128]{1,0:T(8,128)S(1)}, f32[8,128]{1,0:T(8,128)S(1)}, u32[]{:S(2)}, u32[]{:S(2)}) %collective-permute-start.4) | collective-permute-done | bytes 4128 | tf_op jit(solution)/shard_map/ppermute | solution.py:452
  91.6 3.4 %collective-permute-start.5 = (f32[8,128]{1,0:T(8,128)S(1)}, f32[8,128]{1,0:T(8,128)S(1)}, u32[]{:S(2)}, u32[]{:S(2)}) collective-permute-start(f32[8,128]{1,0:T(8,128)S(1)} %add.25), channel_id=1, source_target_pairs={{0,16},{8,24},{16,0},{24,8},{32,48},{40,56},{48,32},{56,40},{64,80... | collective-permute-start | bytes 12296 | tf_op jit(solution)/shard_map/ppermute | solution.py:452
  95.0 3.0 %collective-permute-done.5 = f32[8,128]{1,0:T(8,128)S(1)} collective-permute-done((f32[8,128]{1,0:T(8,128)S(1)}, f32[8,128]{1,0:T(8,128)S(1)}, u32[]{:S(2)}, u32[]{:S(2)}) %collective-permute-start.5) | collective-permute-done | bytes 4128 | tf_op jit(solution)/shard_map/ppermute | solution.py:452
  98.0 2.9 %collective-permute-start.6 = (f32[8,128]{1,0:T(8,128)S(1)}, f32[8,128]{1,0:T(8,128)S(1)}, u32[]{:S(2)}, u32[]{:S(2)}) collective-permute-start(f32[8,128]{1,0:T(8,128)S(1)} %add.26), channel_id=1, source_target_pairs={{0,8},{8,0},{16,24},{24,16},{32,40},{40,32},{48,56},{56,48},{64,72... | collective-permute-start | bytes 12296 | tf_op jit(solution)/shard_map/ppermute | solution.py:452
  100.9 2.5 %collective-permute-done.6 = f32[8,128]{1,0:T(8,128)S(1)} collective-permute-done((f32[8,128]{1,0:T(8,128)S(1)}, f32[8,128]{1,0:T(8,128)S(1)}, u32[]{:S(2)}, u32[]{:S(2)}) %collective-permute-start.6) | collective-permute-done | bytes 4128 | tf_op jit(solution)/shard_map/ppermute | solution.py:452
  103.5 0.0 all-to-all-done.1.a
  103.5 0.8 gather.1
  104.2 5.0 %collective-permute-start.2 = (f32[3,32,256]{2,1,0:T(8,128)S(1)}, f32[3,32,256]{2,1,0:T(8,128)S(1)}, u32[]{:S(2)}, u32[]{:S(2)}) collective-permute-start(f32[3,32,256]{2,1,0:T(8,128)S(1)} %get-tuple-element.9.own), channel_id=1, source_target_pairs={{1,2},{3,4},{5,6},{7,8},{9,10},{11,12},{13,14},{15,16},{17,18},{19... | collective-permute-start | bytes 294920 | tf_op jit(solution)/shard_map/ppermute | solution.py:29
  109.2 1.9 %collective-permute-start.1 = (f32[3,32,256]{2,1,0:T(8,128)S(1)}, f32[3,32,256]{2,1,0:T(8,128)S(1)}, u32[]{:S(2)}, u32[]{:S(2)}) collective-permute-start(f32[3,32,256]{2,1,0:T(8,128)S(1)} %get-tuple-element.9.own), channel_id=1, source_target_pairs={{0,1},{2,3},{4,5},{6,7},{8,9},{10,11},{12,13},{14,15},{16,17},{18,... | collective-permute-start | bytes 294920 | tf_op jit(solution)/shard_map/ppermute | solution.py:29
  111.2 0.6 copy.11
  111.8 2.5 %collective-permute-done.2.cross = f32[3,32,256]{2,1,0:T(8,128)S(1)} collective-permute-done((f32[3,32,256]{2,1,0:T(8,128)S(1)}, f32[3,32,256]{2,1,0:T(8,128)S(1)}, u32[]{:S(2)}, u32[]{:S(2)}) %collective-permute-start.2) | collective-permute-done | bytes 98336 | tf_op jit(solution)/shard_map/ppermute | solution.py:29
  114.4 0.0 collective-permute-done.1.near
  114.4 0.0 copy-done
  114.4 0.0 copy-done.1
  114.4 1.4 %jump.1 = f32[3,5,6,256]{3,2,1,0:T(8,128)} custom-call(s32[5]{0:T(128)S(1)} %stack.23.place, s32[3,6]{1,0:T(4,128)S(1)} %copy-done, s32[3,6]{1,0:T(4,128)S(1)} %copy-done.1, f32[3,32,256]{2,1,0:T(8,128)S(1)} %get-tuple-element.9.own, f32[3,32,256]{2,1,0:T(8,128)S(1)} %collective-permute-done.1.near, f32[3,32,256]{2,1,0:T(8,128)S(1)} %collective-permute-done.2.cross), custom_call_target="tpu_custom_call" | custom-call | tf_op jit(solution)/shard_map/jump/pallas_call | solution.py:487
  (6 shorter events, 0.1 us)
Async XLA Ops:
  3.7 4.5 %collective-permute-start = (f32[968,256]{1,0:T(8,128)S(1)}, f32[968,256]{1,0:T(8,128)S(1)}, u32[]{:S(2)}, u32[]{:S(2)}) collective-permute-start(f32[968,256]{1,0:T(8,128)S(1)} %get-tuple-element.7), channel_id=1, source_target_pairs={{0,1},{1,0},{2,3},{3,2},{4,5},{5,4},{6,7},{7,6},{8,9},{9,8},{10,11... | collective-permute-start | bytes 2973704 | tf_op jit(solution)/shard_map/ppermute | solution.py:419
  52.4 11.7 %all-to-all-start.2 = ((f32[32,8,128]{2,1,0:T(8,128)}), f32[32,8,128]{2,1,0:T(8,128)S(1)}, u32[]{:S(2)}, u32[]{:S(2)}) async-start(f32[32,8,128]{2,1,0:T(8,128)} %get-tuple-element.10), calls=%async_computation.2 | async-start | bytes 262144 | tf_op jit(solution)/shard_map/all_to_all | solution.py:420
  57.5 56.9 %copy-start = (s32[3,6]{1,0:T(4,128)S(1)}, s32[3,6]{1,0:T(4,128)}, u32[]{:S(2)}) copy-start(s32[3,6]{1,0:T(4,128)} %side.1) | copy-start | bytes 220
  57.5 56.9 %copy-start.1 = (s32[3,6]{1,0:T(4,128)S(1)}, s32[3,6]{1,0:T(4,128)}, u32[]{:S(2)}) copy-start(s32[3,6]{1,0:T(4,128)} %patch.1) | copy-start | bytes 220
  64.2 39.3 %all-to-all-start.1 = ((f32[12,80,256]{2,1,0:T(8,128)}), f32[12,80,256]{2,1,0:T(8,128)S(1)}, u32[]{:S(2)}, u32[]{:S(2)}) async-start(f32[12,80,256]{2,1,0:T(8,128)} %fold.1), calls=%async_computation.1 | async-start | bytes 1966080 | tf_op jit(solution)/shard_map/all_to_all | solution.py:473
  67.7 14.5 %collective-permute-start.3 = (f32[8,128]{1,0:T(8,128)S(1)}, f32[8,128]{1,0:T(8,128)S(1)}, u32[]{:S(2)}, u32[]{:S(2)}) collective-permute-start(f32[8,128]{1,0:T(8,128)S(1)} %reduce_sum.9), channel_id=1, source_target_pairs={{0,64},{8,72},{16,80},{24,88},{32,96},{40,104},{48,112},{56,120},{... | collective-permute-start | bytes 12296 | tf_op jit(solution)/shard_map/ppermute | solution.py:452
  82.2 9.4 %collective-permute-start.4 = (f32[8,128]{1,0:T(8,128)S(1)}, f32[8,128]{1,0:T(8,128)S(1)}, u32[]{:S(2)}, u32[]{:S(2)}) collective-permute-start(f32[8,128]{1,0:T(8,128)S(1)} %add.24), channel_id=1, source_target_pairs={{0,32},{8,40},{16,48},{24,56},{32,0},{40,8},{48,16},{56,24},{64,96... | collective-permute-start | bytes 12296 | tf_op jit(solution)/shard_map/ppermute | solution.py:452
  91.6 6.4 %collective-permute-start.5 = (f32[8,128]{1,0:T(8,128)S(1)}, f32[8,128]{1,0:T(8,128)S(1)}, u32[]{:S(2)}, u32[]{:S(2)}) collective-permute-start(f32[8,128]{1,0:T(8,128)S(1)} %add.25), channel_id=1, source_target_pairs={{0,16},{8,24},{16,0},{24,8},{32,48},{40,56},{48,32},{56,40},{64,80... | collective-permute-start | bytes 12296 | tf_op jit(solution)/shard_map/ppermute | solution.py:452
  98.0 5.5 %collective-permute-start.6 = (f32[8,128]{1,0:T(8,128)S(1)}, f32[8,128]{1,0:T(8,128)S(1)}, u32[]{:S(2)}, u32[]{:S(2)}) collective-permute-start(f32[8,128]{1,0:T(8,128)S(1)} %add.26), channel_id=1, source_target_pairs={{0,8},{8,0},{16,24},{24,16},{32,40},{40,32},{48,56},{56,48},{64,72... | collective-permute-start | bytes 12296 | tf_op jit(solution)/shard_map/ppermute | solution.py:452
  104.2 10.1 %collective-permute-start.2 = (f32[3,32,256]{2,1,0:T(8,128)S(1)}, f32[3,32,256]{2,1,0:T(8,128)S(1)}, u32[]{:S(2)}, u32[]{:S(2)}) collective-permute-start(f32[3,32,256]{2,1,0:T(8,128)S(1)} %get-tuple-element.9.own), channel_id=1, source_target_pairs={{1,2},{3,4},{5,6},{7,8},{9,10},{11,12},{13,14},{15,16},{17,18},{19... | collective-permute-start | bytes 294920 | tf_op jit(solution)/shard_map/ppermute | solution.py:29
  109.2 5.1 %collective-permute-start.1 = (f32[3,32,256]{2,1,0:T(8,128)S(1)}, f32[3,32,256]{2,1,0:T(8,128)S(1)}, u32[]{:S(2)}, u32[]{:S(2)}) collective-permute-start(f32[3,32,256]{2,1,0:T(8,128)S(1)} %get-tuple-element.9.own), channel_id=1, source_target_pairs={{0,1},{2,3},{4,5},{6,7},{8,9},{10,11},{12,13},{14,15},{16,17},{18,... | collective-permute-start | bytes 294920 | tf_op jit(solution)/shard_map/ppermute | solution.py:29

commit v11 on v10

--- a/solution.py
+++ b/solution.py
@@ -307,7 +307,7 @@
         copy.wait()
 
 
-def gather_kernel(a, new_data, faces, *, count, fields, edge):
+def gather_kernel(a, summed, new_data, faces, mass, *, count, fields, edge, cells):
     rows = fields * edge
     lanes = edge * edge
     sources = a.shape[0] // count
@@ -318,6 +318,11 @@
             total = total + a[s * count + q]
         sums.append(total)
     whole = jnp.concatenate(sums, axis=0)
+    corner = summed[...]
+    on_diagonal = iota(corner.shape, 0) == iota(corner.shape, 1)
+    for k in range(mass.shape[0]):
+        line = jnp.sum(jnp.where(on_diagonal, corner[:, k:k + 1], 0.0), axis=0, keepdims=True)
+        mass[k:k + 1, :] = line[:, :fields] / cells
     new_data[...] = whole
     high, low = halves(whole)
     stacked = jnp.concatenate([high, low], axis=0)
@@ -471,17 +476,18 @@
         name="fold",
     )(slow(first))
     last = lax.all_to_all(folded, ALL_AXES, 0, 0, tiled=True, axis_index_groups=last_groups)
-    new_data, faces = pl.pallas_call(
-        functools.partial(gather_kernel, count=count, fields=fields, edge=edge),
+    new_data, faces, mass_totals = pl.pallas_call(
+        functools.partial(gather_kernel, count=count, fields=fields, edge=edge, cells=float(patches * devices * edge * lanes)),
         out_shape=(
             jax.ShapeDtypeStruct((count * rows, lanes), F32),
             VMEM((count, FACE_ROWS, lanes), F32),
+            jax.ShapeDtypeStruct((2, fields), F32),
         ),
-        in_specs=[vmem],
-        out_specs=(vmem, vmem),
+        in_specs=[vmem, vmem],
+        out_specs=(vmem, vmem, vmem),
         compiler_params=params,
         name="gather",
-    )(fast(last))
+    )(fast(last), total)
     cross = swapped(faces, 1)
     near = swapped(faces, 0)
     interface_jump = pl.pallas_call(
@@ -492,8 +498,6 @@
         compiler_params=params,
         name="jump",
     )(place, neighbor_side, neighbor_patch, fast(faces), fast(near), fast(cross))
-    total_cells = patches * devices * edge * lanes
-    mass_totals = total[:fields, :2].T / total_cells
     return (new_data.reshape(count, fields, edge, lanes), interface_jump, mass_totals)
 
 

time: 116 us -> 117 us (level)
  transfers between devices with their start and end apart: 9 -> 9, of which waited for: 7 -> 7; matrix products, arithmetic and copies ran while one was open for 1% -> 0% of each run, Pallas kernels for 3% -> 3%
where the time goes in v11:
time: 117 us; the launch traced here: 116 us
  starting transfers between devices  42.6 us (36%)
  blocking collectives  35.4 us (30%)
  waiting for transfers between devices  19.7 us (17%)
  Pallas kernels  17.4 us (15%)
    all_to_all x1, blocking collectives, body(): lax.all_to_all(partials, ALL_AXES, 0, 0, tiled=True, axis_index_groups=fi...  35.4 us
    ppermute x4, starting transfers between devices, crossed(): lax.ppermute(value, 'gy', [(i, i ^ distance) for i in range(size_y)])  25.3 us
    ppermute x4, waiting for transfers between devices, crossed(): lax.ppermute(value, 'gy', [(i, i ^ distance) for i in range(size_y)])  10.4 us
    pallas_call x1, Pallas kernels, body(): pl.pallas_call(functools.partial(partials_kernel, patches=patches, fields...  8.86 us
    ppermute x2, starting transfers between devices, swapped(): return lax.ppermute(block, ALL_AXES, pairs + [(j, i) for i, j in pairs])  6.93 us
    all_to_all x1, starting transfers between devices, body(): plane = lax.all_to_all(mass, PLANE, 0, 0, tiled=True)  5.02 us
    all_to_all x1, waiting for transfers between devices, body(): plane = lax.all_to_all(mass, PLANE, 0, 0, tiled=True)  3.52 us
    all_to_all x1, starting transfers between devices, body(): lax.all_to_all(folded, ALL_AXES, 0, 0, tiled=True, axis_index_groups=last...  3.51 us
  transfers between devices with their start and end apart: 9, of which 7 were waited for; matrix products, arithmetic and copies ran while one was open for 0% of the time, Pallas kernels for 3%

profile of v11, /device:TPU:2, one launch (start us, length us, event | category | flops | bytes accessed | tf_op | source)
XLA Modules:
  0.0 116.0 jit_solution(10999780305636435657)
XLA Ops:
  0.6 0.1 stack.23.place
  0.7 3.0 %head.1 = (f32[32,8,128]{2,1,0:T(8,128)}, f32[968,256]{1,0:T(8,128)S(1)}) custom-call(s32[5]{0:T(128)S(1)} %stack.23.place, s32[32]{0:T(128)} %pair_old.3, s32[32]{0:T(128)} %pair_slot.3, s32[3,32]{1,0:T(4,128)} %bitcast.14, s32[1,32]{1,0:T(1,128)} %bitcast.19, s32[1,32]{1,0:T(1,128)} %bitcast.17, s32[1,32]{1,0:T(1,128)} %bitcast.18, s32[1,32]{1,0:T(1,128)} %bitcast.20, ...), custom_call_target="tpu_custom_call" | custom-call | tf_op jit(solution)/shard_map/head/pallas_call | solution.py:402
  3.7 1.9 %collective-permute-start = (f32[968,256]{1,0:T(8,128)S(1)}, f32[968,256]{1,0:T(8,128)S(1)}, u32[]{:S(2)}, u32[]{:S(2)}) collective-permute-start(f32[968,256]{1,0:T(8,128)S(1)} %get-tuple-element.8), channel_id=1, source_target_pairs={{0,1},{1,0},{2,3},{3,2},{4,5},{5,4},{6,7},{7,6},{8,9},{9,8},{10,11... | collective-permute-start | bytes 2973704 | tf_op jit(solution)/shard_map/ppermute | solution.py:424
  5.6 2.5 %collective-permute-done.peer = f32[968,256]{1,0:T(8,128)S(1)} collective-permute-done((f32[968,256]{1,0:T(8,128)S(1)}, f32[968,256]{1,0:T(8,128)S(1)}, u32[]{:S(2)}, u32[]{:S(2)}) %collective-permute-start) | collective-permute-done | bytes 991264 | tf_op jit(solution)/shard_map/ppermute | solution.py:424
  8.2 8.9 %partials.1 = f32[48,80,256]{2,1,0:T(8,128)} custom-call(s32[5]{0:T(128)S(1)} %stack.23.place, s32[32]{0:T(128)} %pair_old.3, s32[32]{0:T(128)} %pair_slot.3, s32[3,32]{1,0:T(4,128)} %bitcast.16, s32[1,32]{1,0:T(1,128)} %bitcast.21, s32[1536]{0:T(1024)} %ratio_in.3, f32[12,80,256]{2,1,0:T(8,128)} %bitcast.13, f32[968,256]{1,0:T(8,128)S(1)} %collective-permute-done.peer), custom_call_target="tpu_custom_call" | custom-call | tf_op jit(solution)/shard_map/partials/pallas_call | solution.py:426
  17.0 35.4 %all_to_all.15.a = f32[48,80,256]{2,1,0:T(8,128)} all-to-all(f32[48,80,256]{2,1,0:T(8,128)} %partials.1), channel_id=1, replica_groups={{0,128,256,384},{2,130,258,386},{4,132,260,388},{6,134,262,390},{8,136,..., dimensions={0} | all-to-all | bytes 7864320 | tf_op jit(solution)/shard_map/all_to_all | solution.py:453
  52.4 5.0 %all-to-all-start.2 = ((f32[32,8,128]{2,1,0:T(8,128)}), f32[32,8,128]{2,1,0:T(8,128)S(1)}, u32[]{:S(2)}, u32[]{:S(2)}) async-start(f32[32,8,128]{2,1,0:T(8,128)} %get-tuple-element.9), calls=%async_computation.2 | async-start | bytes 262144 | tf_op jit(solution)/shard_map/all_to_all | solution.py:425
  57.5 0.0 copy-start
  57.5 0.0 copy-start.1
  57.5 3.1 %fold.1 = f32[12,80,256]{2,1,0:T(8,128)} custom-call(f32[48,80,256]{2,1,0:T(8,128)} %all_to_all.15.a), custom_call_target="tpu_custom_call" | custom-call | tf_op jit(solution)/shard_map/fold/pallas_call | solution.py:464
  60.6 3.5 %all-to-all-done.2 = f32[32,8,128]{2,1,0:T(8,128)S(1)} async-done(((f32[32,8,128]{2,1,0:T(8,128)}), f32[32,8,128]{2,1,0:T(8,128)S(1)}, u32[]{:S(2)}, u32[]{:S(2)}) %all-to-all-start.2) | async-done | bytes 131104 | tf_op jit(solution)/shard_map/all_to_all | solution.py:425
  64.2 3.5 %all-to-all-start.1 = ((f32[12,80,256]{2,1,0:T(8,128)}), f32[12,80,256]{2,1,0:T(8,128)S(1)}, u32[]{:S(2)}, u32[]{:S(2)}) async-start(f32[12,80,256]{2,1,0:T(8,128)} %fold.1), calls=%async_computation.1 | async-start | bytes 1966080 | tf_op jit(solution)/shard_map/all_to_all | solution.py:478
  67.7 12.9 %collective-permute-start.1 = (f32[8,128]{1,0:T(8,128)S(1)}, f32[8,128]{1,0:T(8,128)S(1)}, u32[]{:S(2)}, u32[]{:S(2)}) collective-permute-start(f32[8,128]{1,0:T(8,128)S(1)} %reduce_sum.9), channel_id=1, source_target_pairs={{0,64},{8,72},{16,80},{24,88},{32,96},{40,104},{48,112},{56,120},{... | collective-permute-start | bytes 12296 | tf_op jit(solution)/shard_map/ppermute | solution.py:457
  80.6 1.6 %collective-permute-done.1 = f32[8,128]{1,0:T(8,128)S(1)} collective-permute-done((f32[8,128]{1,0:T(8,128)S(1)}, f32[8,128]{1,0:T(8,128)S(1)}, u32[]{:S(2)}, u32[]{:S(2)}) %collective-permute-start.1) | collective-permute-done | bytes 4128 | tf_op jit(solution)/shard_map/ppermute | solution.py:457
  82.2 6.0 %collective-permute-start.2 = (f32[8,128]{1,0:T(8,128)S(1)}, f32[8,128]{1,0:T(8,128)S(1)}, u32[]{:S(2)}, u32[]{:S(2)}) collective-permute-start(f32[8,128]{1,0:T(8,128)S(1)} %add.24), channel_id=1, source_target_pairs={{0,32},{8,40},{16,48},{24,56},{32,0},{40,8},{48,16},{56,24},{64,96... | collective-permute-start | bytes 12296 | tf_op jit(solution)/shard_map/ppermute | solution.py:457
  88.2 3.3 %collective-permute-done.2 = f32[8,128]{1,0:T(8,128)S(1)} collective-permute-done((f32[8,128]{1,0:T(8,128)S(1)}, f32[8,128]{1,0:T(8,128)S(1)}, u32[]{:S(2)}, u32[]{:S(2)}) %collective-permute-start.2) | collective-permute-done | bytes 4128 | tf_op jit(solution)/shard_map/ppermute | solution.py:457
  91.6 3.4 %collective-permute-start.3 = (f32[8,128]{1,0:T(8,128)S(1)}, f32[8,128]{1,0:T(8,128)S(1)}, u32[]{:S(2)}, u32[]{:S(2)}) collective-permute-start(f32[8,128]{1,0:T(8,128)S(1)} %add.25), channel_id=1, source_target_pairs={{0,16},{8,24},{16,0},{24,8},{32,48},{40,56},{48,32},{56,40},{64,80... | collective-permute-start | bytes 12296 | tf_op jit(solution)/shard_map/ppermute | solution.py:457
  95.0 3.0 %collective-permute-done.3 = f32[8,128]{1,0:T(8,128)S(1)} collective-permute-done((f32[8,128]{1,0:T(8,128)S(1)}, f32[8,128]{1,0:T(8,128)S(1)}, u32[]{:S(2)}, u32[]{:S(2)}) %collective-permute-start.3) | collective-permute-done | bytes 4128 | tf_op jit(solution)/shard_map/ppermute | solution.py:457
  98.0 2.9 %collective-permute-start.4 = (f32[8,128]{1,0:T(8,128)S(1)}, f32[8,128]{1,0:T(8,128)S(1)}, u32[]{:S(2)}, u32[]{:S(2)}) collective-permute-start(f32[8,128]{1,0:T(8,128)S(1)} %add.26), channel_id=1, source_target_pairs={{0,8},{8,0},{16,24},{24,16},{32,40},{40,32},{48,56},{56,48},{64,72... | collective-permute-start | bytes 12296 | tf_op jit(solution)/shard_map/ppermute | solution.py:457
  100.9 2.5 %collective-permute-done.4 = f32[8,128]{1,0:T(8,128)S(1)} collective-permute-done((f32[8,128]{1,0:T(8,128)S(1)}, f32[8,128]{1,0:T(8,128)S(1)}, u32[]{:S(2)}, u32[]{:S(2)}) %collective-permute-start.4) | collective-permute-done | bytes 4128 | tf_op jit(solution)/shard_map/ppermute | solution.py:457
  103.5 0.0 all-to-all-done.1.a
  103.5 1.0 gather.1
  104.5 5.0 %collective-permute-start.6 = (f32[3,32,256]{2,1,0:T(8,128)S(1)}, f32[3,32,256]{2,1,0:T(8,128)S(1)}, u32[]{:S(2)}, u32[]{:S(2)}) collective-permute-start(f32[3,32,256]{2,1,0:T(8,128)S(1)} %get-tuple-element.11.own), channel_id=1, source_target_pairs={{1,2},{3,4},{5,6},{7,8},{9,10},{11,12},{13,14},{15,16},{17,18},{19... | collective-permute-start | bytes 294920 | tf_op jit(solution)/shard_map/ppermute | solution.py:29
  109.5 1.9 %collective-permute-start.5 = (f32[3,32,256]{2,1,0:T(8,128)S(1)}, f32[3,32,256]{2,1,0:T(8,128)S(1)}, u32[]{:S(2)}, u32[]{:S(2)}) collective-permute-start(f32[3,32,256]{2,1,0:T(8,128)S(1)} %get-tuple-element.11.own), channel_id=1, source_target_pairs={{0,1},{2,3},{4,5},{6,7},{8,9},{10,11},{12,13},{14,15},{16,17},{18,... | collective-permute-start | bytes 294920 | tf_op jit(solution)/shard_map/ppermute | solution.py:29
  111.4 3.2 %collective-permute-done.6.cross = f32[3,32,256]{2,1,0:T(8,128)S(1)} collective-permute-done((f32[3,32,256]{2,1,0:T(8,128)S(1)}, f32[3,32,256]{2,1,0:T(8,128)S(1)}, u32[]{:S(2)}, u32[]{:S(2)}) %collective-permute-start.6) | collective-permute-done | bytes 98336 | tf_op jit(solution)/shard_map/ppermute | solution.py:29
  114.6 0.0 collective-permute-done.5.near
  114.6 0.0 copy-done
  114.6 0.0 copy-done.1
  114.6 1.4 %jump.1 = f32[3,5,6,256]{3,2,1,0:T(8,128)} custom-call(s32[5]{0:T(128)S(1)} %stack.23.place, s32[3,6]{1,0:T(4,128)S(1)} %copy-done, s32[3,6]{1,0:T(4,128)S(1)} %copy-done.1, f32[3,32,256]{2,1,0:T(8,128)S(1)} %get-tuple-element.11.own, f32[3,32,256]{2,1,0:T(8,128)S(1)} %collective-permute-done.5.near, f32[3,32,256]{2,1,0:T(8,128)S(1)} %collective-permute-done.6.cross), custom_call_target="tpu_custom_call" | custom-call | tf_op jit(solution)/shard_map/jump/pallas_call | solution.py:493
  (5 shorter events, 0.0 us)
Async XLA Ops:
  3.7 4.5 %collective-permute-start = (f32[968,256]{1,0:T(8,128)S(1)}, f32[968,256]{1,0:T(8,128)S(1)}, u32[]{:S(2)}, u32[]{:S(2)}) collective-permute-start(f32[968,256]{1,0:T(8,128)S(1)} %get-tuple-element.8), channel_id=1, source_target_pairs={{0,1},{1,0},{2,3},{3,2},{4,5},{5,4},{6,7},{7,6},{8,9},{9,8},{10,11... | collective-permute-start | bytes 2973704 | tf_op jit(solution)/shard_map/ppermute | solution.py:424
  52.4 11.7 %all-to-all-start.2 = ((f32[32,8,128]{2,1,0:T(8,128)}), f32[32,8,128]{2,1,0:T(8,128)S(1)}, u32[]{:S(2)}, u32[]{:S(2)}) async-start(f32[32,8,128]{2,1,0:T(8,128)} %get-tuple-element.9), calls=%async_computation.2 | async-start | bytes 262144 | tf_op jit(solution)/shard_map/all_to_all | solution.py:425
  57.5 57.1 %copy-start = (s32[3,6]{1,0:T(4,128)S(1)}, s32[3,6]{1,0:T(4,128)}, u32[]{:S(2)}) copy-start(s32[3,6]{1,0:T(4,128)} %side.1) | copy-start | bytes 220
  57.5 57.1 %copy-start.1 = (s32[3,6]{1,0:T(4,128)S(1)}, s32[3,6]{1,0:T(4,128)}, u32[]{:S(2)}) copy-start(s32[3,6]{1,0:T(4,128)} %patch.1) | copy-start | bytes 220
  64.2 39.3 %all-to-all-start.1 = ((f32[12,80,256]{2,1,0:T(8,128)}), f32[12,80,256]{2,1,0:T(8,128)S(1)}, u32[]{:S(2)}, u32[]{:S(2)}) async-start(f32[12,80,256]{2,1,0:T(8,128)} %fold.1), calls=%async_computation.1 | async-start | bytes 1966080 | tf_op jit(solution)/shard_map/all_to_all | solution.py:478
  67.7 14.5 %collective-permute-start.1 = (f32[8,128]{1,0:T(8,128)S(1)}, f32[8,128]{1,0:T(8,128)S(1)}, u32[]{:S(2)}, u32[]{:S(2)}) collective-permute-start(f32[8,128]{1,0:T(8,128)S(1)} %reduce_sum.9), channel_id=1, source_target_pairs={{0,64},{8,72},{16,80},{24,88},{32,96},{40,104},{48,112},{56,120},{... | collective-permute-start | bytes 12296 | tf_op jit(solution)/shard_map/ppermute | solution.py:457
  82.2 9.4 %collective-permute-start.2 = (f32[8,128]{1,0:T(8,128)S(1)}, f32[8,128]{1,0:T(8,128)S(1)}, u32[]{:S(2)}, u32[]{:S(2)}) collective-permute-start(f32[8,128]{1,0:T(8,128)S(1)} %add.24), channel_id=1, source_target_pairs={{0,32},{8,40},{16,48},{24,56},{32,0},{40,8},{48,16},{56,24},{64,96... | collective-permute-start | bytes 12296 | tf_op jit(solution)/shard_map/ppermute | solution.py:457
  91.6 6.4 %collective-permute-start.3 = (f32[8,128]{1,0:T(8,128)S(1)}, f32[8,128]{1,0:T(8,128)S(1)}, u32[]{:S(2)}, u32[]{:S(2)}) collective-permute-start(f32[8,128]{1,0:T(8,128)S(1)} %add.25), channel_id=1, source_target_pairs={{0,16},{8,24},{16,0},{24,8},{32,48},{40,56},{48,32},{56,40},{64,80... | collective-permute-start | bytes 12296 | tf_op jit(solution)/shard_map/ppermute | solution.py:457
  98.0 5.5 %collective-permute-start.4 = (f32[8,128]{1,0:T(8,128)S(1)}, f32[8,128]{1,0:T(8,128)S(1)}, u32[]{:S(2)}, u32[]{:S(2)}) collective-permute-start(f32[8,128]{1,0:T(8,128)S(1)} %add.26), channel_id=1, source_target_pairs={{0,8},{8,0},{16,24},{24,16},{32,40},{40,32},{48,56},{56,48},{64,72... | collective-permute-start | bytes 12296 | tf_op jit(solution)/shard_map/ppermute | solution.py:457
  104.5 10.1 %collective-permute-start.6 = (f32[3,32,256]{2,1,0:T(8,128)S(1)}, f32[3,32,256]{2,1,0:T(8,128)S(1)}, u32[]{:S(2)}, u32[]{:S(2)}) collective-permute-start(f32[3,32,256]{2,1,0:T(8,128)S(1)} %get-tuple-element.11.own), channel_id=1, source_target_pairs={{1,2},{3,4},{5,6},{7,8},{9,10},{11,12},{13,14},{15,16},{17,18},{19... | collective-permute-start | bytes 294920 | tf_op jit(solution)/shard_map/ppermute | solution.py:29
  109.5 5.1 %collective-permute-start.5 = (f32[3,32,256]{2,1,0:T(8,128)S(1)}, f32[3,32,256]{2,1,0:T(8,128)S(1)}, u32[]{:S(2)}, u32[]{:S(2)}) collective-permute-start(f32[3,32,256]{2,1,0:T(8,128)S(1)} %get-tuple-element.11.own), channel_id=1, source_target_pairs={{0,1},{2,3},{4,5},{6,7},{8,9},{10,11},{12,13},{14,15},{16,17},{18,... | collective-permute-start | bytes 294920 | tf_op jit(solution)/shard_map/ppermute | solution.py:29
